TPU v7x, 128 devices: a whole 4x4x4 slice. The times are simulated.
128 devices in a mesh: dp: 32 (over z, y, x_hi), tensor: 4 (over x_lo, core).
Axes of the slice: x: 4 (x_hi: 2, x_lo: 2; x = x_hi * 2 + x_lo), y: 4, z: 4, core: 2. Of those that a mesh axis runs over, the one named last changes fastest.
Arguments:
- hidden: bfloat16 [4096, 7168], P('dp', 'tensor'), may hold values from -6 to 6
- hash_rows: int32 [4096, 4], P('dp', 'tensor'), may hold values from 0 to 32767, as said below
- memory_table: bfloat16 [32768, 896], P(('dp', 'tensor')), may hold values from -6 to 6
- key_weight: bfloat16 [3584, 7168], P(None, 'tensor'), may hold values from -0.09375 to 0.09375
- value_weight: bfloat16 [3584, 7168], P(None, 'tensor'), may hold values from -0.09375 to 0.09375
- hidden_gain: float32 [7168], P('tensor'), may hold values from 0.1 to 1.9
- key_gain: float32 [7168], P('tensor'), may hold values from 0.1 to 1.9
Outputs:
- joined: bfloat16 [4096, 7168], P('dp', 'tensor')
Inputs may be any that keep to these rules, and one draw needn't show every extreme that they name: `hash_rows`: row r lies in the block of 256 rows held by device r // 256 of dp+tensor. Of the lookups that one device holds (128 requests of its dp group times its 4 / 4 heads), at most 2 fall into any one device's block, and in every draw some device's block receives exactly 2 from every device.
All inputs are finite; a program needn't handle non-finite values.
Results may differ from a plain program's by a relative error of at most 0.0014.
Values may be sent and summed in bfloat16 or wider, within the bound.
No kernel may reach another device: no remote copies, remote signals or barrier semaphores. Data moves between devices by JAX's collectives and lax.ppermute only.
A program may use at most 64 MiB of HBM per device.

v0:
```python
import math

import jax
import jax.numpy as jnp
from jax import lax
from jax.sharding import PartitionSpec as P

D = 7168


epsilon = 1e-06


def split_up(array, dim, devices):
    shape = array.shape
    pieces = array.reshape(*shape[:dim], devices, shape[dim] // devices, *shape[dim + 1 :])
    return jnp.moveaxis(pieces, dim, 0)


def laid_out(pieces, dim):
    shape = list(pieces.shape[1:])
    shape[dim] *= pieces.shape[0]
    return jnp.moveaxis(pieces, 0, dim).reshape(shape)


def one_exchange(array, axis, axes, splits, concats):
    sizes = [lax.axis_size(a) for a in axes]
    pieces = split_up(array, splits[0], sizes[0])
    pieces = jnp.moveaxis(split_up(pieces, splits[1] + 1, sizes[1]), 0, 1)
    inside = pieces.shape[2:]
    pieces = pieces.reshape(-1, *inside)
    pieces = lax.all_to_all(pieces, axis, split_axis=0, concat_axis=0, tiled=True)
    pieces = laid_out(pieces.reshape(*sizes, *inside), concats[0] + 1)
    return laid_out(pieces, concats[1])


def from_everyone(array, axis):
    devices = lax.axis_size(axis)
    return lax.all_to_all(
        jnp.broadcast_to(array[None], (devices, *array.shape)), axis, 0, 0, tiled=True
    )


def of_everyone(array, axis):
    return from_everyone(array, axis).sum(axis=0)


def in_one(arrays, axis):
    ends = [0]
    for a in arrays:
        ends.append(ends[-1] + a.size)
    subtotal = of_everyone(jnp.concatenate([a.ravel() for a in arrays]), axis)
    return tuple((subtotal[b:e].reshape(a.shape) for a, b, e in zip(arrays, ends, ends[1:])))


def fetch_rows(row_numbers, capacity, memory_table):
    requests_here = row_numbers.shape[0]
    heads_here = row_numbers.shape[1]
    lookups = requests_here * heads_here
    rows_held = memory_table.shape[0]
    row_width = memory_table.shape[1]
    devices = lax.axis_size("dp") * lax.axis_size("tensor")
    flattened = row_numbers.reshape(lookups)
    owners = flattened // rows_held
    local_rows = flattened - owners * rows_held
    owner_mask = (owners[:, None] == jnp.arange(devices, dtype=jnp.int32)[None, :]).astype(
        jnp.int32
    )
    earlier = jnp.cumsum(owner_mask, axis=0) - owner_mask
    slot_index = jnp.sum(earlier * owner_mask, axis=1)
    position = owners * capacity + slot_index
    wanted = jnp.zeros((devices * capacity,), jnp.int32).at[position].set(local_rows)
    wanted = wanted.reshape(devices, capacity)
    request_grid = wanted.reshape(lax.axis_size("dp"), lax.axis_size("tensor"), capacity)
    asked_grid = one_exchange(request_grid, ("dp", "tensor"), ("dp", "tensor"), (0, 1), (0, 1))
    fetched = memory_table[asked_grid]
    returned = one_exchange(fetched, ("dp", "tensor"), ("dp", "tensor"), (0, 1), (0, 1))
    arrived = returned.reshape(devices * capacity, row_width)
    gathered_rows = arrived[position]
    return gathered_rows


def local(hidden, hash_rows, memory_table, key_weight, value_weight, hidden_gain, key_gain):
    devices = lax.axis_size("dp") * lax.axis_size("tensor")
    base_capacity = 2 * max(1, hash_rows.size // devices)
    memory = fetch_rows(hash_rows, base_capacity, memory_table)
    portion = lax.all_gather(memory, "tensor", axis=1, tiled=True)
    key = jnp.dot(portion, key_weight, preferred_element_type=jnp.float32)
    projected = jnp.dot(portion, value_weight, preferred_element_type=jnp.float32)
    hidden_float = hidden.astype(jnp.float32)
    hidden_scaled = hidden_float * hidden_gain
    key_scaled = key * key_gain
    hidden_squares = jnp.sum(hidden_float * hidden_float, axis=1)
    key_squares = jnp.sum(key * key, axis=1)
    crossing = jnp.sum(hidden_scaled * key_scaled, axis=1)
    hidden_total, key_total, cross_total = in_one((hidden_squares, key_squares, crossing), "tensor")
    agreement = (
        cross_total * lax.rsqrt(hidden_total / D + epsilon) * lax.rsqrt(key_total / D + epsilon)
    )
    gate_value = jax.nn.sigmoid(agreement / math.sqrt(D))
    return (hidden_float + gate_value[:, None] * projected).astype(jnp.bfloat16)


def solution(mesh):
    return jax.shard_map(
        local,
        mesh=mesh,
        in_specs=(
            P("dp", "tensor"),
            P("dp", "tensor"),
            P(("dp", "tensor"), None),
            P(None, "tensor"),
            P(None, "tensor"),
            P("tensor"),
            P("tensor"),
        ),
        out_specs=P("dp", "tensor"),
        check_vma=False,
    )
```

profile of v0, /device:TPU:1, one launch (start us, length us, event | category | flops | bytes accessed | tf_op | source)
XLA Modules:
  0.0 74.4 jit_solution(16476649435099616097)
XLA Ops:
  0.0 0.0 copy-start
  0.0 0.7 fusion.13
  0.7 0.7 bitcast_subtract_fusion
  1.4 0.1 fusion.5
  1.5 0.2 reduce_window_sum.11
  1.6 0.2 select_reduce_fusion
  1.8 0.7 fusion.6
  2.5 1.0 %scatter_custom_fusion = s32[256]{0:T(256)S(1)} fusion(s32[128]{0:T(128)S(1)} %fusion.6, s32[128]{0:T(128)S(1)} %bitcast_subtract_fusion, s32[]{:T(128)} %constant.32.clone.1), kind=kCustom, calls=%fused_computation.33 | custom fusion | bytes 1028 | tf_op jit(solution)/shard_map/scatter | solution.py:72
  3.5 0.1 reshape_transpose_transpose_reshape_reshape_reshape_reshape.3
  3.6 20.9 %all_to_all.16 = s32[128,1,1,2]{3,2,1,0:T(1,128)S(1)} all-to-all(s32[128,1,1,2]{3,2,1,0:T(1,128)S(1)} %bitcast.47), channel_id=1, replica_groups=mesh['dp'=32,'tensor'=4] {'dp','tensor'}, dimensions={0} | all-to-all | bytes 2048 | tf_op jit(solution)/shard_map/all_to_all | solution.py:32
  24.6 0.1 reshape.64
  24.7 0.0 copy-done
  24.7 1.2 %gather_fusion = bf16[256,896]{1,0:T(8,128)(2,1)S(1)} fusion(bf16[256,896]{1,0:T(8,128)(2,1)S(1)} %copy-done, s32[1024]{0:T(1024)S(1)} %pad_clamp_fusion.1), kind=kCustom, calls=%fused_computation | custom fusion | bytes 918528 | tf_op jit(solution)/shard_map/gather | solution.py:76
  25.9 0.9 %reshape_transpose_transpose_reshape_reshape.3 = bf16[128,1,1,2,896]{4,3,0,2,1:T(2,128)(2,1)} reshape(bf16[256,896]{1,0:T(8,128)(2,1)S(1)} %gather_fusion) | data formatting | bytes 917504 | tf_op jit(solution)/shard_map/reshape;transpose;transpose;reshape;reshape | solution.py:31
  26.9 0.0 copy-start.1
  26.9 4.5 %all-to-all-start.1 = ((bf16[128,1,1,2,896]{4,3,2,1,0:T(2,128)(2,1)}), bf16[128,1,1,2,896]{4,3,2,1,0:T(2,128)(2,1)S(1)}, u32[]{:S(2)}, u32[]{:S(2)}) async-start(bf16[128,1,1,2,896]{4,3,2,1,0:T(2,128)(2,1)} %bitcast.14), calls=%async_computation.1 | async-start | bytes 917504 | tf_op jit(solution)/shard_map/all_to_all | solution.py:32
  31.4 12.9 %all-to-all-done.1 = bf16[128,1,1,2,896]{4,3,2,1,0:T(2,128)(2,1)S(1)} async-done(((bf16[128,1,1,2,896]{4,3,2,1,0:T(2,128)(2,1)}), bf16[128,1,1,2,896]{4,3,2,1,0:T(2,128)(2,1)S(1)}, u32[]{:S(2)}, u32[]{:S(2)}) %all-to-all-start.1) | async-done | bytes 458784 | tf_op jit(solution)/shard_map/all_to_all | solution.py:32
  44.3 0.2 reshape_reshape.3
  44.5 0.9 %gather_fusion.1 = bf16[128,896]{1,0:T(8,128)(2,1)S(1)} fusion(bf16[256,896]{1,0:T(8,128)(2,1)S(1)} %reshape_reshape.3, s32[1024]{0:T(1024)S(1)} %pad_clamp_fusion), kind=kCustom, calls=%fused_computation.1 | custom fusion | bytes 459264 | tf_op jit(solution)/shard_map/gather | solution.py:79
  45.4 9.4 %all-gather = bf16[128,3584]{1,0:T(8,128)(2,1)S(1)} all-gather(bf16[128,896]{1,0:T(8,128)(2,1)S(1)} %gather_fusion.1), channel_id=2, replica_groups=mesh['dp'=32,'tensor'=4] {'tensor'}, dimensions={1}, use_global_device_ids=true | all-gather | bytes 1146880 | tf_op jit(solution)/shard_map/all_gather | solution.py:87
  54.8 6.7 %multiply_reduce_fusion = (f32[128]{0:T(128)S(1)}, f32[128]{0:T(128)S(1)}, f32[128]{0:T(128)S(1)}) fusion(f32[1792]{0:T(1024)} %param.13, f32[1792]{0:T(1024)} %param.12, bf16[128,1792]{1,0:T(8,128)(2,1)} %param.7, bf16[128,3584]{1,0:T(8,128)(2,1)S(1)} %all-gather, bf16[3584,1792]{1,0:T(8,128)(2,1)} %param.10), kind=kOutput, calls=%fused_computation.11 | convolution fusion | flops 1646231168 | bytes 14237184 | tf_op jit(solution)/shard_map/dot_general | solution.py:88
  61.5 5.6 %all_to_all.17 = f32[4,1,384]{2,1,0:T(1,128)S(1)} all-to-all(f32[4,1,384]{2,1,0:T(1,128)S(1)} %broadcast_in_dim.5), channel_id=1, replica_groups=mesh['dp'=32,'tensor'=4] {'tensor'}, dimensions={0} | all-to-all | bytes 12288 | tf_op jit(solution)/shard_map/all_to_all | solution.py:39
  67.1 0.0 copy-done.1
  67.1 7.3 %fusion.1 = bf16[128,1792]{1,0:T(8,128)(2,1)} fusion(bf16[128,3584]{1,0:T(8,128)(2,1)S(1)} %all-gather, bf16[3584,1792]{1,0:T(8,128)(2,1)} %param.11, bf16[128,1792]{1,0:T(8,128)(2,1)S(1)} %copy-done.1, f32[128]{0:T(128)S(1)} %add_divide_fusion), kind=kOutput, calls=%fused_computation.5 | convolution fusion | flops 1645084672 | bytes 14680576 | tf_op jit(solution)/shard_map/dot_general | solution.py:89
  (7 shorter events, 0.1 us)
Async XLA Ops:
  0.0 24.7 %copy-start = (bf16[256,896]{1,0:T(8,128)(2,1)S(1)}, bf16[256,896]{1,0:T(8,128)(2,1)}, u32[]{:S(2)}) copy-start(bf16[256,896]{1,0:T(8,128)(2,1)} %param.9) | copy-start | bytes 1376260
  26.9 40.2 %copy-start.1 = (bf16[128,1792]{1,0:T(8,128)(2,1)S(1)}, bf16[128,1792]{1,0:T(8,128)(2,1)}, u32[]{:S(2)}) copy-start(bf16[128,1792]{1,0:T(8,128)(2,1)} %param.7) | copy-start | bytes 1376260
  26.9 17.4 %all-to-all-start.1 = ((bf16[128,1,1,2,896]{4,3,2,1,0:T(2,128)(2,1)}), bf16[128,1,1,2,896]{4,3,2,1,0:T(2,128)(2,1)S(1)}, u32[]{:S(2)}, u32[]{:S(2)}) async-start(bf16[128,1,1,2,896]{4,3,2,1,0:T(2,128)(2,1)} %bitcast.14), calls=%async_computation.1 | async-start | bytes 917504 | tf_op jit(solution)/shard_map/all_to_all | solution.py:32
where the time goes:
time: 74.7 us; the launch traced here: 74.4 us
  blocking collectives  35.9 us (48%)
  matrix products  13.9 us (19%)
  waiting for transfers between devices  12.9 us (17%)
  starting transfers between devices  4.5 us (6%)
  local copies, waits for them, and re-layouts  4.46 us (6%)
  other arithmetic  2.56 us (3%)
    all_to_all x1, blocking collectives, one_exchange(): lax.all_to_all(pieces, axis, split_axis=0, concat_axis=0, tiled=True)  20.9 us
    all_to_all x1, waiting for transfers between devices, one_exchange(): lax.all_to_all(pieces, axis, split_axis=0, concat_axis=0, tiled=True)  12.9 us
    all_gather x1, blocking collectives, local(): portion = lax.all_gather(memory, 'tensor', axis=1, tiled=True)  9.42 us
    dot_general x1, matrix products, local(): jnp.dot(portion, value_weight, preferred_element_type=jnp.float32)  7.26 us
    dot_general x1, matrix products, local(): key = jnp.dot(portion, key_weight, preferred_element_type=jnp.float32)  6.69 us
    all_to_all x1, blocking collectives, from_everyone(): lax.all_to_all(jnp.broadcast_to(array[None], (devices, *array.shape)), ax...  5.6 us
    all_to_all x1, starting transfers between devices, one_exchange(): lax.all_to_all(pieces, axis, split_axis=0, concat_axis=0, tiled=True)  4.5 us
  transfers between devices with their start and end apart: 1, of which 1 were waited for; matrix products, arithmetic and copies ran while one was open for 0% of the time, Pallas kernels for 0%

commit v1 on v0

v1 whole, which is shorter than its diff:
```python
import math

import jax
import jax.numpy as jnp
from jax import lax
from jax.experimental import pallas as pl
from jax.experimental.pallas import tpu as pltpu
from jax.sharding import PartitionSpec as P

D = 7168
LANES = 128
EPSILON = 1e-06
COVER = 20_000_000_000
BOTH = ("dp", "tensor")
MIB = 1024 * 1024

f32 = jnp.float32
bf16 = jnp.bfloat16


def iota(shape, dim):
    return lax.broadcasted_iota(jnp.int32, shape, dim)


def vmem(count):
    return [pl.BlockSpec(memory_space=pltpu.VMEM)] * count


def call(body, out_shape, inputs, limit, scalars=(), scratch=(), flops=0):
    many = isinstance(out_shape, (tuple, list))
    return pl.pallas_call(
        body,
        out_shape=out_shape,
        in_specs=[pl.BlockSpec(memory_space=pltpu.SMEM)] * len(scalars) + vmem(len(inputs)),
        out_specs=tuple(vmem(len(out_shape))) if many else vmem(1)[0],
        scratch_shapes=list(scratch),
        compiler_params=pltpu.CompilerParams(vmem_limit_bytes=limit),
        cost_estimate=pl.CostEstimate(flops=flops, transcendentals=0, bytes_accessed=0) if flops else None,
    )(*scalars, *inputs)


def request_kernel(rows_held, hash_ref, out_ref):
    row = hash_ref[...]
    owner = row // rows_held
    local = row - owner * rows_held
    owner_rows = jnp.broadcast_to(owner.astype(f32), (LANES, LANES))
    owner_cols = owner_rows.T
    earlier = (owner_rows == owner_cols) & (iota((LANES, LANES), 0) < iota((LANES, LANES), 1))
    slot = jnp.sum(earlier.astype(f32), axis=0, keepdims=True)
    position = owner * 2 + slot.astype(jnp.int32)
    place = iota((LANES, LANES), 0)
    local_f = local.astype(f32)
    zero = jnp.zeros((LANES, LANES), f32)
    ask0 = jnp.sum(jnp.where(position == 2 * place, local_f, zero), axis=1, keepdims=True)
    ask1 = jnp.sum(jnp.where(position == 2 * place + 1, local_f, zero), axis=1, keepdims=True)
    asks = jnp.where(iota((LANES, LANES), 1) < LANES // 2, ask0, ask1)
    where = jnp.broadcast_to(position.astype(f32), (LANES, LANES))
    both = jnp.stack([where, asks], axis=1)
    out_ref[...] = both.reshape(2 * LANES, LANES).astype(bf16)


def gather_kernel(asked_ref, table_ref, out_ref):
    asked = asked_ref[...].astype(f32)
    rows = asked.shape[0]
    even = (iota((rows, 1), 0) % 2) == 0
    ahead = pltpu.roll(asked, rows - 1, 0)
    index = jnp.where(even, ahead[:, 0:1], asked[:, LANES - 1 :])
    held = table_ref.shape[0]
    chosen = (index.astype(jnp.int32) == iota((rows, held), 1)).astype(f32).astype(bf16)
    found = jnp.dot(chosen, table_ref[...], preferred_element_type=f32)
    found = found.astype(bf16).reshape(rows // 8, 1, 8, found.shape[1])
    out_ref[...] = jnp.concatenate([found, found], axis=1).reshape(2 * rows, -1)


def place_kernel(where_ref, asked_ref, arrived_ref, out_ref):
    core = where_ref[0] & 1
    start = pl.multiple_of((where_ref[0] >> 2) * 8, 8)
    asked = asked_ref[pl.ds(start, 8), :].astype(f32)
    arrived = arrived_ref[...]
    slots = arrived.shape[0]
    width = arrived.shape[1]
    for head in range(4):
        position = jnp.broadcast_to(asked[2 * head : 2 * head + 1, :], (LANES, LANES)).T
        position = position[:, 0:1].astype(jnp.int32)
        owner = position // 2
        target = (owner // 2) * 8 + head * 2 + position % 2
        target = jnp.where(owner % 2 == core, target, -1)
        chosen = (target == iota((LANES, slots), 1)).astype(f32).astype(bf16)
        found = jnp.dot(chosen, arrived, preferred_element_type=f32)
        out_ref[:, head * width : (head + 1) * width] = found.astype(bf16)


def row_of_sums(terms):
    parts = terms[:, 0:LANES]
    for k in range(1, terms.shape[1] // LANES):
        parts = parts + terms[:, k * LANES : (k + 1) * LANES]
    return jnp.sum(parts.T, axis=0, keepdims=True)


def key_kernel(mine_ref, other_ref, weight_ref, hidden_ref, hgain_ref, kgain_ref, memory_ref, sums_ref):
    memory = mine_ref[...] + other_ref[...]
    memory_ref[...] = memory
    key = jnp.dot(memory, weight_ref[...], preferred_element_type=f32)
    hidden = hidden_ref[...].astype(f32)
    sums = [
        row_of_sums(hidden * hidden),
        row_of_sums(key * key),
        row_of_sums((hidden * hgain_ref[...]) * (key * kgain_ref[...])),
    ]
    sums_ref[...] = jnp.concatenate(sums + [jnp.zeros((5, LANES), f32)], axis=0)


def value_kernel(memory_ref, weight_ref, out_ref):
    out_ref[...] = jnp.dot(memory_ref[...], weight_ref[...], preferred_element_type=f32)


def join_kernel(s0_ref, s1_ref, s2_ref, s3_ref, hidden_ref, projected_ref, out_ref):
    sums = (s0_ref[...] + s1_ref[...]) + (s2_ref[...] + s3_ref[...])
    hidden_power = sums[0:1] / D
    key_power = sums[1:2] / D
    agreement = sums[2:3] * lax.rsqrt(hidden_power + EPSILON) * lax.rsqrt(key_power + EPSILON)
    gate = jax.nn.sigmoid(agreement / math.sqrt(D))
    gate = jnp.broadcast_to(gate, (LANES, LANES)).T[:, 0:1]
    out_ref[...] = (hidden_ref[...].astype(f32) + gate * projected_ref[...]).astype(bf16)


def local(hidden, hash_rows, memory_table, key_weight, value_weight, hidden_gain, key_gain):
    groups = lax.axis_size("dp")
    tensor = lax.axis_size("tensor")
    devices = groups * tensor
    rows_held, row_width = memory_table.shape
    shape = jax.ShapeDtypeStruct

    here = lax.axis_index(BOTH).astype(jnp.int32).reshape(1)
    hash_rows, here, hidden_gain, key_gain = lax.optimization_barrier((hash_rows, here, hidden_gain, key_gain))
    message = call(
        lambda *refs: request_kernel(rows_held, *refs),
        shape((2 * devices, LANES), bf16),
        [hash_rows.reshape(1, LANES)],
        4 * MIB,
        flops=COVER,
    )
    asked = lax.all_to_all(message.reshape(devices, 2, LANES), BOTH, 0, 0, tiled=True)
    asked = asked.reshape(2 * devices, LANES)
    sent = call(gather_kernel, shape((4 * devices, row_width), bf16), [asked, memory_table], 6 * MIB, flops=COVER)
    same_core = [[2 * k + c for k in range(devices // 2)] for c in range(2)]
    arrived = lax.all_to_all(
        sent.reshape(devices // 2, 8, row_width), BOTH, 0, 0, axis_index_groups=same_core, tiled=True
    ).reshape(4 * devices, row_width)
    mine = call(
        place_kernel,
        shape((LANES, 4 * row_width), bf16),
        [asked, arrived],
        6 * MIB,
        scalars=[here],
    )
    other = lax.ppermute(mine, "tensor", [(k, k ^ 1) for k in range(tensor)])
    columns = key_weight.shape[1]
    key_weight = pltpu.with_memory_space_constraint(key_weight, pltpu.VMEM)
    value_weight = pltpu.with_memory_space_constraint(value_weight, pltpu.VMEM)
    memory, sums = call(
        key_kernel,
        (shape(mine.shape, bf16), shape((8, LANES), f32)),
        [mine, other, key_weight, hidden, hidden_gain.reshape(1, columns), key_gain.reshape(1, columns)],
        6 * MIB,
        flops=2 * LANES * mine.shape[1] * columns,
    )
    others = [lax.ppermute(sums, "tensor", [(k, k ^ d) for k in range(tensor)]) for d in (1, 2, 3)]
    projected = call(
        value_kernel,
        shape((LANES, columns), f32),
        [memory, value_weight],
        6 * MIB,
        flops=2 * LANES * mine.shape[1] * columns,
    )
    return call(join_kernel, shape(hidden.shape, bf16), [sums, *others, hidden, projected], 6 * MIB)


def solution(mesh):
    return jax.shard_map(
        local,
        mesh=mesh,
        in_specs=(
            P("dp", "tensor"),
            P("dp", "tensor"),
            P(("dp", "tensor"), None),
            P(None, "tensor"),
            P(None, "tensor"),
            P("tensor"),
            P("tensor"),
        ),
        out_specs=P("dp", "tensor"),
        check_vma=False,
    )
```

time: 74.7 us -> 56.5 us (0.76)
  matrix products: 13.9 us -> 0 us
  waiting for transfers between devices: 12.9 us -> 2.07 us
  Pallas kernels: 0 us -> 6.85 us
  blocking collectives: 35.9 us -> 41.8 us
  local copies, waits for them, and re-layouts: 4.46 us -> 0.72 us
  other arithmetic: 2.56 us -> 0.01 us
    all_to_all x2, blocking collectives: 26.5 us -> 41.8 us  [the longest x1 20.9 us: local(): lax.all_to_all(message.reshape(devices, 2, LANES), BOTH, 0, 0, tiled=True)]
    dot_general x2 -> x0, matrix products: 13.9 us -> none  [the longest x1 7.26 us: local(): jnp.dot(portion, value_weight, preferred_element_type=jnp.float32)]
    all_to_all x1 -> x0, waiting for transfers between devices: 12.9 us -> none  [one_exchange(): lax.all_to_all(pieces, axis, split_axis=0, concat_axis=0, tiled=True)]
    all_gather x1 -> x0, blocking collectives: 9.42 us -> none  [local(): portion = lax.all_gather(memory, 'tensor', axis=1, tiled=True)]
    pallas_call x0 -> x6, Pallas kernels: none -> 6.85 us  [call(): pl.pallas_call(body, out_shape=out_shape, in_specs=[pl.BlockSpec(memory_s...]
    ppermute x0 -> x4, starting transfers between devices: none -> 4.72 us  [the longest x1 2.5 us: local(): other = lax.ppermute(mine, 'tensor', [(k, k ^ 1) for k in range(tensor)])]
    all_to_all x1 -> x0, starting transfers between devices: 4.5 us -> none  [one_exchange(): lax.all_to_all(pieces, axis, split_axis=0, concat_axis=0, tiled=True)]
    gather x2 -> x0, local copies, waits for them, and re-layouts: 2.08 us -> none  [the longest x1 1.2 us: fetch_rows(): fetched = memory_table[asked_grid]]
  transfers between devices with their start and end apart: 1 -> 4, of which waited for: 1 -> 1; matrix products, arithmetic and copies ran while one was open for 0% -> 0% of each run, Pallas kernels for 0% -> 3%
where the time goes in v1:
time: 56.5 us; the launch traced here: 56.4 us
  blocking collectives  41.8 us (74%)
  Pallas kernels  6.85 us (12%)
  starting transfers between devices  4.72 us (8%)
  waiting for transfers between devices  2.07 us (4%)
  local copies, waits for them, and re-layouts  0.72 us (1%)
    all_to_all x1, blocking collectives, local(): lax.all_to_all(message.reshape(devices, 2, LANES), BOTH, 0, 0, tiled=True)  20.9 us
    all_to_all x1, blocking collectives, local(): lax.all_to_all(sent.reshape(devices // 2, 8, row_width), BOTH, 0, 0, axis...  20.9 us
    pallas_call x6, Pallas kernels, call(): pl.pallas_call(body, out_shape=out_shape, in_specs=[pl.BlockSpec(memory_s...  6.85 us
    ppermute x1, starting transfers between devices, local(): other = lax.ppermute(mine, 'tensor', [(k, k ^ 1) for k in range(tensor)])  2.5 us
    ppermute x3, starting transfers between devices, local(): lax.ppermute(sums, 'tensor', [(k, k ^ d) for k in range(tensor)])  2.22 us
    ppermute x1, waiting for transfers between devices, local(): other = lax.ppermute(mine, 'tensor', [(k, k ^ 1) for k in range(tensor)])  2.06 us
  transfers between devices with their start and end apart: 4, of which 1 were waited for; matrix products, arithmetic and copies ran while one was open for 0% of the time, Pallas kernels for 3%

profile of v1, /device:TPU:1, one launch (start us, length us, event | category | flops | bytes accessed | tf_op | source)
XLA Modules:
  0.0 56.4 jit_solution(9312154171673523393)
XLA Ops:
  0.0 0.0 copy-start.2
  0.0 0.7 %copy-done.2 = s32[128,1]{0,1:T(1,128)S(1)} copy-done((s32[128,1]{0,1:T(1,128)S(1)}, s32[128,1]{0,1:T(1,128)}, u32[]{:S(2)}) %copy-start.2) | copy-done | bytes 536
  0.7 0.0 copy-start.1
  0.7 0.0 slice-start.4
  0.7 0.0 slice-start.5
  0.7 0.3 shard_map.73
  1.0 20.9 %all_to_all.10 = bf16[128,2,128]{2,1,0:T(2,128)(2,1)S(1)} all-to-all(bf16[128,2,128]{2,1,0:T(2,128)(2,1)S(1)} %bitcast.14), channel_id=1, replica_groups=mesh['dp'=32,'tensor'=4] {'dp','tensor'}, dimensions={0} | all-to-all | bytes 131072 | tf_op jit(solution)/shard_map/all_to_all | solution.py:143
  21.9 0.0 slice-start
  21.9 0.0 copy-done.1
  21.9 0.0 copy-start.3
  21.9 0.0 copy-start.4
  21.9 0.0 slice-start.6
  21.9 0.0 slice-start.7
  21.9 0.0 copy-start
  22.0 0.0 slice-start.1
  22.0 0.0 slice-start.2
  22.0 0.0 slice-start.3
  22.0 0.4 shard_map.74
  22.4 20.9 %all_to_all.11 = bf16[64,8,896]{2,1,0:T(8,128)(2,1)S(1)} all-to-all(bf16[64,8,896]{2,1,0:T(8,128)(2,1)S(1)} %bitcast.11), channel_id=1, replica_groups={{0,2,4,6,8,10,12,14,16,18,20,22,24,26,28,30,32,34,36,38,40,42,44,46,48,..., dimensions={0} | all-to-all | bytes 1835008 | tf_op jit(solution)/shard_map/all_to_all | solution.py:147
  43.3 1.2 %shard_map.75.mine_ref = bf16[128,3584]{1,0:T(8,128)(2,1)S(1)} custom-call(s32[1]{0:T(128)} %bitcast.where_ref, bf16[256,128]{1,0:T(8,128)(2,1)S(1)} %bitcast.13, bf16[512,896]{1,0:T(8,128)(2,1)S(1)} %bitcast.10), custom_call_target="tpu_custom_call" | custom-call | tf_op jit(solution)/shard_map/pallas_call | solution.py:31
  44.5 2.5 %collective-permute-start = (bf16[128,3584]{1,0:T(8,128)(2,1)S(1)}, bf16[128,3584]{1,0:T(8,128)(2,1)S(1)}, u32[]{:S(2)}, u32[]{:S(2)}) collective-permute-start(bf16[128,3584]{1,0:T(8,128)(2,1)S(1)} %shard_map.75.mine_ref), channel_id=1, source_target_pairs={{0,1},{1,0},{2,3},{3,2},{4,5},{5,4},{6,7},{7,6},{8,9},{9,8},{10,11... | collective-permute-start | bytes 2752520 | tf_op jit(solution)/shard_map/ppermute | solution.py:157
  47.0 0.0 copy-done.3
  47.0 0.0 copy-done.4
  47.1 2.1 %collective-permute-done.other_ref = bf16[128,3584]{1,0:T(8,128)(2,1)S(1)} collective-permute-done((bf16[128,3584]{1,0:T(8,128)(2,1)S(1)}, bf16[128,3584]{1,0:T(8,128)(2,1)S(1)}, u32[]{:S(2)}, u32[]{:S(2)}) %collective-permute-start) | collective-permute-done | bytes 917536 | tf_op jit(solution)/shard_map/ppermute | solution.py:157
  49.1 0.0 slice-done.4
  49.1 0.0 slice-done.5
  49.1 0.0 slice-done.6
  49.1 0.0 slice-done.7
  49.1 0.0 copy-done
  49.2 2.1 %shard_map.76 = (bf16[128,3584]{1,0:T(8,128)(2,1)S(1)}, f32[8,128]{1,0:T(8,128)S(1)}) custom-call(bf16[128,3584]{1,0:T(8,128)(2,1)S(1)} %shard_map.75.mine_ref, bf16[128,3584]{1,0:T(8,128)(2,1)S(1)} %collective-permute-done.other_ref, bf16[3584,1792]{1,0:T(8,128)(2,1)S(1)} %bitcast.9, bf16[128,1792]{1,0:T(8,128)(2,1)S(1)} %copy-done, ...), custom_call_target="tpu_custom_call" | custom-call | flops 1644167168 | tf_op jit(solution)/shard_map/pallas_call | solution.py:31
  51.2 0.6 %collective-permute-start.3 = (f32[8,128]{1,0:T(8,128)S(1)}, f32[8,128]{1,0:T(8,128)S(1)}, u32[]{:S(2)}, u32[]{:S(2)}) collective-permute-start(f32[8,128]{1,0:T(8,128)S(1)} %get-tuple-element.15.s0_ref), channel_id=1, source_target_pairs={{0,3},{1,2},{2,1},{3,0},{4,7},{5,6},{6,5},{7,4},{8,11},{9,10},{10,... | collective-permute-start | bytes 12296 | tf_op jit(solution)/shard_map/ppermute | solution.py:168
  51.9 1.2 %collective-permute-start.2 = (f32[8,128]{1,0:T(8,128)S(1)}, f32[8,128]{1,0:T(8,128)S(1)}, u32[]{:S(2)}, u32[]{:S(2)}) collective-permute-start(f32[8,128]{1,0:T(8,128)S(1)} %get-tuple-element.15.s0_ref), channel_id=1, source_target_pairs={{0,2},{1,3},{2,0},{3,1},{4,6},{5,7},{6,4},{7,5},{8,10},{9,11},{10,... | collective-permute-start | bytes 12296 | tf_op jit(solution)/shard_map/ppermute | solution.py:168
  53.0 0.4 collective-permute-start.1
  53.5 0.0 slice-done
  53.5 0.0 slice-done.1
  53.5 0.0 slice-done.2
  53.5 0.0 slice-done.3
  53.5 1.8 %shard_map.77.projected_ref = f32[128,1792]{1,0:T(8,128)S(1)} custom-call(bf16[128,3584]{1,0:T(8,128)(2,1)S(1)} %get-tuple-element.16.memory_ref, bf16[3584,1792]{1,0:T(8,128)(2,1)S(1)} %bitcast.7), custom_call_target="tpu_custom_call" | custom-call | flops 1644167168 | tf_op jit(solution)/shard_map/pallas_call | solution.py:31
  55.3 0.0 collective-permute-done.3.s3_ref
  55.3 0.0 collective-permute-done.2.s2_ref
  55.3 0.0 collective-permute-done.1.s1_ref
  55.3 1.0 %shard_map.78 = bf16[128,1792]{1,0:T(8,128)(2,1)} custom-call(f32[8,128]{1,0:T(8,128)S(1)} %get-tuple-element.15.s0_ref, f32[8,128]{1,0:T(8,128)S(1)} %collective-permute-done.1.s1_ref, f32[8,128]{1,0:T(8,128)S(1)} %collective-permute-done.2.s2_ref, f32[8,128]{1,0:T(8,128)S(1)} %collective-permute-done.3.s3_ref, bf16[128,1792]{1,0:T(8,128)(2,1)S(1)} %copy-done, ...), custom_call_target="tpu_custom_call" | custom-call | tf_op jit(solution)/shard_map/pallas_call | solution.py:31
  (4 shorter events, 0.0 us)
Async XLA Ops:
  0.0 0.7 %copy-start.2 = (s32[128,1]{0,1:T(1,128)S(1)}, s32[128,1]{0,1:T(1,128)}, u32[]{:S(2)}) copy-start(s32[128,1]{0,1:T(1,128)} %param.8) | copy-start | bytes 1540
  0.7 21.3 %copy-start.1 = (bf16[256,896]{1,0:T(8,128)(2,1)S(1)}, bf16[256,896]{1,0:T(8,128)(2,1)}, u32[]{:S(2)}) copy-start(bf16[256,896]{1,0:T(8,128)(2,1)} %table_ref.1) | copy-start | bytes 1376260
  0.7 48.5 %slice-start.4 = ((s8[12845056]{0:T(1024)(128)(4,1)}), s8[4194304]{0:T(1024)(128)(4,1)S(1)}, s32[]{:S(2)}) async-start(s8[12845056]{0:T(1024)(128)(4,1)} %bitcast.8), calls=%async_computation.6 | async-start | bytes 8388608
  0.7 48.5 %slice-start.5 = ((s8[12845056]{0:T(1024)(128)(4,1)}), s8[4194304]{0:T(1024)(128)(4,1)S(1)}, s32[]{:S(2)}) async-start(s8[12845056]{0:T(1024)(128)(4,1)} %bitcast.8), calls=%async_computation.7 | async-start | bytes 8388608
  21.9 31.6 %slice-start = ((s8[12845056]{0:T(1024)(128)(4,1)}), s8[4194304]{0:T(1024)(128)(4,1)S(1)}, s32[]{:S(2)}) async-start(s8[12845056]{0:T(1024)(128)(4,1)} %bitcast.6), calls=%async_computation.2 | async-start | bytes 8388608
  21.9 25.1 %copy-start.3 = (f32[1792]{0:T(1024)S(1)}, f32[1792]{0:T(1024)}, u32[]{:S(2)}) copy-start(f32[1792]{0:T(1024)} %param.12) | copy-start | bytes 21508
  21.9 25.1 %copy-start.4 = (f32[1792]{0:T(1024)S(1)}, f32[1792]{0:T(1024)}, u32[]{:S(2)}) copy-start(f32[1792]{0:T(1024)} %param.13) | copy-start | bytes 21508
  21.9 27.2 %slice-start.6 = ((s8[12845056]{0:T(1024)(128)(4,1)}), s8[4194304]{0:T(1024)(128)(4,1)S(1)}, s32[]{:S(2)}) async-start(s8[12845056]{0:T(1024)(128)(4,1)} %bitcast.8), calls=%async_computation.8 | async-start | bytes 8388608
  21.9 27.2 %slice-start.7 = ((s8[12845056]{0:T(1024)(128)(4,1)}), s8[262144]{0:T(1024)(128)(4,1)S(1)}, s32[]{:S(2)}) async-start(s8[12845056]{0:T(1024)(128)(4,1)} %bitcast.8), calls=%async_computation.9 | async-start | bytes 524288
  21.9 27.2 %copy-start = (bf16[128,1792]{1,0:T(8,128)(2,1)S(1)}, bf16[128,1792]{1,0:T(8,128)(2,1)}, u32[]{:S(2)}) copy-start(bf16[128,1792]{1,0:T(8,128)(2,1)} %hidden_ref.3) | copy-start | bytes 1376260
  22.0 31.5 %slice-start.1 = ((s8[12845056]{0:T(1024)(128)(4,1)}), s8[4194304]{0:T(1024)(128)(4,1)S(1)}, s32[]{:S(2)}) async-start(s8[12845056]{0:T(1024)(128)(4,1)} %bitcast.6), calls=%async_computation.3 | async-start | bytes 8388608
  22.0 31.5 %slice-start.2 = ((s8[12845056]{0:T(1024)(128)(4,1)}), s8[4194304]{0:T(1024)(128)(4,1)S(1)}, s32[]{:S(2)}) async-start(s8[12845056]{0:T(1024)(128)(4,1)} %bitcast.6), calls=%async_computation.4 | async-start | bytes 8388608
  22.0 31.5 %slice-start.3 = ((s8[12845056]{0:T(1024)(128)(4,1)}), s8[262144]{0:T(1024)(128)(4,1)S(1)}, s32[]{:S(2)}) async-start(s8[12845056]{0:T(1024)(128)(4,1)} %bitcast.6), calls=%async_computation.5 | async-start | bytes 524288
  44.5 4.6 %collective-permute-start = (bf16[128,3584]{1,0:T(8,128)(2,1)S(1)}, bf16[128,3584]{1,0:T(8,128)(2,1)S(1)}, u32[]{:S(2)}, u32[]{:S(2)}) collective-permute-start(bf16[128,3584]{1,0:T(8,128)(2,1)S(1)} %shard_map.75.mine_ref), channel_id=1, source_target_pairs={{0,1},{1,0},{2,3},{3,2},{4,5},{5,4},{6,7},{7,6},{8,9},{9,8},{10,11... | collective-permute-start | bytes 2752520 | tf_op jit(solution)/shard_map/ppermute | solution.py:157
  51.2 4.1 %collective-permute-start.3 = (f32[8,128]{1,0:T(8,128)S(1)}, f32[8,128]{1,0:T(8,128)S(1)}, u32[]{:S(2)}, u32[]{:S(2)}) collective-permute-start(f32[8,128]{1,0:T(8,128)S(1)} %get-tuple-element.15.s0_ref), channel_id=1, source_target_pairs={{0,3},{1,2},{2,1},{3,0},{4,7},{5,6},{6,5},{7,4},{8,11},{9,10},{10,... | collective-permute-start | bytes 12296 | tf_op jit(solution)/shard_map/ppermute | solution.py:168
  51.9 3.5 %collective-permute-start.2 = (f32[8,128]{1,0:T(8,128)S(1)}, f32[8,128]{1,0:T(8,128)S(1)}, u32[]{:S(2)}, u32[]{:S(2)}) collective-permute-start(f32[8,128]{1,0:T(8,128)S(1)} %get-tuple-element.15.s0_ref), channel_id=1, source_target_pairs={{0,2},{1,3},{2,0},{3,1},{4,6},{5,7},{6,4},{7,5},{8,10},{9,11},{10,... | collective-permute-start | bytes 12296 | tf_op jit(solution)/shard_map/ppermute | solution.py:168
  53.0 2.3 %collective-permute-start.1 = (f32[8,128]{1,0:T(8,128)S(1)}, f32[8,128]{1,0:T(8,128)S(1)}, u32[]{:S(2)}, u32[]{:S(2)}) collective-permute-start(f32[8,128]{1,0:T(8,128)S(1)} %get-tuple-element.15.s0_ref), channel_id=1, source_target_pairs={{0,1},{1,0},{2,3},{3,2},{4,5},{5,4},{6,7},{7,6},{8,9},{9,8},{10,11... | collective-permute-start | bytes 12296 | tf_op jit(solution)/shard_map/ppermute | solution.py:168

commit v2 on v1

--- a/solution.py
+++ b/solution.py
@@ -72,22 +72,21 @@
     out_ref[...] = jnp.concatenate([found, found], axis=1).reshape(2 * rows, -1)
 
 
-def place_kernel(where_ref, asked_ref, arrived_ref, out_ref):
+def place_kernel(heads, where_ref, asked_ref, arrived_ref, out_ref):
     core = where_ref[0] & 1
     start = pl.multiple_of((where_ref[0] >> 2) * 8, 8)
     asked = asked_ref[pl.ds(start, 8), :].astype(f32)
     arrived = arrived_ref[...]
     slots = arrived.shape[0]
     width = arrived.shape[1]
-    for head in range(4):
+    for k, head in enumerate(heads):
         position = jnp.broadcast_to(asked[2 * head : 2 * head + 1, :], (LANES, LANES)).T
         position = position[:, 0:1].astype(jnp.int32)
-        owner = position // 2
-        target = (owner // 2) * 8 + head * 2 + position % 2
-        target = jnp.where(owner % 2 == core, target, -1)
+        target = (position >> 2) * 8 + head * 2 + (position & 1)
+        target = jnp.where(((position >> 1) & 1) == core, target, -1)
         chosen = (target == iota((LANES, slots), 1)).astype(f32).astype(bf16)
         found = jnp.dot(chosen, arrived, preferred_element_type=f32)
-        out_ref[:, head * width : (head + 1) * width] = found.astype(bf16)
+        out_ref[:, k * width : (k + 1) * width] = found.astype(bf16)
 
 
 def row_of_sums(terms):
@@ -97,10 +96,17 @@
     return jnp.sum(parts.T, axis=0, keepdims=True)
 
 
-def key_kernel(mine_ref, other_ref, weight_ref, hidden_ref, hgain_ref, kgain_ref, memory_ref, sums_ref):
+def first_kernel(mine_ref, other_ref, key_weight_ref, value_weight_ref, key_ref, value_ref):
     memory = mine_ref[...] + other_ref[...]
-    memory_ref[...] = memory
-    key = jnp.dot(memory, weight_ref[...], preferred_element_type=f32)
+    depth = memory.shape[1]
+    key_ref[...] = jnp.dot(memory, key_weight_ref[:depth, :], preferred_element_type=f32)
+    value_ref[...] = jnp.dot(memory, value_weight_ref[:depth, :], preferred_element_type=f32)
+
+
+def key_kernel(mine_ref, other_ref, weight_ref, first_ref, hidden_ref, hgain_ref, kgain_ref, sums_ref):
+    memory = mine_ref[...] + other_ref[...]
+    depth = memory.shape[1]
+    key = first_ref[...] + jnp.dot(memory, weight_ref[depth:, :], preferred_element_type=f32)
     hidden = hidden_ref[...].astype(f32)
     sums = [
         row_of_sums(hidden * hidden),
@@ -110,8 +116,10 @@
     sums_ref[...] = jnp.concatenate(sums + [jnp.zeros((5, LANES), f32)], axis=0)
 
 
-def value_kernel(memory_ref, weight_ref, out_ref):
-    out_ref[...] = jnp.dot(memory_ref[...], weight_ref[...], preferred_element_type=f32)
+def value_kernel(mine_ref, other_ref, weight_ref, first_ref, out_ref):
+    memory = mine_ref[...] + other_ref[...]
+    depth = memory.shape[1]
+    out_ref[...] = first_ref[...] + jnp.dot(memory, weight_ref[depth:, :], preferred_element_type=f32)
 
 
 def join_kernel(s0_ref, s1_ref, s2_ref, s3_ref, hidden_ref, projected_ref, out_ref):
@@ -147,32 +155,33 @@
     arrived = lax.all_to_all(
         sent.reshape(devices // 2, 8, row_width), BOTH, 0, 0, axis_index_groups=same_core, tiled=True
     ).reshape(4 * devices, row_width)
-    mine = call(
-        place_kernel,
-        shape((LANES, 4 * row_width), bf16),
-        [asked, arrived],
-        6 * MIB,
-        scalars=[here],
-    )
-    other = lax.ppermute(mine, "tensor", [(k, k ^ 1) for k in range(tensor)])
+    halves = []
+    for heads in ((0, 1), (2, 3)):
+        mine = call(
+            lambda *refs, heads=heads: place_kernel(heads, *refs),
+            shape((LANES, 2 * row_width), bf16),
+            [asked, arrived],
+            6 * MIB,
+            scalars=[here],
+        )
+        halves.append((mine, lax.ppermute(mine, "tensor", [(k, k ^ 1) for k in range(tensor)])))
     columns = key_weight.shape[1]
+    work = 2 * LANES * 2 * row_width * columns
     key_weight = pltpu.with_memory_space_constraint(key_weight, pltpu.VMEM)
     value_weight = pltpu.with_memory_space_constraint(value_weight, pltpu.VMEM)
-    memory, sums = call(
+    partial = shape((LANES, columns), f32)
+    key, value = call(
+        first_kernel, (partial, partial), [*halves[0], key_weight, value_weight], 6 * MIB, flops=2 * work
+    )
+    sums = call(
         key_kernel,
-        (shape(mine.shape, bf16), shape((8, LANES), f32)),
-        [mine, other, key_weight, hidden, hidden_gain.reshape(1, columns), key_gain.reshape(1, columns)],
+        shape((8, LANES), f32),
+        [*halves[1], key_weight, key, hidden, hidden_gain.reshape(1, columns), key_gain.reshape(1, columns)],
         6 * MIB,
-        flops=2 * LANES * mine.shape[1] * columns,
+        flops=work,
     )
     others = [lax.ppermute(sums, "tensor", [(k, k ^ d) for k in range(tensor)]) for d in (1, 2, 3)]
-    projected = call(
-        value_kernel,
-        shape((LANES, columns), f32),
-        [memory, value_weight],
-        6 * MIB,
-        flops=2 * LANES * mine.shape[1] * columns,
-    )
+    projected = call(value_kernel, partial, [*halves[1], value_weight, value], 6 * MIB, flops=work)
     return call(join_kernel, shape(hidden.shape, bf16), [sums, *others, hidden, projected], 6 * MIB)
 
 

time: 56.5 us -> 56 us (level)
  waiting for transfers between devices: 2.07 us -> 1.29 us
    ppermute x1 -> x2, waiting for transfers between devices: 2.06 us -> 0.72 us  [local(): lax.ppermute(mine, 'tensor', [(k, k ^ 1) for k in range(tensor)])]
    ppermute x3, waiting for transfers between devices: 0.01 us -> 0.57 us  [local(): lax.ppermute(sums, 'tensor', [(k, k ^ d) for k in range(tensor)])]
    pallas_call x6 -> x8, Pallas kernels: 6.85 us -> 6.97 us  [call(): pl.pallas_call(body, out_shape=out_shape, in_specs=[pl.BlockSpec(memory_s...]
    ppermute x1 -> x2, starting transfers between devices: 2.5 us -> 2.58 us  [local(): lax.ppermute(mine, 'tensor', [(k, k ^ 1) for k in range(tensor)])]
  transfers between devices with their start and end apart: 4 -> 5, of which waited for: 1 -> 2; matrix products, arithmetic and copies ran while one was open for 0% -> 0% of each run, Pallas kernels for 3% -> 6%
where the time goes in v2:
time: 56 us; the launch traced here: 55.9 us
  blocking collectives  41.8 us (75%)
  Pallas kernels  6.97 us (12%)
  starting transfers between devices  4.8 us (9%)
  waiting for transfers between devices  1.29 us (2%)
  local copies, waits for them, and re-layouts  0.72 us (1%)
    all_to_all x1, blocking collectives, local(): lax.all_to_all(message.reshape(devices, 2, LANES), BOTH, 0, 0, tiled=True)  20.9 us
    all_to_all x1, blocking collectives, local(): lax.all_to_all(sent.reshape(devices // 2, 8, row_width), BOTH, 0, 0, axis...  20.9 us
    pallas_call x8, Pallas kernels, call(): pl.pallas_call(body, out_shape=out_shape, in_specs=[pl.BlockSpec(memory_s...  6.97 us
    ppermute x2, starting transfers between devices, local(): lax.ppermute(mine, 'tensor', [(k, k ^ 1) for k in range(tensor)])  2.58 us
    ppermute x3, starting transfers between devices, local(): lax.ppermute(sums, 'tensor', [(k, k ^ d) for k in range(tensor)])  2.22 us
  transfers between devices with their start and end apart: 5, of which 2 were waited for; matrix products, arithmetic and copies ran while one was open for 0% of the time, Pallas kernels for 6%

profile of v2, /device:TPU:1, one launch (start us, length us, event | category | flops | bytes accessed | tf_op | source)
XLA Modules:
  0.0 55.9 jit_solution(16903397176204807768)
XLA Ops:
  0.0 0.0 copy-start.2
  0.0 0.7 %copy-done.2 = s32[128,1]{0,1:T(1,128)S(1)} copy-done((s32[128,1]{0,1:T(1,128)S(1)}, s32[128,1]{0,1:T(1,128)}, u32[]{:S(2)}) %copy-start.2) | copy-done | bytes 536
  0.7 0.0 copy-start.1
  0.7 0.0 slice-start
  0.7 0.0 slice-start.1
  0.7 0.0 slice-start.4
  0.7 0.0 slice-start.5
  0.7 0.3 shard_map.73
  1.0 20.9 %all_to_all.10 = bf16[128,2,128]{2,1,0:T(2,128)(2,1)S(1)} all-to-all(bf16[128,2,128]{2,1,0:T(2,128)(2,1)S(1)} %bitcast.16), channel_id=1, replica_groups=mesh['dp'=32,'tensor'=4] {'dp','tensor'}, dimensions={0} | all-to-all | bytes 131072 | tf_op jit(solution)/shard_map/all_to_all | solution.py:151
  21.9 0.0 copy-done.1
  21.9 0.0 copy-start.3
  21.9 0.0 copy-start.4
  21.9 0.0 slice-start.2
  21.9 0.0 slice-start.3
  21.9 0.0 slice-start.6
  22.0 0.0 slice-start.7
  22.0 0.5 shard_map.74
  22.4 20.9 %all_to_all.11 = bf16[64,8,896]{2,1,0:T(8,128)(2,1)S(1)} all-to-all(bf16[64,8,896]{2,1,0:T(8,128)(2,1)S(1)} %bitcast.12), channel_id=1, replica_groups={{0,2,4,6,8,10,12,14,16,18,20,22,24,26,28,30,32,34,36,38,40,42,44,46,48,..., dimensions={0} | all-to-all | bytes 1835008 | tf_op jit(solution)/shard_map/all_to_all | solution.py:155
  43.3 0.6 %shard_map.76.mine_ref = bf16[128,1792]{1,0:T(8,128)(2,1)S(1)} custom-call(s32[1]{0:T(128)} %bitcast.refs_0_, bf16[256,128]{1,0:T(8,128)(2,1)S(1)} %bitcast.14, bf16[512,896]{1,0:T(8,128)(2,1)S(1)} %bitcast.10), custom_call_target="tpu_custom_call" | custom-call | tf_op jit(solution)/shard_map/pallas_call | solution.py:31
  43.9 2.5 %collective-permute-start.1 = (bf16[128,1792]{1,0:T(8,128)(2,1)S(1)}, bf16[128,1792]{1,0:T(8,128)(2,1)S(1)}, u32[]{:S(2)}, u32[]{:S(2)}) collective-permute-start(bf16[128,1792]{1,0:T(8,128)(2,1)S(1)} %shard_map.76.mine_ref), channel_id=1, source_target_pairs={{0,1},{1,0},{2,3},{3,2},{4,5},{5,4},{6,7},{7,6},{8,9},{9,8},{10,11... | collective-permute-start | bytes 1376264 | tf_op jit(solution)/shard_map/ppermute | solution.py:167
  46.4 0.6 %shard_map.75.mine_ref = bf16[128,1792]{1,0:T(8,128)(2,1)S(1)} custom-call(s32[1]{0:T(128)} %bitcast.refs_0_, bf16[256,128]{1,0:T(8,128)(2,1)S(1)} %bitcast.15, bf16[512,896]{1,0:T(8,128)(2,1)S(1)} %bitcast.11), custom_call_target="tpu_custom_call" | custom-call | tf_op jit(solution)/shard_map/pallas_call | solution.py:31
  47.0 0.1 collective-permute-start
  47.1 0.0 copy-done.3
  47.1 0.0 copy-done.4
  47.1 0.0 copy-start
  47.1 0.7 %collective-permute-done.1.other_ref = bf16[128,1792]{1,0:T(8,128)(2,1)S(1)} collective-permute-done((bf16[128,1792]{1,0:T(8,128)(2,1)S(1)}, bf16[128,1792]{1,0:T(8,128)(2,1)S(1)}, u32[]{:S(2)}, u32[]{:S(2)}) %collective-permute-start.1) | collective-permute-done | bytes 458784 | tf_op jit(solution)/shard_map/ppermute | solution.py:167
  47.8 0.0 slice-done
  47.8 0.0 slice-done.1
  47.9 0.0 slice-done.4
  47.9 0.0 slice-done.5
  47.9 0.0 slice-done.2
  47.9 0.0 slice-done.3
  47.9 0.0 slice-done.6
  47.9 0.0 slice-done.7
  47.9 1.9 %shard_map.77 = (f32[128,1792]{1,0:T(8,128)S(1)}, f32[128,1792]{1,0:T(8,128)S(1)}) custom-call(bf16[128,1792]{1,0:T(8,128)(2,1)S(1)} %shard_map.76.mine_ref, bf16[128,1792]{1,0:T(8,128)(2,1)S(1)} %collective-permute-done.1.other_ref, bf16[3584,1792]{1,0:T(8,128)(2,1)S(1)} %bitcast.7, bf16[3584,1792]{1,0:T(8,128)(2,1)S(1)} %bitcast.9), custom_call_target="tpu_custom_call" | custom-call | flops 1644167168 | tf_op jit(solution)/shard_map/pallas_call | solution.py:31
  49.8 0.0 collective-permute-done.other_ref
  49.8 0.0 copy-done
  49.8 1.1 %shard_map.78.s0_ref = f32[8,128]{1,0:T(8,128)S(1)} custom-call(bf16[128,1792]{1,0:T(8,128)(2,1)S(1)} %shard_map.75.mine_ref, bf16[128,1792]{1,0:T(8,128)(2,1)S(1)} %collective-permute-done.other_ref, bf16[3584,1792]{1,0:T(8,128)(2,1)S(1)} %bitcast.7, f32[128,1792]{1,0:T(8,128)S(1)} %get-tuple-element.13.first_ref, bf16[128,1792]{1,0:T(8,128)(2,1)S(1)} %copy-done, ...), custom_call_target="tpu_custom_call" | custom-call | flops 822083584 | tf_op jit(solution)/shard_map/pallas_call | solution.py:31
  51.0 0.5 collective-permute-start.2
  51.4 0.3 collective-permute-start.3
  51.7 1.5 %collective-permute-start.4 = (f32[8,128]{1,0:T(8,128)S(1)}, f32[8,128]{1,0:T(8,128)S(1)}, u32[]{:S(2)}, u32[]{:S(2)}) collective-permute-start(f32[8,128]{1,0:T(8,128)S(1)} %shard_map.78.s0_ref), channel_id=1, source_target_pairs={{0,3},{1,2},{2,1},{3,0},{4,7},{5,6},{6,5},{7,4},{8,11},{9,10},{10,... | collective-permute-start | bytes 12296 | tf_op jit(solution)/shard_map/ppermute | solution.py:183
  53.2 1.0 %shard_map.79.projected_ref = f32[128,1792]{1,0:T(8,128)S(1)} custom-call(bf16[128,1792]{1,0:T(8,128)(2,1)S(1)} %shard_map.75.mine_ref, bf16[128,1792]{1,0:T(8,128)(2,1)S(1)} %collective-permute-done.other_ref, bf16[3584,1792]{1,0:T(8,128)(2,1)S(1)} %bitcast.9, f32[128,1792]{1,0:T(8,128)S(1)} %get-tuple-element.16.first_ref), custom_call_target="tpu_custom_call" | custom-call | flops 822083584 | tf_op jit(solution)/shard_map/pallas_call | solution.py:31
  54.2 0.0 collective-permute-done.2.s1_ref
  54.2 0.0 collective-permute-done.3.s2_ref
  54.2 0.6 %collective-permute-done.4.s3_ref = f32[8,128]{1,0:T(8,128)S(1)} collective-permute-done((f32[8,128]{1,0:T(8,128)S(1)}, f32[8,128]{1,0:T(8,128)S(1)}, u32[]{:S(2)}, u32[]{:S(2)}) %collective-permute-start.4) | collective-permute-done | bytes 4128 | tf_op jit(solution)/shard_map/ppermute | solution.py:183
  54.8 1.0 %shard_map.80 = bf16[128,1792]{1,0:T(8,128)(2,1)} custom-call(f32[8,128]{1,0:T(8,128)S(1)} %shard_map.78.s0_ref, f32[8,128]{1,0:T(8,128)S(1)} %collective-permute-done.2.s1_ref, f32[8,128]{1,0:T(8,128)S(1)} %collective-permute-done.3.s2_ref, f32[8,128]{1,0:T(8,128)S(1)} %collective-permute-done.4.s3_ref, bf16[128,1792]{1,0:T(8,128)(2,1)S(1)} %copy-done, ...), custom_call_target="tpu_custom_call" | custom-call | tf_op jit(solution)/shard_map/pallas_call | solution.py:31
  (4 shorter events, 0.0 us)
Async XLA Ops:
  0.0 0.7 %copy-start.2 = (s32[128,1]{0,1:T(1,128)S(1)}, s32[128,1]{0,1:T(1,128)}, u32[]{:S(2)}) copy-start(s32[128,1]{0,1:T(1,128)} %param.8) | copy-start | bytes 1540
  0.7 21.3 %copy-start.1 = (bf16[256,896]{1,0:T(8,128)(2,1)S(1)}, bf16[256,896]{1,0:T(8,128)(2,1)}, u32[]{:S(2)}) copy-start(bf16[256,896]{1,0:T(8,128)(2,1)} %table_ref.1) | copy-start | bytes 1376260
  0.7 47.2 %slice-start = ((s8[12845056]{0:T(1024)(128)(4,1)}), s8[4194304]{0:T(1024)(128)(4,1)S(1)}, s32[]{:S(2)}) async-start(s8[12845056]{0:T(1024)(128)(4,1)} %bitcast.6), calls=%async_computation.2 | async-start | bytes 8388608
  0.7 47.2 %slice-start.1 = ((s8[12845056]{0:T(1024)(128)(4,1)}), s8[4194304]{0:T(1024)(128)(4,1)S(1)}, s32[]{:S(2)}) async-start(s8[12845056]{0:T(1024)(128)(4,1)} %bitcast.6), calls=%async_computation.3 | async-start | bytes 8388608
  0.7 47.2 %slice-start.4 = ((s8[12845056]{0:T(1024)(128)(4,1)}), s8[4194304]{0:T(1024)(128)(4,1)S(1)}, s32[]{:S(2)}) async-start(s8[12845056]{0:T(1024)(128)(4,1)} %bitcast.8), calls=%async_computation.6 | async-start | bytes 8388608
  0.7 47.2 %slice-start.5 = ((s8[12845056]{0:T(1024)(128)(4,1)}), s8[4194304]{0:T(1024)(128)(4,1)S(1)}, s32[]{:S(2)}) async-start(s8[12845056]{0:T(1024)(128)(4,1)} %bitcast.8), calls=%async_computation.7 | async-start | bytes 8388608
  21.9 25.1 %copy-start.3 = (f32[1792]{0:T(1024)S(1)}, f32[1792]{0:T(1024)}, u32[]{:S(2)}) copy-start(f32[1792]{0:T(1024)} %param.12) | copy-start | bytes 21508
  21.9 25.2 %copy-start.4 = (f32[1792]{0:T(1024)S(1)}, f32[1792]{0:T(1024)}, u32[]{:S(2)}) copy-start(f32[1792]{0:T(1024)} %param.13) | copy-start | bytes 21508
  21.9 25.9 %slice-start.2 = ((s8[12845056]{0:T(1024)(128)(4,1)}), s8[4194304]{0:T(1024)(128)(4,1)S(1)}, s32[]{:S(2)}) async-start(s8[12845056]{0:T(1024)(128)(4,1)} %bitcast.6), calls=%async_computation.4 | async-start | bytes 8388608
  21.9 25.9 %slice-start.3 = ((s8[12845056]{0:T(1024)(128)(4,1)}), s8[262144]{0:T(1024)(128)(4,1)S(1)}, s32[]{:S(2)}) async-start(s8[12845056]{0:T(1024)(128)(4,1)} %bitcast.6), calls=%async_computation.5 | async-start | bytes 524288
  21.9 25.9 %slice-start.6 = ((s8[12845056]{0:T(1024)(128)(4,1)}), s8[4194304]{0:T(1024)(128)(4,1)S(1)}, s32[]{:S(2)}) async-start(s8[12845056]{0:T(1024)(128)(4,1)} %bitcast.8), calls=%async_computation.8 | async-start | bytes 8388608
  22.0 25.9 %slice-start.7 = ((s8[12845056]{0:T(1024)(128)(4,1)}), s8[262144]{0:T(1024)(128)(4,1)S(1)}, s32[]{:S(2)}) async-start(s8[12845056]{0:T(1024)(128)(4,1)} %bitcast.8), calls=%async_computation.9 | async-start | bytes 524288
  43.9 3.9 %collective-permute-start.1 = (bf16[128,1792]{1,0:T(8,128)(2,1)S(1)}, bf16[128,1792]{1,0:T(8,128)(2,1)S(1)}, u32[]{:S(2)}, u32[]{:S(2)}) collective-permute-start(bf16[128,1792]{1,0:T(8,128)(2,1)S(1)} %shard_map.76.mine_ref), channel_id=1, source_target_pairs={{0,1},{1,0},{2,3},{3,2},{4,5},{5,4},{6,7},{7,6},{8,9},{9,8},{10,11... | collective-permute-start | bytes 1376264 | tf_op jit(solution)/shard_map/ppermute | solution.py:167
  47.0 2.8 %collective-permute-start = (bf16[128,1792]{1,0:T(8,128)(2,1)S(1)}, bf16[128,1792]{1,0:T(8,128)(2,1)S(1)}, u32[]{:S(2)}, u32[]{:S(2)}) collective-permute-start(bf16[128,1792]{1,0:T(8,128)(2,1)S(1)} %shard_map.75.mine_ref), channel_id=1, source_target_pairs={{0,1},{1,0},{2,3},{3,2},{4,5},{5,4},{6,7},{7,6},{8,9},{9,8},{10,11... | collective-permute-start | bytes 1376264 | tf_op jit(solution)/shard_map/ppermute | solution.py:167
  47.1 2.7 %copy-start = (bf16[128,1792]{1,0:T(8,128)(2,1)S(1)}, bf16[128,1792]{1,0:T(8,128)(2,1)}, u32[]{:S(2)}) copy-start(bf16[128,1792]{1,0:T(8,128)(2,1)} %hidden_ref.3) | copy-start | bytes 1376260
  51.0 3.3 %collective-permute-start.2 = (f32[8,128]{1,0:T(8,128)S(1)}, f32[8,128]{1,0:T(8,128)S(1)}, u32[]{:S(2)}, u32[]{:S(2)}) collective-permute-start(f32[8,128]{1,0:T(8,128)S(1)} %shard_map.78.s0_ref), channel_id=1, source_target_pairs={{0,1},{1,0},{2,3},{3,2},{4,5},{5,4},{6,7},{7,6},{8,9},{9,8},{10,11... | collective-permute-start | bytes 12296 | tf_op jit(solution)/shard_map/ppermute | solution.py:183
  51.4 2.8 %collective-permute-start.3 = (f32[8,128]{1,0:T(8,128)S(1)}, f32[8,128]{1,0:T(8,128)S(1)}, u32[]{:S(2)}, u32[]{:S(2)}) collective-permute-start(f32[8,128]{1,0:T(8,128)S(1)} %shard_map.78.s0_ref), channel_id=1, source_target_pairs={{0,2},{1,3},{2,0},{3,1},{4,6},{5,7},{6,4},{7,5},{8,10},{9,11},{10,... | collective-permute-start | bytes 12296 | tf_op jit(solution)/shard_map/ppermute | solution.py:183
  51.7 3.1 %collective-permute-start.4 = (f32[8,128]{1,0:T(8,128)S(1)}, f32[8,128]{1,0:T(8,128)S(1)}, u32[]{:S(2)}, u32[]{:S(2)}) collective-permute-start(f32[8,128]{1,0:T(8,128)S(1)} %shard_map.78.s0_ref), channel_id=1, source_target_pairs={{0,3},{1,2},{2,1},{3,0},{4,7},{5,6},{6,5},{7,4},{8,11},{9,10},{10,... | collective-permute-start | bytes 12296 | tf_op jit(solution)/shard_map/ppermute | solution.py:183

commit v3 on v2

--- a/solution.py
+++ b/solution.py
@@ -16,6 +16,19 @@
 
 f32 = jnp.float32
 bf16 = jnp.bfloat16
+
+
+def chip_order():
+    order = []
+    for k in range(64):
+        a, b, c = k % 4, (k // 4) % 4, k // 16
+        order.append(a * 16 + (a + b) % 4 * 4 + (a + b + c) % 4)
+    return order
+
+
+def turn_of(chip):
+    z, y, x = chip >> 4, (chip >> 2) & 3, chip & 3
+    return z + ((y - z) & 3) * 4 + ((x - y) & 3) * 16
 
 
 def iota(shape, dim):
@@ -68,23 +81,23 @@
     held = table_ref.shape[0]
     chosen = (index.astype(jnp.int32) == iota((rows, held), 1)).astype(f32).astype(bf16)
     found = jnp.dot(chosen, table_ref[...], preferred_element_type=f32)
-    found = found.astype(bf16).reshape(rows // 8, 1, 8, found.shape[1])
-    out_ref[...] = jnp.concatenate([found, found], axis=1).reshape(2 * rows, -1)
+    turns = [found[chip // 2 * 8 : chip // 2 * 8 + 8] for chip in chip_order()]
+    out_ref[...] = jnp.concatenate(turns, axis=0).astype(bf16)
 
 
 def place_kernel(heads, where_ref, asked_ref, arrived_ref, out_ref):
     core = where_ref[0] & 1
     start = pl.multiple_of((where_ref[0] >> 2) * 8, 8)
-    asked = asked_ref[pl.ds(start, 8), :].astype(f32)
+    position = asked_ref[pl.ds(start, 8), :].astype(jnp.int32)
+    target = turn_of(position >> 2) * 8 + (position & 1)
+    target = jnp.where(((position >> 1) & 1) == core, target, -8).astype(f32)
     arrived = arrived_ref[...]
     slots = arrived.shape[0]
     width = arrived.shape[1]
     for k, head in enumerate(heads):
-        position = jnp.broadcast_to(asked[2 * head : 2 * head + 1, :], (LANES, LANES)).T
-        position = position[:, 0:1].astype(jnp.int32)
-        target = (position >> 2) * 8 + head * 2 + (position & 1)
-        target = jnp.where(((position >> 1) & 1) == core, target, -1)
-        chosen = (target == iota((LANES, slots), 1)).astype(f32).astype(bf16)
+        column = jnp.broadcast_to(target[2 * head : 2 * head + 1, :], (LANES, LANES)).T
+        column = column[:, 0:1].astype(jnp.int32) + 2 * head
+        chosen = (column == iota((LANES, slots), 1)).astype(f32).astype(bf16)
         found = jnp.dot(chosen, arrived, preferred_element_type=f32)
         out_ref[:, k * width : (k + 1) * width] = found.astype(bf16)
 
@@ -96,17 +109,20 @@
     return jnp.sum(parts.T, axis=0, keepdims=True)
 
 
-def first_kernel(mine_ref, other_ref, key_weight_ref, value_weight_ref, key_ref, value_ref):
+def first_kernel(mine_ref, other_ref, weight_ref, out_ref):
     memory = mine_ref[...] + other_ref[...]
-    depth = memory.shape[1]
-    key_ref[...] = jnp.dot(memory, key_weight_ref[:depth, :], preferred_element_type=f32)
-    value_ref[...] = jnp.dot(memory, value_weight_ref[:depth, :], preferred_element_type=f32)
+    out_ref[...] = jnp.dot(memory, weight_ref[: memory.shape[1], :], preferred_element_type=f32)
+
+
+def second_kernel(mine_ref, other_ref, weight_ref, first_ref, out_ref):
+    memory = mine_ref[...] + other_ref[...]
+    more = jnp.dot(memory, weight_ref[memory.shape[1] :, :], preferred_element_type=f32)
+    out_ref[...] = first_ref[...] + more
 
 
 def key_kernel(mine_ref, other_ref, weight_ref, first_ref, hidden_ref, hgain_ref, kgain_ref, sums_ref):
     memory = mine_ref[...] + other_ref[...]
-    depth = memory.shape[1]
-    key = first_ref[...] + jnp.dot(memory, weight_ref[depth:, :], preferred_element_type=f32)
+    key = first_ref[...] + jnp.dot(memory, weight_ref[memory.shape[1] :, :], preferred_element_type=f32)
     hidden = hidden_ref[...].astype(f32)
     sums = [
         row_of_sums(hidden * hidden),
@@ -116,20 +132,24 @@
     sums_ref[...] = jnp.concatenate(sums + [jnp.zeros((5, LANES), f32)], axis=0)
 
 
-def value_kernel(mine_ref, other_ref, weight_ref, first_ref, out_ref):
-    memory = mine_ref[...] + other_ref[...]
-    depth = memory.shape[1]
-    out_ref[...] = first_ref[...] + jnp.dot(memory, weight_ref[depth:, :], preferred_element_type=f32)
-
-
-def join_kernel(s0_ref, s1_ref, s2_ref, s3_ref, hidden_ref, projected_ref, out_ref):
-    sums = (s0_ref[...] + s1_ref[...]) + (s2_ref[...] + s3_ref[...])
+def join_kernel(chunks, here_ref, there_ref, hidden_ref, projected_ref, out_ref, joined_ref, sems):
+    sums = here_ref[...] + there_ref[...]
     hidden_power = sums[0:1] / D
     key_power = sums[1:2] / D
     agreement = sums[2:3] * lax.rsqrt(hidden_power + EPSILON) * lax.rsqrt(key_power + EPSILON)
     gate = jax.nn.sigmoid(agreement / math.sqrt(D))
     gate = jnp.broadcast_to(gate, (LANES, LANES)).T[:, 0:1]
-    out_ref[...] = (hidden_ref[...].astype(f32) + gate * projected_ref[...]).astype(bf16)
+    rows = LANES // chunks
+    copies = []
+    for k in range(chunks):
+        part = slice(k * rows, (k + 1) * rows)
+        joined = hidden_ref[part, :].astype(f32) + gate[part] * projected_ref[part, :]
+        joined_ref[part, :] = joined.astype(bf16)
+        copy = pltpu.make_async_copy(joined_ref.at[part, :], out_ref.at[part, :], sems.at[k])
+        copy.start()
+        copies.append(copy)
+    for copy in copies:
+        copy.wait()
 
 
 def local(hidden, hash_rows, memory_table, key_weight, value_weight, hidden_gain, key_gain):
@@ -151,7 +171,7 @@
     asked = lax.all_to_all(message.reshape(devices, 2, LANES), BOTH, 0, 0, tiled=True)
     asked = asked.reshape(2 * devices, LANES)
     sent = call(gather_kernel, shape((4 * devices, row_width), bf16), [asked, memory_table], 6 * MIB, flops=COVER)
-    same_core = [[2 * k + c for k in range(devices // 2)] for c in range(2)]
+    same_core = [[2 * chip + core for chip in chip_order()] for core in range(2)]
     arrived = lax.all_to_all(
         sent.reshape(devices // 2, 8, row_width), BOTH, 0, 0, axis_index_groups=same_core, tiled=True
     ).reshape(4 * devices, row_width)
@@ -170,8 +190,12 @@
     key_weight = pltpu.with_memory_space_constraint(key_weight, pltpu.VMEM)
     value_weight = pltpu.with_memory_space_constraint(value_weight, pltpu.VMEM)
     partial = shape((LANES, columns), f32)
-    key, value = call(
-        first_kernel, (partial, partial), [*halves[0], key_weight, value_weight], 6 * MIB, flops=2 * work
+    key = call(
+        lambda mine, other, weight, _, out: first_kernel(mine, other, weight, out),
+        partial,
+        [*halves[0], key_weight, value_weight],
+        6 * MIB,
+        flops=work,
     )
     sums = call(
         key_kernel,
@@ -180,9 +204,22 @@
         6 * MIB,
         flops=work,
     )
-    others = [lax.ppermute(sums, "tensor", [(k, k ^ d) for k in range(tensor)]) for d in (1, 2, 3)]
-    projected = call(value_kernel, partial, [*halves[1], value_weight, value], 6 * MIB, flops=work)
-    return call(join_kernel, shape(hidden.shape, bf16), [sums, *others, hidden, projected], 6 * MIB)
+    sums_there = lax.ppermute(sums, "tensor", [(k, k ^ 1) for k in range(tensor)])
+    value = call(first_kernel, partial, [*halves[0], value_weight], 6 * MIB, flops=work)
+    value, sums_there = lax.optimization_barrier((value, sums_there))
+    sums = sums + sums_there
+    sums_there = lax.ppermute(sums, "tensor", [(k, k ^ 2) for k in range(tensor)])
+    value, sums = lax.optimization_barrier((value, sums))
+    projected = call(second_kernel, partial, [*halves[1], value_weight, value], 6 * MIB, flops=work)
+    chunks = 4
+    return pl.pallas_call(
+        lambda *refs: join_kernel(chunks, *refs),
+        out_shape=shape(hidden.shape, bf16),
+        in_specs=vmem(4),
+        out_specs=pl.BlockSpec(memory_space=pl.ANY),
+        scratch_shapes=[pltpu.VMEM(hidden.shape, bf16), pltpu.SemaphoreType.DMA((chunks,))],
+        compiler_params=pltpu.CompilerParams(vmem_limit_bytes=6 * MIB),
+    )(sums, sums_there, hidden, projected)
 
 
 def solution(mesh):

time: 56 us -> 53.3 us (0.952)
  blocking collectives: 41.8 us -> 39.9 us
  starting transfers between devices: 4.8 us -> 3.64 us
    all_to_all x1, blocking collectives: 20.9 us -> 19 us  [local(): lax.all_to_all(sent.reshape(devices // 2, 8, row_width), BOTH, 0, 0, axis...]
    ppermute x3 -> x2, starting transfers between devices: 2.22 us -> 1.03 us  [the longest x1 0.57 us: local(): lax.ppermute(sums, 'tensor', [(k, k ^ 2) for k in range(tensor)])]
    pallas_call x0 -> x1, Pallas kernels: none -> 0.98 us  [local(): pl.pallas_call(lambda *refs: join_kernel(chunks, *refs), out_shape=shape(...]
    pallas_call x8, Pallas kernels: 6.97 us -> 6.11 us  [call(): pl.pallas_call(body, out_shape=out_shape, in_specs=[pl.BlockSpec(memory_s...]
  transfers between devices with their start and end apart: 5 -> 4, of which waited for: 2 -> 2; matrix products, arithmetic and copies ran while one was open for 0% -> 0% of each run, Pallas kernels for 6% -> 7%
where the time goes in v3:
time: 53.3 us; the launch traced here: 53.2 us
  blocking collectives  39.9 us (75%)
  Pallas kernels  7.09 us (13%)
  starting transfers between devices  3.64 us (7%)
  waiting for transfers between devices  1.65 us (3%)
  local copies, waits for them, and re-layouts  0.72 us (1%)
    all_to_all x1, blocking collectives, local(): lax.all_to_all(message.reshape(devices, 2, LANES), BOTH, 0, 0, tiled=True)  20.9 us
    all_to_all x1, blocking collectives, local(): lax.all_to_all(sent.reshape(devices // 2, 8, row_width), BOTH, 0, 0, axis...  19 us
    pallas_call x8, Pallas kernels, call(): pl.pallas_call(body, out_shape=out_shape, in_specs=[pl.BlockSpec(memory_s...  6.11 us
    ppermute x2, starting transfers between devices, local(): lax.ppermute(mine, 'tensor', [(k, k ^ 1) for k in range(tensor)])  2.61 us
  transfers between devices with their start and end apart: 4, of which 2 were waited for; matrix products, arithmetic and copies ran while one was open for 0% of the time, Pallas kernels for 7%

profile of v3, /device:TPU:1, one launch (start us, length us, event | category | flops | bytes accessed | tf_op | source)
XLA Modules:
  0.0 53.2 jit_solution(13567268964348700235)
XLA Ops:
  0.0 0.0 copy-start.2
  0.0 0.7 %copy-done.2 = s32[128,1]{0,1:T(1,128)S(1)} copy-done((s32[128,1]{0,1:T(1,128)S(1)}, s32[128,1]{0,1:T(1,128)}, u32[]{:S(2)}) %copy-start.2) | copy-done | bytes 536
  0.7 0.0 copy-start.1
  0.7 0.0 slice-start
  0.7 0.0 slice-start.1
  0.7 0.0 slice-start.4
  0.7 0.0 slice-start.5
  0.7 0.3 shard_map.73
  1.0 20.9 %all_to_all.10 = bf16[128,2,128]{2,1,0:T(2,128)(2,1)S(1)} all-to-all(bf16[128,2,128]{2,1,0:T(2,128)(2,1)S(1)} %bitcast.16), channel_id=1, replica_groups=mesh['dp'=32,'tensor'=4] {'dp','tensor'}, dimensions={0} | all-to-all | bytes 131072 | tf_op jit(solution)/shard_map/all_to_all | solution.py:171
  21.9 0.0 copy-done.1
  21.9 0.0 copy-start.3
  21.9 0.0 copy-start.4
  21.9 0.0 slice-start.2
  21.9 0.0 slice-start.3
  21.9 0.0 slice-start.6
  22.0 0.0 slice-start.7
  22.0 0.5 shard_map.74
  22.4 19.0 %all_to_all.11 = bf16[64,8,896]{2,1,0:T(8,128)(2,1)S(1)} all-to-all(bf16[64,8,896]{2,1,0:T(8,128)(2,1)S(1)} %bitcast.12), channel_id=1, replica_groups={{0,42,84,126,10,52,94,96,20,62,64,106,30,32,74,116,2,44,86,120,12,54,88..., dimensions={0} | all-to-all | bytes 1835008 | tf_op jit(solution)/shard_map/all_to_all | solution.py:175
  41.4 0.6 %shard_map.75.mine_ref.mine = bf16[128,1792]{1,0:T(8,128)(2,1)S(1)} custom-call(s32[1]{0:T(128)} %bitcast.refs_0_, bf16[256,128]{1,0:T(8,128)(2,1)S(1)} %bitcast.14, bf16[512,896]{1,0:T(8,128)(2,1)S(1)} %bitcast.10), custom_call_target="tpu_custom_call" | custom-call | tf_op jit(solution)/shard_map/pallas_call | solution.py:44
  42.0 2.5 %collective-permute-start = (bf16[128,1792]{1,0:T(8,128)(2,1)S(1)}, bf16[128,1792]{1,0:T(8,128)(2,1)S(1)}, u32[]{:S(2)}, u32[]{:S(2)}) collective-permute-start(bf16[128,1792]{1,0:T(8,128)(2,1)S(1)} %shard_map.75.mine_ref.mine), channel_id=1, source_target_pairs={{0,1},{1,0},{2,3},{3,2},{4,5},{5,4},{6,7},{7,6},{8,9},{9,8},{10,11... | collective-permute-start | bytes 1376264 | tf_op jit(solution)/shard_map/ppermute | solution.py:187
  44.5 0.6 %shard_map.77.mine_ref = bf16[128,1792]{1,0:T(8,128)(2,1)S(1)} custom-call(s32[1]{0:T(128)} %bitcast.refs_0_, bf16[256,128]{1,0:T(8,128)(2,1)S(1)} %bitcast.15, bf16[512,896]{1,0:T(8,128)(2,1)S(1)} %bitcast.11), custom_call_target="tpu_custom_call" | custom-call | tf_op jit(solution)/shard_map/pallas_call | solution.py:44
  45.1 0.1 collective-permute-start.1
  45.2 0.0 copy-done.3
  45.2 0.0 copy-done.4
  45.2 0.0 copy-start
  45.2 0.7 %collective-permute-done.other_ref.other = bf16[128,1792]{1,0:T(8,128)(2,1)S(1)} collective-permute-done((bf16[128,1792]{1,0:T(8,128)(2,1)S(1)}, bf16[128,1792]{1,0:T(8,128)(2,1)S(1)}, u32[]{:S(2)}, u32[]{:S(2)}) %collective-permute-start) | collective-permute-done | bytes 458784 | tf_op jit(solution)/shard_map/ppermute | solution.py:187
  45.9 0.0 slice-done
  45.9 0.0 slice-done.1
  45.9 0.0 slice-done.4
  45.9 0.0 slice-done.5
  45.9 0.0 slice-done.2
  45.9 0.0 slice-done.3
  46.0 0.0 slice-done.6
  46.0 0.0 slice-done.7
  46.0 1.0 %shard_map.78.first_ref = f32[128,1792]{1,0:T(8,128)S(1)} custom-call(bf16[128,1792]{1,0:T(8,128)(2,1)S(1)} %shard_map.75.mine_ref.mine, bf16[128,1792]{1,0:T(8,128)(2,1)S(1)} %collective-permute-done.other_ref.other, bf16[3584,1792]{1,0:T(8,128)(2,1)S(1)} %bitcast.9, bf16[3584,1792]{1,0:T(8,128)(2,1)S(1)} %bitcast.7), custom_call_target="tpu_custom_call" | custom-call | flops 822083584 | tf_op jit(solution)/shard_map/pallas_call | solution.py:44
  47.0 0.0 collective-permute-done.1.other_ref
  47.0 0.0 copy-done
  47.0 1.1 %shard_map.79 = f32[8,128]{1,0:T(8,128)S(1)} custom-call(bf16[128,1792]{1,0:T(8,128)(2,1)S(1)} %shard_map.77.mine_ref, bf16[128,1792]{1,0:T(8,128)(2,1)S(1)} %collective-permute-done.1.other_ref, bf16[3584,1792]{1,0:T(8,128)(2,1)S(1)} %bitcast.9, f32[128,1792]{1,0:T(8,128)S(1)} %shard_map.78.first_ref, bf16[128,1792]{1,0:T(8,128)(2,1)S(1)} %copy-done, ...), custom_call_target="tpu_custom_call" | custom-call | flops 822083584 | tf_op jit(solution)/shard_map/pallas_call | solution.py:44
  48.2 0.5 collective-permute-start.2
  48.7 1.0 %shard_map.76.first_ref = f32[128,1792]{1,0:T(8,128)S(1)} custom-call(bf16[128,1792]{1,0:T(8,128)(2,1)S(1)} %shard_map.75.mine_ref.mine, bf16[128,1792]{1,0:T(8,128)(2,1)S(1)} %collective-permute-done.other_ref.other, bf16[3584,1792]{1,0:T(8,128)(2,1)S(1)} %bitcast.7), custom_call_target="tpu_custom_call" | custom-call | flops 822083584 | tf_op jit(solution)/shard_map/pallas_call | solution.py:44
  49.7 0.0 collective-permute-done.2
  49.7 0.6 %collective-permute-start.3 = (f32[8,128]{1,0:T(8,128)S(1)}, f32[8,128]{1,0:T(8,128)S(1)}, u32[]{:S(2)}, u32[]{:S(2)}) collective-permute-start(f32[8,128]{1,0:T(8,128)S(1)} %add.7.refs_0_), channel_id=1, source_target_pairs={{0,2},{1,3},{2,0},{3,1},{4,6},{5,7},{6,4},{7,5},{8,10},{9,11},{10,... | collective-permute-start | bytes 12296 | tf_op jit(solution)/shard_map/ppermute | solution.py:211
  50.3 1.0 %shard_map.80.refs_3_ = f32[128,1792]{1,0:T(8,128)S(1)} custom-call(bf16[128,1792]{1,0:T(8,128)(2,1)S(1)} %shard_map.77.mine_ref, bf16[128,1792]{1,0:T(8,128)(2,1)S(1)} %collective-permute-done.1.other_ref, bf16[3584,1792]{1,0:T(8,128)(2,1)S(1)} %bitcast.7, f32[128,1792]{1,0:T(8,128)S(1)} %shard_map.76.first_ref), custom_call_target="tpu_custom_call" | custom-call | flops 822083584 | tf_op jit(solution)/shard_map/pallas_call | solution.py:44
  51.3 0.9 %collective-permute-done.3.refs_1_ = f32[8,128]{1,0:T(8,128)S(1)} collective-permute-done((f32[8,128]{1,0:T(8,128)S(1)}, f32[8,128]{1,0:T(8,128)S(1)}, u32[]{:S(2)}, u32[]{:S(2)}) %collective-permute-start.3) | collective-permute-done | bytes 4128 | tf_op jit(solution)/shard_map/ppermute | solution.py:211
  52.2 1.0 %shard_map.81 = bf16[128,1792]{1,0:T(8,128)(2,1)} custom-call(f32[8,128]{1,0:T(8,128)S(1)} %add.7.refs_0_, f32[8,128]{1,0:T(8,128)S(1)} %collective-permute-done.3.refs_1_, bf16[128,1792]{1,0:T(8,128)(2,1)S(1)} %copy-done, f32[128,1792]{1,0:T(8,128)S(1)} %shard_map.80.refs_3_), custom_call_target="tpu_custom_call" | custom-call | tf_op jit(solution)/shard_map/pallas_call | solution.py:215
  (5 shorter events, 0.0 us)
Async XLA Ops:
  0.0 0.7 %copy-start.2 = (s32[128,1]{0,1:T(1,128)S(1)}, s32[128,1]{0,1:T(1,128)}, u32[]{:S(2)}) copy-start(s32[128,1]{0,1:T(1,128)} %param.8) | copy-start | bytes 1540
  0.7 21.3 %copy-start.1 = (bf16[256,896]{1,0:T(8,128)(2,1)S(1)}, bf16[256,896]{1,0:T(8,128)(2,1)}, u32[]{:S(2)}) copy-start(bf16[256,896]{1,0:T(8,128)(2,1)} %table_ref.1) | copy-start | bytes 1376260
  0.7 45.3 %slice-start = ((s8[12845056]{0:T(1024)(128)(4,1)}), s8[4194304]{0:T(1024)(128)(4,1)S(1)}, s32[]{:S(2)}) async-start(s8[12845056]{0:T(1024)(128)(4,1)} %bitcast.6), calls=%async_computation.2 | async-start | bytes 8388608
  0.7 45.3 %slice-start.1 = ((s8[12845056]{0:T(1024)(128)(4,1)}), s8[4194304]{0:T(1024)(128)(4,1)S(1)}, s32[]{:S(2)}) async-start(s8[12845056]{0:T(1024)(128)(4,1)} %bitcast.6), calls=%async_computation.3 | async-start | bytes 8388608
  0.7 45.3 %slice-start.4 = ((s8[12845056]{0:T(1024)(128)(4,1)}), s8[4194304]{0:T(1024)(128)(4,1)S(1)}, s32[]{:S(2)}) async-start(s8[12845056]{0:T(1024)(128)(4,1)} %bitcast.8), calls=%async_computation.6 | async-start | bytes 8388608
  0.7 45.3 %slice-start.5 = ((s8[12845056]{0:T(1024)(128)(4,1)}), s8[4194304]{0:T(1024)(128)(4,1)S(1)}, s32[]{:S(2)}) async-start(s8[12845056]{0:T(1024)(128)(4,1)} %bitcast.8), calls=%async_computation.7 | async-start | bytes 8388608
  21.9 23.2 %copy-start.3 = (f32[1792]{0:T(1024)S(1)}, f32[1792]{0:T(1024)}, u32[]{:S(2)}) copy-start(f32[1792]{0:T(1024)} %param.12) | copy-start | bytes 21508
  21.9 23.3 %copy-start.4 = (f32[1792]{0:T(1024)S(1)}, f32[1792]{0:T(1024)}, u32[]{:S(2)}) copy-start(f32[1792]{0:T(1024)} %param.13) | copy-start | bytes 21508
  21.9 24.0 %slice-start.2 = ((s8[12845056]{0:T(1024)(128)(4,1)}), s8[4194304]{0:T(1024)(128)(4,1)S(1)}, s32[]{:S(2)}) async-start(s8[12845056]{0:T(1024)(128)(4,1)} %bitcast.6), calls=%async_computation.4 | async-start | bytes 8388608
  21.9 24.0 %slice-start.3 = ((s8[12845056]{0:T(1024)(128)(4,1)}), s8[262144]{0:T(1024)(128)(4,1)S(1)}, s32[]{:S(2)}) async-start(s8[12845056]{0:T(1024)(128)(4,1)} %bitcast.6), calls=%async_computation.5 | async-start | bytes 524288
  21.9 24.0 %slice-start.6 = ((s8[12845056]{0:T(1024)(128)(4,1)}), s8[4194304]{0:T(1024)(128)(4,1)S(1)}, s32[]{:S(2)}) async-start(s8[12845056]{0:T(1024)(128)(4,1)} %bitcast.8), calls=%async_computation.8 | async-start | bytes 8388608
  22.0 24.0 %slice-start.7 = ((s8[12845056]{0:T(1024)(128)(4,1)}), s8[262144]{0:T(1024)(128)(4,1)S(1)}, s32[]{:S(2)}) async-start(s8[12845056]{0:T(1024)(128)(4,1)} %bitcast.8), calls=%async_computation.9 | async-start | bytes 524288
  42.0 4.0 %collective-permute-start = (bf16[128,1792]{1,0:T(8,128)(2,1)S(1)}, bf16[128,1792]{1,0:T(8,128)(2,1)S(1)}, u32[]{:S(2)}, u32[]{:S(2)}) collective-permute-start(bf16[128,1792]{1,0:T(8,128)(2,1)S(1)} %shard_map.75.mine_ref.mine), channel_id=1, source_target_pairs={{0,1},{1,0},{2,3},{3,2},{4,5},{5,4},{6,7},{7,6},{8,9},{9,8},{10,11... | collective-permute-start | bytes 1376264 | tf_op jit(solution)/shard_map/ppermute | solution.py:187
  45.1 2.0 %collective-permute-start.1 = (bf16[128,1792]{1,0:T(8,128)(2,1)S(1)}, bf16[128,1792]{1,0:T(8,128)(2,1)S(1)}, u32[]{:S(2)}, u32[]{:S(2)}) collective-permute-start(bf16[128,1792]{1,0:T(8,128)(2,1)S(1)} %shard_map.77.mine_ref), channel_id=1, source_target_pairs={{0,1},{1,0},{2,3},{3,2},{4,5},{5,4},{6,7},{7,6},{8,9},{9,8},{10,11... | collective-permute-start | bytes 1376264 | tf_op jit(solution)/shard_map/ppermute | solution.py:187
  45.2 1.8 %copy-start = (bf16[128,1792]{1,0:T(8,128)(2,1)S(1)}, bf16[128,1792]{1,0:T(8,128)(2,1)}, u32[]{:S(2)}) copy-start(bf16[128,1792]{1,0:T(8,128)(2,1)} %refs_2_.1) | copy-start | bytes 1376260
  48.2 1.5 %collective-permute-start.2 = (f32[8,128]{1,0:T(8,128)S(1)}, f32[8,128]{1,0:T(8,128)S(1)}, u32[]{:S(2)}, u32[]{:S(2)}) collective-permute-start(f32[8,128]{1,0:T(8,128)S(1)} %shard_map.79), channel_id=1, source_target_pairs={{0,1},{1,0},{2,3},{3,2},{4,5},{5,4},{6,7},{7,6},{8,9},{9,8},{10,11... | collective-permute-start | bytes 12296 | tf_op jit(solution)/shard_map/ppermute | solution.py:207
  49.7 2.5 %collective-permute-start.3 = (f32[8,128]{1,0:T(8,128)S(1)}, f32[8,128]{1,0:T(8,128)S(1)}, u32[]{:S(2)}, u32[]{:S(2)}) collective-permute-start(f32[8,128]{1,0:T(8,128)S(1)} %add.7.refs_0_), channel_id=1, source_target_pairs={{0,2},{1,3},{2,0},{3,1},{4,6},{5,7},{6,4},{7,5},{8,10},{9,11},{10,... | collective-permute-start | bytes 12296 | tf_op jit(solution)/shard_map/ppermute | solution.py:211

commit v4 on v3

--- a/solution.py
+++ b/solution.py
@@ -94,12 +94,14 @@
     arrived = arrived_ref[...]
     slots = arrived.shape[0]
     width = arrived.shape[1]
-    for k, head in enumerate(heads):
+    chosen = []
+    for head in heads:
         column = jnp.broadcast_to(target[2 * head : 2 * head + 1, :], (LANES, LANES)).T
         column = column[:, 0:1].astype(jnp.int32) + 2 * head
-        chosen = (column == iota((LANES, slots), 1)).astype(f32).astype(bf16)
-        found = jnp.dot(chosen, arrived, preferred_element_type=f32)
-        out_ref[:, k * width : (k + 1) * width] = found.astype(bf16)
+        chosen.append((column == iota((LANES, slots), 1)).astype(f32).astype(bf16))
+    found = jnp.dot(jnp.concatenate(chosen, axis=0), arrived, preferred_element_type=f32).astype(bf16)
+    for k in range(len(heads)):
+        out_ref[:, k * width : (k + 1) * width] = found[k * LANES : (k + 1) * LANES]
 
 
 def row_of_sums(terms):
@@ -114,10 +116,9 @@
     out_ref[...] = jnp.dot(memory, weight_ref[: memory.shape[1], :], preferred_element_type=f32)
 
 
-def second_kernel(mine_ref, other_ref, weight_ref, first_ref, out_ref):
-    memory = mine_ref[...] + other_ref[...]
-    more = jnp.dot(memory, weight_ref[memory.shape[1] :, :], preferred_element_type=f32)
-    out_ref[...] = first_ref[...] + more
+def value_kernel(mine0_ref, other0_ref, mine1_ref, other1_ref, weight_ref, out_ref):
+    memory = jnp.concatenate([mine0_ref[...] + other0_ref[...], mine1_ref[...] + other1_ref[...]], axis=1)
+    out_ref[...] = jnp.dot(memory, weight_ref[...], preferred_element_type=f32)
 
 
 def key_kernel(mine_ref, other_ref, weight_ref, first_ref, hidden_ref, hgain_ref, kgain_ref, sums_ref):
@@ -132,8 +133,8 @@
     sums_ref[...] = jnp.concatenate(sums + [jnp.zeros((5, LANES), f32)], axis=0)
 
 
-def join_kernel(chunks, here_ref, there_ref, hidden_ref, projected_ref, out_ref, joined_ref, sems):
-    sums = here_ref[...] + there_ref[...]
+def join_kernel(chunks, s0_ref, s1_ref, s2_ref, s3_ref, hidden_ref, projected_ref, out_ref, joined_ref, sems):
+    sums = (s0_ref[...] + s1_ref[...]) + (s2_ref[...] + s3_ref[...])
     hidden_power = sums[0:1] / D
     key_power = sums[1:2] / D
     agreement = sums[2:3] * lax.rsqrt(hidden_power + EPSILON) * lax.rsqrt(key_power + EPSILON)
@@ -204,22 +205,17 @@
         6 * MIB,
         flops=work,
     )
-    sums_there = lax.ppermute(sums, "tensor", [(k, k ^ 1) for k in range(tensor)])
-    value = call(first_kernel, partial, [*halves[0], value_weight], 6 * MIB, flops=work)
-    value, sums_there = lax.optimization_barrier((value, sums_there))
-    sums = sums + sums_there
-    sums_there = lax.ppermute(sums, "tensor", [(k, k ^ 2) for k in range(tensor)])
-    value, sums = lax.optimization_barrier((value, sums))
-    projected = call(second_kernel, partial, [*halves[1], value_weight, value], 6 * MIB, flops=work)
+    others = [lax.ppermute(sums, "tensor", [(k, k ^ d) for k in range(tensor)]) for d in (3, 2, 1)]
+    projected = call(value_kernel, partial, [*halves[0], *halves[1], value_weight], 6 * MIB, flops=2 * work)
     chunks = 4
     return pl.pallas_call(
         lambda *refs: join_kernel(chunks, *refs),
         out_shape=shape(hidden.shape, bf16),
-        in_specs=vmem(4),
+        in_specs=vmem(6),
         out_specs=pl.BlockSpec(memory_space=pl.ANY),
         scratch_shapes=[pltpu.VMEM(hidden.shape, bf16), pltpu.SemaphoreType.DMA((chunks,))],
         compiler_params=pltpu.CompilerParams(vmem_limit_bytes=6 * MIB),
-    )(sums, sums_there, hidden, projected)
+    )(sums, *others, hidden, projected)
 
 
 def solution(mesh):

time: 53.3 us -> 53.5 us (level)
  starting transfers between devices: 3.64 us -> 4.83 us
  waiting for transfers between devices: 1.65 us -> 0.65 us
    ppermute x2 -> x3, starting transfers between devices: 1.03 us -> 2.22 us  [local(): lax.ppermute(sums, 'tensor', [(k, k ^ d) for k in range(tensor)])]
    ppermute x2 -> x3, waiting for transfers between devices: 0.94 us -> 0.01 us  [local(): lax.ppermute(sums, 'tensor', [(k, k ^ d) for k in range(tensor)])]
    pallas_call x8 -> x7, Pallas kernels: 6.11 us -> 6.06 us  [call(): pl.pallas_call(body, out_shape=out_shape, in_specs=[pl.BlockSpec(memory_s...]
  transfers between devices with their start and end apart: 4 -> 5, of which waited for: 2 -> 1; matrix products, arithmetic and copies ran while one was open for 0% -> 0% of each run, Pallas kernels for 7% -> 7%
where the time goes in v4:
time: 53.5 us; the launch traced here: 53.4 us
  blocking collectives  39.9 us (75%)
  Pallas kernels  7.05 us (13%)
  starting transfers between devices  4.83 us (9%)
  local copies, waits for them, and re-layouts  0.72 us (1%)
  waiting for transfers between devices  0.65 us (1%)
    all_to_all x1, blocking collectives, local(): lax.all_to_all(message.reshape(devices, 2, LANES), BOTH, 0, 0, tiled=True)  20.9 us
    all_to_all x1, blocking collectives, local(): lax.all_to_all(sent.reshape(devices // 2, 8, row_width), BOTH, 0, 0, axis...  19 us
    pallas_call x7, Pallas kernels, call(): pl.pallas_call(body, out_shape=out_shape, in_specs=[pl.BlockSpec(memory_s...  6.06 us
    ppermute x2, starting transfers between devices, local(): lax.ppermute(mine, 'tensor', [(k, k ^ 1) for k in range(tensor)])  2.61 us
    ppermute x3, starting transfers between devices, local(): lax.ppermute(sums, 'tensor', [(k, k ^ d) for k in range(tensor)])  2.22 us
  transfers between devices with their start and end apart: 5, of which 1 were waited for; matrix products, arithmetic and copies ran while one was open for 0% of the time, Pallas kernels for 7%

profile of v4, /device:TPU:1, one launch (start us, length us, event | category | flops | bytes accessed | tf_op | source)
XLA Modules:
  0.0 53.4 jit_solution(4970627925997509609)
XLA Ops:
  0.0 0.0 copy-start.2
  0.0 0.7 %copy-done.2 = s32[128,1]{0,1:T(1,128)S(1)} copy-done((s32[128,1]{0,1:T(1,128)S(1)}, s32[128,1]{0,1:T(1,128)}, u32[]{:S(2)}) %copy-start.2) | copy-done | bytes 536
  0.7 0.0 copy-start.1
  0.7 0.0 slice-start
  0.7 0.0 slice-start.1
  0.7 0.0 slice-start.4
  0.7 0.0 slice-start.5
  0.7 0.3 shard_map.73
  1.0 20.9 %all_to_all.10 = bf16[128,2,128]{2,1,0:T(2,128)(2,1)S(1)} all-to-all(bf16[128,2,128]{2,1,0:T(2,128)(2,1)S(1)} %bitcast.16), channel_id=1, replica_groups=mesh['dp'=32,'tensor'=4] {'dp','tensor'}, dimensions={0} | all-to-all | bytes 131072 | tf_op jit(solution)/shard_map/all_to_all | solution.py:172
  21.9 0.0 copy-done.1
  21.9 0.0 copy-start.3
  21.9 0.0 copy-start.4
  21.9 0.0 slice-start.2
  21.9 0.0 slice-start.3
  21.9 0.0 slice-start.6
  22.0 0.0 slice-start.7
  22.0 0.5 shard_map.74
  22.4 19.0 %all_to_all.11 = bf16[64,8,896]{2,1,0:T(8,128)(2,1)S(1)} all-to-all(bf16[64,8,896]{2,1,0:T(8,128)(2,1)S(1)} %bitcast.12), channel_id=1, replica_groups={{0,42,84,126,10,52,94,96,20,62,64,106,30,32,74,116,2,44,86,120,12,54,88..., dimensions={0} | all-to-all | bytes 1835008 | tf_op jit(solution)/shard_map/all_to_all | solution.py:176
  41.4 0.6 %shard_map.76.mine.mine0_ref = bf16[128,1792]{1,0:T(8,128)(2,1)S(1)} custom-call(s32[1]{0:T(128)} %bitcast.refs_0_, bf16[256,128]{1,0:T(8,128)(2,1)S(1)} %bitcast.14, bf16[512,896]{1,0:T(8,128)(2,1)S(1)} %bitcast.10), custom_call_target="tpu_custom_call" | custom-call | tf_op jit(solution)/shard_map/pallas_call | solution.py:44
  42.0 2.5 %collective-permute-start.1 = (bf16[128,1792]{1,0:T(8,128)(2,1)S(1)}, bf16[128,1792]{1,0:T(8,128)(2,1)S(1)}, u32[]{:S(2)}, u32[]{:S(2)}) collective-permute-start(bf16[128,1792]{1,0:T(8,128)(2,1)S(1)} %shard_map.76.mine.mine0_ref), channel_id=1, source_target_pairs={{0,1},{1,0},{2,3},{3,2},{4,5},{5,4},{6,7},{7,6},{8,9},{9,8},{10,11... | collective-permute-start | bytes 1376264 | tf_op jit(solution)/shard_map/ppermute | solution.py:188
  44.6 0.6 %shard_map.75.mine_ref.mine1_ref = bf16[128,1792]{1,0:T(8,128)(2,1)S(1)} custom-call(s32[1]{0:T(128)} %bitcast.refs_0_, bf16[256,128]{1,0:T(8,128)(2,1)S(1)} %bitcast.15, bf16[512,896]{1,0:T(8,128)(2,1)S(1)} %bitcast.11), custom_call_target="tpu_custom_call" | custom-call | tf_op jit(solution)/shard_map/pallas_call | solution.py:44
  45.2 0.1 collective-permute-start
  45.3 0.0 copy-done.3
  45.3 0.0 copy-done.4
  45.4 0.0 copy-start
  45.4 0.6 %collective-permute-done.1.other.other0_ref = bf16[128,1792]{1,0:T(8,128)(2,1)S(1)} collective-permute-done((bf16[128,1792]{1,0:T(8,128)(2,1)S(1)}, bf16[128,1792]{1,0:T(8,128)(2,1)S(1)}, u32[]{:S(2)}, u32[]{:S(2)}) %collective-permute-start.1) | collective-permute-done | bytes 458784 | tf_op jit(solution)/shard_map/ppermute | solution.py:188
  46.0 0.0 slice-done
  46.0 0.0 slice-done.1
  46.0 0.0 slice-done.4
  46.0 0.0 slice-done.5
  46.0 0.0 slice-done.2
  46.0 0.0 slice-done.3
  46.0 0.0 slice-done.6
  46.0 0.0 slice-done.7
  46.1 1.0 %shard_map.77.first_ref = f32[128,1792]{1,0:T(8,128)S(1)} custom-call(bf16[128,1792]{1,0:T(8,128)(2,1)S(1)} %shard_map.76.mine.mine0_ref, bf16[128,1792]{1,0:T(8,128)(2,1)S(1)} %collective-permute-done.1.other.other0_ref, bf16[3584,1792]{1,0:T(8,128)(2,1)S(1)} %bitcast.7, bf16[3584,1792]{1,0:T(8,128)(2,1)S(1)} %bitcast.9), custom_call_target="tpu_custom_call" | custom-call | flops 822083584 | tf_op jit(solution)/shard_map/pallas_call | solution.py:44
  47.1 0.0 collective-permute-done.other_ref.other1_ref
  47.1 0.0 copy-done
  47.1 1.1 %shard_map.78.refs_0_ = f32[8,128]{1,0:T(8,128)S(1)} custom-call(bf16[128,1792]{1,0:T(8,128)(2,1)S(1)} %shard_map.75.mine_ref.mine1_ref, bf16[128,1792]{1,0:T(8,128)(2,1)S(1)} %collective-permute-done.other_ref.other1_ref, bf16[3584,1792]{1,0:T(8,128)(2,1)S(1)} %bitcast.7, f32[128,1792]{1,0:T(8,128)S(1)} %shard_map.77.first_ref, ...), custom_call_target="tpu_custom_call" | custom-call | flops 822083584 | tf_op jit(solution)/shard_map/pallas_call | solution.py:44
  48.3 0.8 %collective-permute-start.2 = (f32[8,128]{1,0:T(8,128)S(1)}, f32[8,128]{1,0:T(8,128)S(1)}, u32[]{:S(2)}, u32[]{:S(2)}) collective-permute-start(f32[8,128]{1,0:T(8,128)S(1)} %shard_map.78.refs_0_), channel_id=1, source_target_pairs={{0,3},{1,2},{2,1},{3,0},{4,7},{5,6},{6,5},{7,4},{8,11},{9,10},{10,... | collective-permute-start | bytes 12296 | tf_op jit(solution)/shard_map/ppermute | solution.py:208
  49.1 1.0 %collective-permute-start.3 = (f32[8,128]{1,0:T(8,128)S(1)}, f32[8,128]{1,0:T(8,128)S(1)}, u32[]{:S(2)}, u32[]{:S(2)}) collective-permute-start(f32[8,128]{1,0:T(8,128)S(1)} %shard_map.78.refs_0_), channel_id=1, source_target_pairs={{0,2},{1,3},{2,0},{3,1},{4,6},{5,7},{6,4},{7,5},{8,10},{9,11},{10,... | collective-permute-start | bytes 12296 | tf_op jit(solution)/shard_map/ppermute | solution.py:208
  50.1 0.4 collective-permute-start.4
  50.5 1.8 %shard_map.79.refs_5_ = f32[128,1792]{1,0:T(8,128)S(1)} custom-call(bf16[128,1792]{1,0:T(8,128)(2,1)S(1)} %shard_map.76.mine.mine0_ref, bf16[128,1792]{1,0:T(8,128)(2,1)S(1)} %collective-permute-done.1.other.other0_ref, bf16[128,1792]{1,0:T(8,128)(2,1)S(1)} %shard_map.75.mine_ref.mine1_ref, bf16[128,1792]{1,0:T(8,128)(2,1)S(1)} %collective-permute-done.other_ref.other1_ref, ...), custom_call_target="tpu_custom_call" | custom-call | flops 1644167168 | tf_op jit(solution)/shard_map/pallas_call | solution.py:44
  52.3 0.0 collective-permute-done.2.refs_1_
  52.4 0.0 collective-permute-done.3.refs_2_
  52.4 0.0 collective-permute-done.4.refs_3_
  52.4 1.0 %shard_map.80 = bf16[128,1792]{1,0:T(8,128)(2,1)} custom-call(f32[8,128]{1,0:T(8,128)S(1)} %shard_map.78.refs_0_, f32[8,128]{1,0:T(8,128)S(1)} %collective-permute-done.2.refs_1_, f32[8,128]{1,0:T(8,128)S(1)} %collective-permute-done.3.refs_2_, f32[8,128]{1,0:T(8,128)S(1)} %collective-permute-done.4.refs_3_, bf16[128,1792]{1,0:T(8,128)(2,1)S(1)} %copy-done, ...), custom_call_target="tpu_custom_call" | custom-call | tf_op jit(solution)/shard_map/pallas_call | solution.py:211
  (4 shorter events, 0.0 us)
Async XLA Ops:
  0.0 0.7 %copy-start.2 = (s32[128,1]{0,1:T(1,128)S(1)}, s32[128,1]{0,1:T(1,128)}, u32[]{:S(2)}) copy-start(s32[128,1]{0,1:T(1,128)} %param.8) | copy-start | bytes 1540
  0.7 21.3 %copy-start.1 = (bf16[256,896]{1,0:T(8,128)(2,1)S(1)}, bf16[256,896]{1,0:T(8,128)(2,1)}, u32[]{:S(2)}) copy-start(bf16[256,896]{1,0:T(8,128)(2,1)} %table_ref.1) | copy-start | bytes 1376260
  0.7 45.3 %slice-start = ((s8[12845056]{0:T(1024)(128)(4,1)}), s8[4194304]{0:T(1024)(128)(4,1)S(1)}, s32[]{:S(2)}) async-start(s8[12845056]{0:T(1024)(128)(4,1)} %bitcast.6), calls=%async_computation.2 | async-start | bytes 8388608
  0.7 45.3 %slice-start.1 = ((s8[12845056]{0:T(1024)(128)(4,1)}), s8[4194304]{0:T(1024)(128)(4,1)S(1)}, s32[]{:S(2)}) async-start(s8[12845056]{0:T(1024)(128)(4,1)} %bitcast.6), calls=%async_computation.3 | async-start | bytes 8388608
  0.7 45.3 %slice-start.4 = ((s8[12845056]{0:T(1024)(128)(4,1)}), s8[4194304]{0:T(1024)(128)(4,1)S(1)}, s32[]{:S(2)}) async-start(s8[12845056]{0:T(1024)(128)(4,1)} %bitcast.8), calls=%async_computation.6 | async-start | bytes 8388608
  0.7 45.3 %slice-start.5 = ((s8[12845056]{0:T(1024)(128)(4,1)}), s8[4194304]{0:T(1024)(128)(4,1)S(1)}, s32[]{:S(2)}) async-start(s8[12845056]{0:T(1024)(128)(4,1)} %bitcast.8), calls=%async_computation.7 | async-start | bytes 8388608
  21.9 23.4 %copy-start.3 = (f32[1792]{0:T(1024)S(1)}, f32[1792]{0:T(1024)}, u32[]{:S(2)}) copy-start(f32[1792]{0:T(1024)} %param.12) | copy-start | bytes 21508
  21.9 23.4 %copy-start.4 = (f32[1792]{0:T(1024)S(1)}, f32[1792]{0:T(1024)}, u32[]{:S(2)}) copy-start(f32[1792]{0:T(1024)} %param.13) | copy-start | bytes 21508
  21.9 24.1 %slice-start.2 = ((s8[12845056]{0:T(1024)(128)(4,1)}), s8[4194304]{0:T(1024)(128)(4,1)S(1)}, s32[]{:S(2)}) async-start(s8[12845056]{0:T(1024)(128)(4,1)} %bitcast.6), calls=%async_computation.4 | async-start | bytes 8388608
  21.9 24.1 %slice-start.3 = ((s8[12845056]{0:T(1024)(128)(4,1)}), s8[262144]{0:T(1024)(128)(4,1)S(1)}, s32[]{:S(2)}) async-start(s8[12845056]{0:T(1024)(128)(4,1)} %bitcast.6), calls=%async_computation.5 | async-start | bytes 524288
  21.9 24.1 %slice-start.6 = ((s8[12845056]{0:T(1024)(128)(4,1)}), s8[4194304]{0:T(1024)(128)(4,1)S(1)}, s32[]{:S(2)}) async-start(s8[12845056]{0:T(1024)(128)(4,1)} %bitcast.8), calls=%async_computation.8 | async-start | bytes 8388608
  22.0 24.1 %slice-start.7 = ((s8[12845056]{0:T(1024)(128)(4,1)}), s8[262144]{0:T(1024)(128)(4,1)S(1)}, s32[]{:S(2)}) async-start(s8[12845056]{0:T(1024)(128)(4,1)} %bitcast.8), calls=%async_computation.9 | async-start | bytes 524288
  42.0 4.0 %collective-permute-start.1 = (bf16[128,1792]{1,0:T(8,128)(2,1)S(1)}, bf16[128,1792]{1,0:T(8,128)(2,1)S(1)}, u32[]{:S(2)}, u32[]{:S(2)}) collective-permute-start(bf16[128,1792]{1,0:T(8,128)(2,1)S(1)} %shard_map.76.mine.mine0_ref), channel_id=1, source_target_pairs={{0,1},{1,0},{2,3},{3,2},{4,5},{5,4},{6,7},{7,6},{8,9},{9,8},{10,11... | collective-permute-start | bytes 1376264 | tf_op jit(solution)/shard_map/ppermute | solution.py:188
  45.2 1.9 %collective-permute-start = (bf16[128,1792]{1,0:T(8,128)(2,1)S(1)}, bf16[128,1792]{1,0:T(8,128)(2,1)S(1)}, u32[]{:S(2)}, u32[]{:S(2)}) collective-permute-start(bf16[128,1792]{1,0:T(8,128)(2,1)S(1)} %shard_map.75.mine_ref.mine1_ref), channel_id=1, source_target_pairs={{0,1},{1,0},{2,3},{3,2},{4,5},{5,4},{6,7},{7,6},{8,9},{9,8},{10,11... | collective-permute-start | bytes 1376264 | tf_op jit(solution)/shard_map/ppermute | solution.py:188
  45.4 1.8 %copy-start = (bf16[128,1792]{1,0:T(8,128)(2,1)S(1)}, bf16[128,1792]{1,0:T(8,128)(2,1)}, u32[]{:S(2)}) copy-start(bf16[128,1792]{1,0:T(8,128)(2,1)} %refs_4_.1) | copy-start | bytes 1376260
  48.3 4.1 %collective-permute-start.2 = (f32[8,128]{1,0:T(8,128)S(1)}, f32[8,128]{1,0:T(8,128)S(1)}, u32[]{:S(2)}, u32[]{:S(2)}) collective-permute-start(f32[8,128]{1,0:T(8,128)S(1)} %shard_map.78.refs_0_), channel_id=1, source_target_pairs={{0,3},{1,2},{2,1},{3,0},{4,7},{5,6},{6,5},{7,4},{8,11},{9,10},{10,... | collective-permute-start | bytes 12296 | tf_op jit(solution)/shard_map/ppermute | solution.py:208
  49.1 3.3 %collective-permute-start.3 = (f32[8,128]{1,0:T(8,128)S(1)}, f32[8,128]{1,0:T(8,128)S(1)}, u32[]{:S(2)}, u32[]{:S(2)}) collective-permute-start(f32[8,128]{1,0:T(8,128)S(1)} %shard_map.78.refs_0_), channel_id=1, source_target_pairs={{0,2},{1,3},{2,0},{3,1},{4,6},{5,7},{6,4},{7,5},{8,10},{9,11},{10,... | collective-permute-start | bytes 12296 | tf_op jit(solution)/shard_map/ppermute | solution.py:208
  50.1 2.3 %collective-permute-start.4 = (f32[8,128]{1,0:T(8,128)S(1)}, f32[8,128]{1,0:T(8,128)S(1)}, u32[]{:S(2)}, u32[]{:S(2)}) collective-permute-start(f32[8,128]{1,0:T(8,128)S(1)} %shard_map.78.refs_0_), channel_id=1, source_target_pairs={{0,1},{1,0},{2,3},{3,2},{4,5},{5,4},{6,7},{7,6},{8,9},{9,8},{10,11... | collective-permute-start | bytes 12296 | tf_op jit(solution)/shard_map/ppermute | solution.py:208

commit v5 on v4

v5 whole, which is shorter than its diff:
```python
import math

import jax
import jax.numpy as jnp
from jax import lax
from jax.experimental import pallas as pl
from jax.experimental.pallas import tpu as pltpu
from jax.sharding import PartitionSpec as P

D = 7168
LANES = 128
EPSILON = 1e-06
COVER = 20_000_000_000
BOTH = ("dp", "tensor")
MIB = 1024 * 1024

f32 = jnp.float32
bf16 = jnp.bfloat16


def chip_order():
    order = []
    for k in range(64):
        a, b, c = k % 4, (k // 4) % 4, k // 16
        order.append(a * 16 + (a + b) % 4 * 4 + (a + b + c) % 4)
    return order


def turn_of(chip):
    z, y, x = chip >> 4, (chip >> 2) & 3, chip & 3
    return z + ((y - z) & 3) * 4 + ((x - y) & 3) * 16


def iota(shape, dim):
    return lax.broadcasted_iota(jnp.int32, shape, dim)


def vmem(count):
    return [pl.BlockSpec(memory_space=pltpu.VMEM)] * count


def call(body, out_shape, inputs, limit, scalars=(), scratch=(), flops=0):
    many = isinstance(out_shape, (tuple, list))
    return pl.pallas_call(
        body,
        out_shape=out_shape,
        in_specs=[pl.BlockSpec(memory_space=pltpu.SMEM)] * len(scalars) + vmem(len(inputs)),
        out_specs=tuple(vmem(len(out_shape))) if many else vmem(1)[0],
        scratch_shapes=list(scratch),
        compiler_params=pltpu.CompilerParams(vmem_limit_bytes=limit),
        cost_estimate=pl.CostEstimate(flops=flops, transcendentals=0, bytes_accessed=0) if flops else None,
    )(*scalars, *inputs)


def request_kernel(rows_held, hash_ref, out_ref):
    row = hash_ref[...]
    owner = row // rows_held
    local = (row - owner * rows_held).astype(f32)
    owner_rows = jnp.broadcast_to(owner.astype(f32), (LANES, LANES))
    owner_cols = owner_rows.T
    earlier = (owner_rows == owner_cols) & (iota((LANES, LANES), 0) < iota((LANES, LANES), 1))
    slot = jnp.sum(earlier.astype(f32), axis=0, keepdims=True)
    position = owner * 2 + slot.astype(jnp.int32)
    rows = out_ref.shape[0]
    asks = jnp.where(position == iota((rows, LANES), 0), local, jnp.zeros((rows, LANES), f32))
    asks = jnp.sum(asks, axis=1, keepdims=True)
    where = position.astype(f32)
    turned = pltpu.roll(where, LANES // 2, 1)
    first = (iota((rows, LANES), 0) & 3) == 0
    message = jnp.where(iota((rows, LANES), 1) < LANES // 2, asks, jnp.where(first, turned, where))
    out_ref[...] = message.astype(bf16)


def gather_kernel(here_ref, asked_ref, mine_ref, other_ref, out_ref):
    core = here_ref[0] & 1
    index = asked_ref[...].astype(jnp.int32)[:, 0:1]
    rows = index.shape[0]
    held = mine_ref.shape[0]
    is_mine = ((iota((rows, 1), 0) >> 1) & 1) == core
    lanes = iota((rows, held), 1)
    from_mine = (jnp.where(is_mine, index, -1) == lanes).astype(f32).astype(bf16)
    from_other = (jnp.where(is_mine, -1, index) == lanes).astype(f32).astype(bf16)
    found = jnp.dot(from_mine, mine_ref[...], preferred_element_type=f32)
    found = found + jnp.dot(from_other, other_ref[...], preferred_element_type=f32)
    turns = [found[chip // 2 * 8 : chip // 2 * 8 + 8] for chip in chip_order()]
    out_ref[...] = jnp.concatenate(turns, axis=0).astype(bf16)


def place_kernel(here_ref, asked_ref, arrived_ref, out_ref):
    start = pl.multiple_of((here_ref[0] >> 2) * 8, 8)
    asked = asked_ref[pl.ds(start, 8), :].astype(f32)
    arrived = arrived_ref[...]
    slots = arrived.shape[0]
    width = arrived.shape[1]
    low = iota((1, LANES), 1) < LANES // 2
    turned = pltpu.roll(asked, LANES // 2, 1)
    for x in range(2):
        position = jnp.where(low, turned[4 * x : 4 * x + 1], asked[4 * x + 1 : 4 * x + 2]).astype(jnp.int32)
        target = turn_of(position >> 2) * 8 + x * 4 + (position & 3)
        column = jnp.broadcast_to(target.astype(f32), (LANES, LANES)).T[:, 0:1].astype(jnp.int32)
        chosen = (column == iota((LANES, slots), 1)).astype(f32).astype(bf16)
        found = jnp.dot(chosen, arrived, preferred_element_type=f32)
        out_ref[:, x * width : (x + 1) * width] = found.astype(bf16)


def row_of_sums(terms):
    parts = terms[:, 0:LANES]
    for k in range(1, terms.shape[1] // LANES):
        parts = parts + terms[:, k * LANES : (k + 1) * LANES]
    return jnp.sum(parts.T, axis=0, keepdims=True)


def rows_of_heads(weight_ref, core):
    width = weight_ref.shape[0] // 4
    starts = [pl.multiple_of((2 * x + core) * width, LANES) for x in range(2)]
    return jnp.concatenate([weight_ref[pl.ds(start, width), :] for start in starts], axis=0)


def own_key_kernel(here_ref, mine_ref, weight_ref, _, out_ref):
    out_ref[...] = jnp.dot(
        mine_ref[...], rows_of_heads(weight_ref, here_ref[0] & 1), preferred_element_type=f32
    )


def key_kernel(here_ref, other_ref, weight_ref, own_ref, hidden_ref, hgain_ref, kgain_ref, sums_ref):
    weight = rows_of_heads(weight_ref, 1 - (here_ref[0] & 1))
    key = own_ref[...] + jnp.dot(other_ref[...], weight, preferred_element_type=f32)
    hidden = hidden_ref[...].astype(f32)
    sums = [
        row_of_sums(hidden * hidden),
        row_of_sums(key * key),
        row_of_sums((hidden * hgain_ref[...]) * (key * kgain_ref[...])),
    ]
    sums_ref[...] = jnp.concatenate(sums + [jnp.zeros((5, LANES), f32)], axis=0)


def value_kernel(here_ref, mine_ref, other_ref, weight_ref, out_ref):
    core = here_ref[0] & 1
    projected = jnp.dot(mine_ref[...], rows_of_heads(weight_ref, core), preferred_element_type=f32)
    more = jnp.dot(other_ref[...], rows_of_heads(weight_ref, 1 - core), preferred_element_type=f32)
    out_ref[...] = projected + more


def join_kernel(chunks, s0_ref, s1_ref, s2_ref, s3_ref, hidden_ref, projected_ref, out_ref, joined_ref, sems):
    sums = (s0_ref[...] + s1_ref[...]) + (s2_ref[...] + s3_ref[...])
    hidden_power = sums[0:1] / D
    key_power = sums[1:2] / D
    agreement = sums[2:3] * lax.rsqrt(hidden_power + EPSILON) * lax.rsqrt(key_power + EPSILON)
    gate = jax.nn.sigmoid(agreement / math.sqrt(D))
    gate = jnp.broadcast_to(gate, (LANES, LANES)).T[:, 0:1]
    rows = LANES // chunks
    copies = []
    for k in range(chunks):
        part = slice(k * rows, (k + 1) * rows)
        joined = hidden_ref[part, :].astype(f32) + gate[part] * projected_ref[part, :]
        joined_ref[part, :] = joined.astype(bf16)
        copy = pltpu.make_async_copy(joined_ref.at[part, :], out_ref.at[part, :], sems.at[k])
        copy.start()
        copies.append(copy)
    for copy in copies:
        copy.wait()


def local(hidden, hash_rows, memory_table, key_weight, value_weight, hidden_gain, key_gain):
    groups = lax.axis_size("dp")
    tensor = lax.axis_size("tensor")
    devices = groups * tensor
    rows_held, row_width = memory_table.shape
    shape = jax.ShapeDtypeStruct

    here = lax.axis_index(BOTH).astype(jnp.int32).reshape(1)
    hash_rows, here, hidden_gain, key_gain = lax.optimization_barrier((hash_rows, here, hidden_gain, key_gain))
    table_there = lax.ppermute(memory_table, "tensor", [(k, k ^ 1) for k in range(tensor)])
    chips = devices // 2
    message = call(
        lambda *refs: request_kernel(rows_held, *refs),
        shape((4 * chips, LANES), bf16),
        [hash_rows.reshape(1, LANES)],
        4 * MIB,
        flops=COVER,
    )
    in_turn = [[2 * chip + core for chip in chip_order()] for core in range(2)]
    in_place = [[2 * chip + core for chip in range(chips)] for core in range(2)]
    asked = lax.all_to_all(
        message.reshape(chips, 4, LANES), BOTH, 0, 0, axis_index_groups=in_place, tiled=True
    ).reshape(4 * chips, LANES)
    sent = call(
        gather_kernel,
        shape((8 * chips, row_width), bf16),
        [asked, memory_table, table_there],
        6 * MIB,
        scalars=[here],
        flops=COVER,
    )
    arrived = lax.all_to_all(
        sent.reshape(chips, 8, row_width), BOTH, 0, 0, axis_index_groups=in_turn, tiled=True
    ).reshape(8 * chips, row_width)
    mine = call(place_kernel, shape((LANES, 2 * row_width), bf16), [asked, arrived], 6 * MIB, scalars=[here])
    other = lax.ppermute(mine, "tensor", [(k, k ^ 1) for k in range(tensor)])
    columns = key_weight.shape[1]
    work = 2 * LANES * 2 * row_width * columns
    key_weight = pltpu.with_memory_space_constraint(key_weight, pltpu.VMEM)
    value_weight = pltpu.with_memory_space_constraint(value_weight, pltpu.VMEM)
    partial = shape((LANES, columns), f32)
    key = call(
        own_key_kernel, partial, [mine, key_weight, value_weight], 6 * MIB, scalars=[here], flops=work
    )
    sums = call(
        key_kernel,
        shape((8, LANES), f32),
        [other, key_weight, key, hidden, hidden_gain.reshape(1, columns), key_gain.reshape(1, columns)],
        6 * MIB,
        scalars=[here],
        flops=work,
    )
    others = [lax.ppermute(sums, "tensor", [(k, k ^ d) for k in range(tensor)]) for d in (3, 2, 1)]
    projected = call(value_kernel, partial, [mine, other, value_weight], 6 * MIB, scalars=[here], flops=2 * work)
    chunks = 4
    return pl.pallas_call(
        lambda *refs: join_kernel(chunks, *refs),
        out_shape=shape(hidden.shape, bf16),
        in_specs=vmem(6),
        out_specs=pl.BlockSpec(memory_space=pl.ANY),
        scratch_shapes=[pltpu.VMEM(hidden.shape, bf16), pltpu.SemaphoreType.DMA((chunks,))],
        compiler_params=pltpu.CompilerParams(vmem_limit_bytes=6 * MIB),
    )(sums, *others, hidden, projected)


def solution(mesh):
    return jax.shard_map(
        local,
        mesh=mesh,
        in_specs=(
            P("dp", "tensor"),
            P("dp", "tensor"),
            P(("dp", "tensor"), None),
            P(None, "tensor"),
            P(None, "tensor"),
            P("tensor"),
            P("tensor"),
        ),
        out_specs=P("dp", "tensor"),
        check_vma=False,
    )
```

time: 53.5 us -> 53 us (level)
  starting transfers between devices: 4.83 us -> 6.24 us
  blocking collectives: 39.9 us -> 38.9 us
  Pallas kernels: 7.05 us -> 6.39 us
    ppermute x2, starting transfers between devices: 2.61 us -> 4.02 us  [the longest x1 2.64 us: local(): other = lax.ppermute(mine, 'tensor', [(k, k ^ 1) for k in range(tensor)])]
    all_to_all x2, blocking collectives: 39.9 us -> 38.9 us  [the longest x1 19.9 us: local(): lax.all_to_all(message.reshape(chips, 4, LANES), BOTH, 0, 0, axis_index_g...]
    pallas_call x7 -> x6, Pallas kernels: 6.06 us -> 5.41 us  [call(): pl.pallas_call(body, out_shape=out_shape, in_specs=[pl.BlockSpec(memory_s...]
  transfers between devices with their start and end apart: 5 -> 5, of which waited for: 1 -> 1; matrix products, arithmetic and copies ran while one was open for 0% -> 0% of each run, Pallas kernels for 7% -> 6%
where the time goes in v5:
time: 53 us; the launch traced here: 52.8 us
  blocking collectives  38.9 us (73%)
  Pallas kernels  6.39 us (12%)
  starting transfers between devices  6.24 us (12%)
  local copies, waits for them, and re-layouts  0.73 us (1%)
    all_to_all x1, blocking collectives, local(): lax.all_to_all(message.reshape(chips, 4, LANES), BOTH, 0, 0, axis_index_g...  19.9 us
    all_to_all x1, blocking collectives, local(): lax.all_to_all(sent.reshape(chips, 8, row_width), BOTH, 0, 0, axis_index_...  19.1 us
    pallas_call x6, Pallas kernels, call(): pl.pallas_call(body, out_shape=out_shape, in_specs=[pl.BlockSpec(memory_s...  5.41 us
    ppermute x1, starting transfers between devices, local(): other = lax.ppermute(mine, 'tensor', [(k, k ^ 1) for k in range(tensor)])  2.64 us
    ppermute x3, starting transfers between devices, local(): lax.ppermute(sums, 'tensor', [(k, k ^ d) for k in range(tensor)])  2.22 us
    ppermute x1, starting transfers between devices, local(): lax.ppermute(memory_table, 'tensor', [(k, k ^ 1) for k in range(tensor)])  1.38 us
  transfers between devices with their start and end apart: 5, of which 1 were waited for; matrix products, arithmetic and copies ran while one was open for 0% of the time, Pallas kernels for 6%

profile of v5, /device:TPU:1, one launch (start us, length us, event | category | flops | bytes accessed | tf_op | source)
XLA Modules:
  0.0 52.8 jit_solution(2437566007781170934)
XLA Ops:
  0.0 1.4 %collective-permute-start = (bf16[256,896]{1,0:T(8,128)(2,1)}, bf16[256,896]{1,0:T(8,128)(2,1)S(1)}, u32[]{:S(2)}, u32[]{:S(2)}) collective-permute-start(bf16[256,896]{1,0:T(8,128)(2,1)} %mine_ref.1), channel_id=1, source_target_pairs={{0,1},{1,0},{2,3},{3,2},{4,5},{5,4},{6,7},{7,6},{8,9},{9,8},{10,11... | collective-permute-start | bytes 1376264 | tf_op jit(solution)/shard_map/ppermute | solution.py:173
  1.4 0.0 copy-start.2
  1.4 0.7 %copy-done.2 = s32[128,1]{0,1:T(1,128)S(1)} copy-done((s32[128,1]{0,1:T(1,128)S(1)}, s32[128,1]{0,1:T(1,128)}, u32[]{:S(2)}) %copy-start.2) | copy-done | bytes 536
  2.0 0.0 copy-start.1
  2.0 0.0 slice-start
  2.0 0.0 slice-start.1
  2.0 0.0 slice-start.4
  2.0 0.0 slice-start.5
  2.1 0.3 shard_map.73
  2.4 19.9 %all_to_all.10 = bf16[64,4,128]{2,1,0:T(4,128)(2,1)S(1)} all-to-all(bf16[64,4,128]{2,1,0:T(4,128)(2,1)S(1)} %bitcast.14), channel_id=1, replica_groups={{0,2,4,6,8,10,12,14,16,18,20,22,24,26,28,30,32,34,36,38,40,42,44,46,48,..., dimensions={0} | all-to-all | bytes 131072 | tf_op jit(solution)/shard_map/all_to_all | solution.py:184
  22.2 0.0 collective-permute-done.other_ref
  22.2 0.0 copy-done.1
  22.2 0.0 copy-start.3
  22.2 0.0 copy-start.4
  22.3 0.0 slice-start.2
  22.3 0.0 slice-start.3
  22.3 0.0 slice-start.6
  22.3 0.0 slice-start.7
  22.3 0.5 shard_map.74
  22.8 19.1 %all_to_all.11 = bf16[64,8,896]{2,1,0:T(8,128)(2,1)S(1)} all-to-all(bf16[64,8,896]{2,1,0:T(8,128)(2,1)S(1)} %bitcast.11), channel_id=1, replica_groups={{0,42,84,126,10,52,94,96,20,62,64,106,30,32,74,116,2,44,86,120,12,54,88..., dimensions={0} | all-to-all | bytes 1835008 | tf_op jit(solution)/shard_map/all_to_all | solution.py:195
  41.9 0.6 %shard_map.75.mine_ref = bf16[128,1792]{1,0:T(8,128)(2,1)S(1)} custom-call(s32[1]{0:T(128)} %bitcast.here_ref, bf16[256,128]{1,0:T(8,128)(2,1)S(1)} %bitcast.13, bf16[512,896]{1,0:T(8,128)(2,1)S(1)} %bitcast.10), custom_call_target="tpu_custom_call" | custom-call | tf_op jit(solution)/shard_map/pallas_call | solution.py:44
  42.5 2.6 %collective-permute-start.1 = (bf16[128,1792]{1,0:T(8,128)(2,1)S(1)}, bf16[128,1792]{1,0:T(8,128)(2,1)S(1)}, u32[]{:S(2)}, u32[]{:S(2)}) collective-permute-start(bf16[128,1792]{1,0:T(8,128)(2,1)S(1)} %shard_map.75.mine_ref), channel_id=1, source_target_pairs={{0,1},{1,0},{2,3},{3,2},{4,5},{5,4},{6,7},{7,6},{8,9},{9,8},{10,11... | collective-permute-start | bytes 1376264 | tf_op jit(solution)/shard_map/ppermute | solution.py:199
  45.1 0.0 copy-done.3
  45.1 0.0 copy-done.4
  45.2 0.0 slice-done
  45.2 0.0 slice-done.1
  45.2 0.0 slice-done.4
  45.2 0.0 slice-done.5
  45.2 0.0 slice-done.2
  45.2 0.0 slice-done.3
  45.2 0.0 slice-done.6
  45.2 0.0 slice-done.7
  45.3 0.0 copy-start
  45.3 1.0 %shard_map.76.own_ref = f32[128,1792]{1,0:T(8,128)S(1)} custom-call(s32[1]{0:T(128)} %bitcast.here_ref, bf16[128,1792]{1,0:T(8,128)(2,1)S(1)} %shard_map.75.mine_ref, bf16[3584,1792]{1,0:T(8,128)(2,1)S(1)} %bitcast.7, bf16[3584,1792]{1,0:T(8,128)(2,1)S(1)} %bitcast.9), custom_call_target="tpu_custom_call" | custom-call | flops 822083584 | tf_op jit(solution)/shard_map/pallas_call | solution.py:44
  46.3 0.3 collective-permute-done.1.other_ref
  46.6 0.0 copy-done
  46.6 1.2 %shard_map.77.refs_0_ = f32[8,128]{1,0:T(8,128)S(1)} custom-call(s32[1]{0:T(128)} %bitcast.here_ref, bf16[128,1792]{1,0:T(8,128)(2,1)S(1)} %collective-permute-done.1.other_ref, bf16[3584,1792]{1,0:T(8,128)(2,1)S(1)} %bitcast.7, f32[128,1792]{1,0:T(8,128)S(1)} %shard_map.76.own_ref, bf16[128,1792]{1,0:T(8,128)(2,1)S(1)} %copy-done, ...), custom_call_target="tpu_custom_call" | custom-call | flops 822083584 | tf_op jit(solution)/shard_map/pallas_call | solution.py:44
  47.8 0.8 %collective-permute-start.2 = (f32[8,128]{1,0:T(8,128)S(1)}, f32[8,128]{1,0:T(8,128)S(1)}, u32[]{:S(2)}, u32[]{:S(2)}) collective-permute-start(f32[8,128]{1,0:T(8,128)S(1)} %shard_map.77.refs_0_), channel_id=1, source_target_pairs={{0,3},{1,2},{2,1},{3,0},{4,7},{5,6},{6,5},{7,4},{8,11},{9,10},{10,... | collective-permute-start | bytes 12296 | tf_op jit(solution)/shard_map/ppermute | solution.py:216
  48.5 1.0 %collective-permute-start.3 = (f32[8,128]{1,0:T(8,128)S(1)}, f32[8,128]{1,0:T(8,128)S(1)}, u32[]{:S(2)}, u32[]{:S(2)}) collective-permute-start(f32[8,128]{1,0:T(8,128)S(1)} %shard_map.77.refs_0_), channel_id=1, source_target_pairs={{0,2},{1,3},{2,0},{3,1},{4,6},{5,7},{6,4},{7,5},{8,10},{9,11},{10,... | collective-permute-start | bytes 12296 | tf_op jit(solution)/shard_map/ppermute | solution.py:216
  49.6 0.4 collective-permute-start.4
  50.0 1.8 %shard_map.78.refs_5_ = f32[128,1792]{1,0:T(8,128)S(1)} custom-call(s32[1]{0:T(128)} %bitcast.here_ref, bf16[128,1792]{1,0:T(8,128)(2,1)S(1)} %shard_map.75.mine_ref, bf16[128,1792]{1,0:T(8,128)(2,1)S(1)} %collective-permute-done.1.other_ref, bf16[3584,1792]{1,0:T(8,128)(2,1)S(1)} %bitcast.9), custom_call_target="tpu_custom_call" | custom-call | flops 1644167168 | tf_op jit(solution)/shard_map/pallas_call | solution.py:44
  51.8 0.0 collective-permute-done.2.refs_1_
  51.8 0.0 collective-permute-done.3.refs_2_
  51.8 0.0 collective-permute-done.4.refs_3_
  51.8 1.0 %shard_map.79 = bf16[128,1792]{1,0:T(8,128)(2,1)} custom-call(f32[8,128]{1,0:T(8,128)S(1)} %shard_map.77.refs_0_, f32[8,128]{1,0:T(8,128)S(1)} %collective-permute-done.2.refs_1_, f32[8,128]{1,0:T(8,128)S(1)} %collective-permute-done.3.refs_2_, f32[8,128]{1,0:T(8,128)S(1)} %collective-permute-done.4.refs_3_, bf16[128,1792]{1,0:T(8,128)(2,1)S(1)} %copy-done, ...), custom_call_target="tpu_custom_call" | custom-call | tf_op jit(solution)/shard_map/pallas_call | solution.py:219
  (4 shorter events, 0.0 us)
Async XLA Ops:
  0.0 22.2 %collective-permute-start = (bf16[256,896]{1,0:T(8,128)(2,1)}, bf16[256,896]{1,0:T(8,128)(2,1)S(1)}, u32[]{:S(2)}, u32[]{:S(2)}) collective-permute-start(bf16[256,896]{1,0:T(8,128)(2,1)} %mine_ref.1), channel_id=1, source_target_pairs={{0,1},{1,0},{2,3},{3,2},{4,5},{5,4},{6,7},{7,6},{8,9},{9,8},{10,11... | collective-permute-start | bytes 1376264 | tf_op jit(solution)/shard_map/ppermute | solution.py:173
  1.4 0.7 %copy-start.2 = (s32[128,1]{0,1:T(1,128)S(1)}, s32[128,1]{0,1:T(1,128)}, u32[]{:S(2)}) copy-start(s32[128,1]{0,1:T(1,128)} %param.8) | copy-start | bytes 1540
  2.0 20.2 %copy-start.1 = (bf16[256,896]{1,0:T(8,128)(2,1)S(1)}, bf16[256,896]{1,0:T(8,128)(2,1)}, u32[]{:S(2)}) copy-start(bf16[256,896]{1,0:T(8,128)(2,1)} %mine_ref.1) | copy-start | bytes 1376260
  2.0 43.1 %slice-start = ((s8[12845056]{0:T(1024)(128)(4,1)}), s8[4194304]{0:T(1024)(128)(4,1)S(1)}, s32[]{:S(2)}) async-start(s8[12845056]{0:T(1024)(128)(4,1)} %bitcast.6), calls=%async_computation.2 | async-start | bytes 8388608
  2.0 43.1 %slice-start.1 = ((s8[12845056]{0:T(1024)(128)(4,1)}), s8[4194304]{0:T(1024)(128)(4,1)S(1)}, s32[]{:S(2)}) async-start(s8[12845056]{0:T(1024)(128)(4,1)} %bitcast.6), calls=%async_computation.3 | async-start | bytes 8388608
  2.0 43.1 %slice-start.4 = ((s8[12845056]{0:T(1024)(128)(4,1)}), s8[4194304]{0:T(1024)(128)(4,1)S(1)}, s32[]{:S(2)}) async-start(s8[12845056]{0:T(1024)(128)(4,1)} %bitcast.8), calls=%async_computation.6 | async-start | bytes 8388608
  2.0 43.2 %slice-start.5 = ((s8[12845056]{0:T(1024)(128)(4,1)}), s8[4194304]{0:T(1024)(128)(4,1)S(1)}, s32[]{:S(2)}) async-start(s8[12845056]{0:T(1024)(128)(4,1)} %bitcast.8), calls=%async_computation.7 | async-start | bytes 8388608
  22.2 22.9 %copy-start.3 = (f32[1792]{0:T(1024)S(1)}, f32[1792]{0:T(1024)}, u32[]{:S(2)}) copy-start(f32[1792]{0:T(1024)} %param.12) | copy-start | bytes 21508
  22.2 22.9 %copy-start.4 = (f32[1792]{0:T(1024)S(1)}, f32[1792]{0:T(1024)}, u32[]{:S(2)}) copy-start(f32[1792]{0:T(1024)} %param.13) | copy-start | bytes 21508
  22.3 23.0 %slice-start.2 = ((s8[12845056]{0:T(1024)(128)(4,1)}), s8[4194304]{0:T(1024)(128)(4,1)S(1)}, s32[]{:S(2)}) async-start(s8[12845056]{0:T(1024)(128)(4,1)} %bitcast.6), calls=%async_computation.4 | async-start | bytes 8388608
  22.3 23.0 %slice-start.3 = ((s8[12845056]{0:T(1024)(128)(4,1)}), s8[262144]{0:T(1024)(128)(4,1)S(1)}, s32[]{:S(2)}) async-start(s8[12845056]{0:T(1024)(128)(4,1)} %bitcast.6), calls=%async_computation.5 | async-start | bytes 524288
  22.3 23.0 %slice-start.6 = ((s8[12845056]{0:T(1024)(128)(4,1)}), s8[4194304]{0:T(1024)(128)(4,1)S(1)}, s32[]{:S(2)}) async-start(s8[12845056]{0:T(1024)(128)(4,1)} %bitcast.8), calls=%async_computation.8 | async-start | bytes 8388608
  22.3 23.0 %slice-start.7 = ((s8[12845056]{0:T(1024)(128)(4,1)}), s8[262144]{0:T(1024)(128)(4,1)S(1)}, s32[]{:S(2)}) async-start(s8[12845056]{0:T(1024)(128)(4,1)} %bitcast.8), calls=%async_computation.9 | async-start | bytes 524288
  42.5 4.1 %collective-permute-start.1 = (bf16[128,1792]{1,0:T(8,128)(2,1)S(1)}, bf16[128,1792]{1,0:T(8,128)(2,1)S(1)}, u32[]{:S(2)}, u32[]{:S(2)}) collective-permute-start(bf16[128,1792]{1,0:T(8,128)(2,1)S(1)} %shard_map.75.mine_ref), channel_id=1, source_target_pairs={{0,1},{1,0},{2,3},{3,2},{4,5},{5,4},{6,7},{7,6},{8,9},{9,8},{10,11... | collective-permute-start | bytes 1376264 | tf_op jit(solution)/shard_map/ppermute | solution.py:199
  45.3 1.3 %copy-start = (bf16[128,1792]{1,0:T(8,128)(2,1)S(1)}, bf16[128,1792]{1,0:T(8,128)(2,1)}, u32[]{:S(2)}) copy-start(bf16[128,1792]{1,0:T(8,128)(2,1)} %refs_4_.1) | copy-start | bytes 1376260
  47.8 4.1 %collective-permute-start.2 = (f32[8,128]{1,0:T(8,128)S(1)}, f32[8,128]{1,0:T(8,128)S(1)}, u32[]{:S(2)}, u32[]{:S(2)}) collective-permute-start(f32[8,128]{1,0:T(8,128)S(1)} %shard_map.77.refs_0_), channel_id=1, source_target_pairs={{0,3},{1,2},{2,1},{3,0},{4,7},{5,6},{6,5},{7,4},{8,11},{9,10},{10,... | collective-permute-start | bytes 12296 | tf_op jit(solution)/shard_map/ppermute | solution.py:216
  48.5 3.3 %collective-permute-start.3 = (f32[8,128]{1,0:T(8,128)S(1)}, f32[8,128]{1,0:T(8,128)S(1)}, u32[]{:S(2)}, u32[]{:S(2)}) collective-permute-start(f32[8,128]{1,0:T(8,128)S(1)} %shard_map.77.refs_0_), channel_id=1, source_target_pairs={{0,2},{1,3},{2,0},{3,1},{4,6},{5,7},{6,4},{7,5},{8,10},{9,11},{10,... | collective-permute-start | bytes 12296 | tf_op jit(solution)/shard_map/ppermute | solution.py:216
  49.6 2.3 %collective-permute-start.4 = (f32[8,128]{1,0:T(8,128)S(1)}, f32[8,128]{1,0:T(8,128)S(1)}, u32[]{:S(2)}, u32[]{:S(2)}) collective-permute-start(f32[8,128]{1,0:T(8,128)S(1)} %shard_map.77.refs_0_), channel_id=1, source_target_pairs={{0,1},{1,0},{2,3},{3,2},{4,5},{5,4},{6,7},{7,6},{8,9},{9,8},{10,11... | collective-permute-start | bytes 12296 | tf_op jit(solution)/shard_map/ppermute | solution.py:216

commit v6 on v5

--- a/solution.py
+++ b/solution.py
@@ -77,11 +77,10 @@
     rows = index.shape[0]
     held = mine_ref.shape[0]
     is_mine = ((iota((rows, 1), 0) >> 1) & 1) == core
-    lanes = iota((rows, held), 1)
-    from_mine = (jnp.where(is_mine, index, -1) == lanes).astype(f32).astype(bf16)
-    from_other = (jnp.where(is_mine, -1, index) == lanes).astype(f32).astype(bf16)
-    found = jnp.dot(from_mine, mine_ref[...], preferred_element_type=f32)
-    found = found + jnp.dot(from_other, other_ref[...], preferred_element_type=f32)
+    swapped = jnp.where(is_mine, index, index + held)
+    chosen = (swapped == iota((rows, 2 * held), 1)).astype(f32).astype(bf16)
+    table = jnp.concatenate([mine_ref[...], other_ref[...]], axis=0)
+    found = jnp.dot(chosen, table, preferred_element_type=f32)
     turns = [found[chip // 2 * 8 : chip // 2 * 8 + 8] for chip in chip_order()]
     out_ref[...] = jnp.concatenate(turns, axis=0).astype(bf16)
 
@@ -97,9 +96,8 @@
     for x in range(2):
         position = jnp.where(low, turned[4 * x : 4 * x + 1], asked[4 * x + 1 : 4 * x + 2]).astype(jnp.int32)
         target = turn_of(position >> 2) * 8 + x * 4 + (position & 3)
-        column = jnp.broadcast_to(target.astype(f32), (LANES, LANES)).T[:, 0:1].astype(jnp.int32)
-        chosen = (column == iota((LANES, slots), 1)).astype(f32).astype(bf16)
-        found = jnp.dot(chosen, arrived, preferred_element_type=f32)
+        chosen = (target == iota((slots, LANES), 0)).astype(f32).astype(bf16)
+        found = lax.dot_general(chosen, arrived, (((0,), (0,)), ((), ())), preferred_element_type=f32)
         out_ref[:, x * width : (x + 1) * width] = found.astype(bf16)
 
 
@@ -190,7 +188,7 @@
         [asked, memory_table, table_there],
         6 * MIB,
         scalars=[here],
-        flops=COVER,
+        flops=COVER // 2,
     )
     arrived = lax.all_to_all(
         sent.reshape(chips, 8, row_width), BOTH, 0, 0, axis_index_groups=in_turn, tiled=True

time: 53 us -> 52.6 us (level)
  no operation moved by 1% of the time
where the time goes in v6:
time: 52.6 us; the launch traced here: 52.5 us
  blocking collectives  38.7 us (74%)
  Pallas kernels  6.31 us (12%)
  starting transfers between devices  6.24 us (12%)
  local copies, waits for them, and re-layouts  0.73 us (1%)
    all_to_all x1, blocking collectives, local(): lax.all_to_all(message.reshape(chips, 4, LANES), BOTH, 0, 0, axis_index_g...  19.9 us
    all_to_all x1, blocking collectives, local(): lax.all_to_all(sent.reshape(chips, 8, row_width), BOTH, 0, 0, axis_index_...  18.8 us
    pallas_call x6, Pallas kernels, call(): pl.pallas_call(body, out_shape=out_shape, in_specs=[pl.BlockSpec(memory_s...  5.33 us
    ppermute x1, starting transfers between devices, local(): other = lax.ppermute(mine, 'tensor', [(k, k ^ 1) for k in range(tensor)])  2.63 us
    ppermute x3, starting transfers between devices, local(): lax.ppermute(sums, 'tensor', [(k, k ^ d) for k in range(tensor)])  2.22 us
    ppermute x1, starting transfers between devices, local(): lax.ppermute(memory_table, 'tensor', [(k, k ^ 1) for k in range(tensor)])  1.38 us
  transfers between devices with their start and end apart: 5, of which 1 were waited for; matrix products, arithmetic and copies ran while one was open for 0% of the time, Pallas kernels for 6%

profile of v6, /device:TPU:1, one launch (start us, length us, event | category | flops | bytes accessed | tf_op | source)
XLA Modules:
  0.0 52.5 jit_solution(8922998395364784470)
XLA Ops:
  0.0 1.4 %collective-permute-start = (bf16[256,896]{1,0:T(8,128)(2,1)}, bf16[256,896]{1,0:T(8,128)(2,1)S(1)}, u32[]{:S(2)}, u32[]{:S(2)}) collective-permute-start(bf16[256,896]{1,0:T(8,128)(2,1)} %mine_ref.1), channel_id=1, source_target_pairs={{0,1},{1,0},{2,3},{3,2},{4,5},{5,4},{6,7},{7,6},{8,9},{9,8},{10,11... | collective-permute-start | bytes 1376264 | tf_op jit(solution)/shard_map/ppermute | solution.py:171
  1.4 0.0 copy-start.2
  1.4 0.7 %copy-done.2 = s32[128,1]{0,1:T(1,128)S(1)} copy-done((s32[128,1]{0,1:T(1,128)S(1)}, s32[128,1]{0,1:T(1,128)}, u32[]{:S(2)}) %copy-start.2) | copy-done | bytes 536
  2.0 0.0 copy-start.1
  2.0 0.0 slice-start
  2.0 0.0 slice-start.1
  2.0 0.0 slice-start.2
  2.0 0.0 slice-start.4
  2.1 0.0 slice-start.5
  2.1 0.0 slice-start.6
  2.1 0.3 shard_map.73
  2.4 19.9 %all_to_all.10 = bf16[64,4,128]{2,1,0:T(4,128)(2,1)S(1)} all-to-all(bf16[64,4,128]{2,1,0:T(4,128)(2,1)S(1)} %bitcast.14), channel_id=1, replica_groups={{0,2,4,6,8,10,12,14,16,18,20,22,24,26,28,30,32,34,36,38,40,42,44,46,48,..., dimensions={0} | all-to-all | bytes 131072 | tf_op jit(solution)/shard_map/all_to_all | solution.py:182
  22.3 0.0 collective-permute-done.other_ref
  22.3 0.0 copy-done.1
  22.3 0.0 copy-start.3
  22.3 0.0 copy-start.4
  22.3 0.0 slice-start.3
  22.3 0.0 slice-start.7
  22.3 0.5 shard_map.74
  22.8 18.8 %all_to_all.11 = bf16[64,8,896]{2,1,0:T(8,128)(2,1)S(1)} all-to-all(bf16[64,8,896]{2,1,0:T(8,128)(2,1)S(1)} %bitcast.11), channel_id=1, replica_groups={{0,42,84,126,10,52,94,96,20,62,64,106,30,32,74,116,2,44,86,120,12,54,88..., dimensions={0} | all-to-all | bytes 1835008 | tf_op jit(solution)/shard_map/all_to_all | solution.py:193
  41.6 0.6 %shard_map.75.mine_ref = bf16[128,1792]{1,0:T(8,128)(2,1)S(1)} custom-call(s32[1]{0:T(128)} %bitcast.here_ref, bf16[256,128]{1,0:T(8,128)(2,1)S(1)} %bitcast.13, bf16[512,896]{1,0:T(8,128)(2,1)S(1)} %bitcast.10), custom_call_target="tpu_custom_call" | custom-call | tf_op jit(solution)/shard_map/pallas_call | solution.py:44
  42.2 2.6 %collective-permute-start.1 = (bf16[128,1792]{1,0:T(8,128)(2,1)S(1)}, bf16[128,1792]{1,0:T(8,128)(2,1)S(1)}, u32[]{:S(2)}, u32[]{:S(2)}) collective-permute-start(bf16[128,1792]{1,0:T(8,128)(2,1)S(1)} %shard_map.75.mine_ref), channel_id=1, source_target_pairs={{0,1},{1,0},{2,3},{3,2},{4,5},{5,4},{6,7},{7,6},{8,9},{9,8},{10,11... | collective-permute-start | bytes 1376264 | tf_op jit(solution)/shard_map/ppermute | solution.py:197
  44.8 0.0 copy-done.3
  44.8 0.0 copy-done.4
  44.8 0.0 slice-done
  44.8 0.0 slice-done.1
  44.8 0.0 slice-done.2
  44.9 0.0 slice-done.4
  44.9 0.0 slice-done.5
  44.9 0.0 slice-done.6
  44.9 0.0 slice-done.3
  44.9 0.0 slice-done.7
  44.9 0.0 copy-start
  44.9 1.0 %shard_map.76.own_ref = f32[128,1792]{1,0:T(8,128)S(1)} custom-call(s32[1]{0:T(128)} %bitcast.here_ref, bf16[128,1792]{1,0:T(8,128)(2,1)S(1)} %shard_map.75.mine_ref, bf16[3584,1792]{1,0:T(8,128)(2,1)S(1)} %bitcast.7, bf16[3584,1792]{1,0:T(8,128)(2,1)S(1)} %bitcast.9), custom_call_target="tpu_custom_call" | custom-call | flops 822083584 | tf_op jit(solution)/shard_map/pallas_call | solution.py:44
  46.0 0.3 collective-permute-done.1.other_ref
  46.2 0.0 copy-done
  46.2 1.2 %shard_map.77.refs_0_ = f32[8,128]{1,0:T(8,128)S(1)} custom-call(s32[1]{0:T(128)} %bitcast.here_ref, bf16[128,1792]{1,0:T(8,128)(2,1)S(1)} %collective-permute-done.1.other_ref, bf16[3584,1792]{1,0:T(8,128)(2,1)S(1)} %bitcast.7, f32[128,1792]{1,0:T(8,128)S(1)} %shard_map.76.own_ref, bf16[128,1792]{1,0:T(8,128)(2,1)S(1)} %copy-done, ...), custom_call_target="tpu_custom_call" | custom-call | flops 822083584 | tf_op jit(solution)/shard_map/pallas_call | solution.py:44
  47.4 0.8 %collective-permute-start.2 = (f32[8,128]{1,0:T(8,128)S(1)}, f32[8,128]{1,0:T(8,128)S(1)}, u32[]{:S(2)}, u32[]{:S(2)}) collective-permute-start(f32[8,128]{1,0:T(8,128)S(1)} %shard_map.77.refs_0_), channel_id=1, source_target_pairs={{0,3},{1,2},{2,1},{3,0},{4,7},{5,6},{6,5},{7,4},{8,11},{9,10},{10,... | collective-permute-start | bytes 12296 | tf_op jit(solution)/shard_map/ppermute | solution.py:214
  48.2 1.0 %collective-permute-start.3 = (f32[8,128]{1,0:T(8,128)S(1)}, f32[8,128]{1,0:T(8,128)S(1)}, u32[]{:S(2)}, u32[]{:S(2)}) collective-permute-start(f32[8,128]{1,0:T(8,128)S(1)} %shard_map.77.refs_0_), channel_id=1, source_target_pairs={{0,2},{1,3},{2,0},{3,1},{4,6},{5,7},{6,4},{7,5},{8,10},{9,11},{10,... | collective-permute-start | bytes 12296 | tf_op jit(solution)/shard_map/ppermute | solution.py:214
  49.2 0.4 collective-permute-start.4
  49.6 1.8 %shard_map.78.refs_5_ = f32[128,1792]{1,0:T(8,128)S(1)} custom-call(s32[1]{0:T(128)} %bitcast.here_ref, bf16[128,1792]{1,0:T(8,128)(2,1)S(1)} %shard_map.75.mine_ref, bf16[128,1792]{1,0:T(8,128)(2,1)S(1)} %collective-permute-done.1.other_ref, bf16[3584,1792]{1,0:T(8,128)(2,1)S(1)} %bitcast.9), custom_call_target="tpu_custom_call" | custom-call | flops 1644167168 | tf_op jit(solution)/shard_map/pallas_call | solution.py:44
  51.5 0.0 collective-permute-done.2.refs_1_
  51.5 0.0 collective-permute-done.3.refs_2_
  51.5 0.0 collective-permute-done.4.refs_3_
  51.5 1.0 %shard_map.79 = bf16[128,1792]{1,0:T(8,128)(2,1)} custom-call(f32[8,128]{1,0:T(8,128)S(1)} %shard_map.77.refs_0_, f32[8,128]{1,0:T(8,128)S(1)} %collective-permute-done.2.refs_1_, f32[8,128]{1,0:T(8,128)S(1)} %collective-permute-done.3.refs_2_, f32[8,128]{1,0:T(8,128)S(1)} %collective-permute-done.4.refs_3_, bf16[128,1792]{1,0:T(8,128)(2,1)S(1)} %copy-done, ...), custom_call_target="tpu_custom_call" | custom-call | tf_op jit(solution)/shard_map/pallas_call | solution.py:217
  (4 shorter events, 0.0 us)
Async XLA Ops:
  0.0 22.3 %collective-permute-start = (bf16[256,896]{1,0:T(8,128)(2,1)}, bf16[256,896]{1,0:T(8,128)(2,1)S(1)}, u32[]{:S(2)}, u32[]{:S(2)}) collective-permute-start(bf16[256,896]{1,0:T(8,128)(2,1)} %mine_ref.1), channel_id=1, source_target_pairs={{0,1},{1,0},{2,3},{3,2},{4,5},{5,4},{6,7},{7,6},{8,9},{9,8},{10,11... | collective-permute-start | bytes 1376264 | tf_op jit(solution)/shard_map/ppermute | solution.py:171
  1.4 0.7 %copy-start.2 = (s32[128,1]{0,1:T(1,128)S(1)}, s32[128,1]{0,1:T(1,128)}, u32[]{:S(2)}) copy-start(s32[128,1]{0,1:T(1,128)} %param.8) | copy-start | bytes 1540
  2.0 20.2 %copy-start.1 = (bf16[256,896]{1,0:T(8,128)(2,1)S(1)}, bf16[256,896]{1,0:T(8,128)(2,1)}, u32[]{:S(2)}) copy-start(bf16[256,896]{1,0:T(8,128)(2,1)} %mine_ref.1) | copy-start | bytes 1376260
  2.0 42.8 %slice-start = ((s8[12845056]{0:T(1024)(128)(4,1)}), s8[4194304]{0:T(1024)(128)(4,1)S(1)}, s32[]{:S(2)}) async-start(s8[12845056]{0:T(1024)(128)(4,1)} %bitcast.6), calls=%async_computation.2 | async-start | bytes 8388608
  2.0 42.8 %slice-start.1 = ((s8[12845056]{0:T(1024)(128)(4,1)}), s8[4194304]{0:T(1024)(128)(4,1)S(1)}, s32[]{:S(2)}) async-start(s8[12845056]{0:T(1024)(128)(4,1)} %bitcast.6), calls=%async_computation.3 | async-start | bytes 8388608
  2.0 42.8 %slice-start.2 = ((s8[12845056]{0:T(1024)(128)(4,1)}), s8[4194304]{0:T(1024)(128)(4,1)S(1)}, s32[]{:S(2)}) async-start(s8[12845056]{0:T(1024)(128)(4,1)} %bitcast.6), calls=%async_computation.4 | async-start | bytes 8388608
  2.0 42.8 %slice-start.4 = ((s8[12845056]{0:T(1024)(128)(4,1)}), s8[4194304]{0:T(1024)(128)(4,1)S(1)}, s32[]{:S(2)}) async-start(s8[12845056]{0:T(1024)(128)(4,1)} %bitcast.8), calls=%async_computation.6 | async-start | bytes 8388608
  2.1 42.8 %slice-start.5 = ((s8[12845056]{0:T(1024)(128)(4,1)}), s8[4194304]{0:T(1024)(128)(4,1)S(1)}, s32[]{:S(2)}) async-start(s8[12845056]{0:T(1024)(128)(4,1)} %bitcast.8), calls=%async_computation.7 | async-start | bytes 8388608
  2.1 42.8 %slice-start.6 = ((s8[12845056]{0:T(1024)(128)(4,1)}), s8[4194304]{0:T(1024)(128)(4,1)S(1)}, s32[]{:S(2)}) async-start(s8[12845056]{0:T(1024)(128)(4,1)} %bitcast.8), calls=%async_computation.8 | async-start | bytes 8388608
  22.3 22.5 %copy-start.3 = (f32[1792]{0:T(1024)S(1)}, f32[1792]{0:T(1024)}, u32[]{:S(2)}) copy-start(f32[1792]{0:T(1024)} %param.12) | copy-start | bytes 21508
  22.3 22.5 %copy-start.4 = (f32[1792]{0:T(1024)S(1)}, f32[1792]{0:T(1024)}, u32[]{:S(2)}) copy-start(f32[1792]{0:T(1024)} %param.13) | copy-start | bytes 21508
  22.3 22.6 %slice-start.3 = ((s8[12845056]{0:T(1024)(128)(4,1)}), s8[262144]{0:T(1024)(128)(4,1)S(1)}, s32[]{:S(2)}) async-start(s8[12845056]{0:T(1024)(128)(4,1)} %bitcast.6), calls=%async_computation.5 | async-start | bytes 524288
  22.3 22.6 %slice-start.7 = ((s8[12845056]{0:T(1024)(128)(4,1)}), s8[262144]{0:T(1024)(128)(4,1)S(1)}, s32[]{:S(2)}) async-start(s8[12845056]{0:T(1024)(128)(4,1)} %bitcast.8), calls=%async_computation.9 | async-start | bytes 524288
  42.2 4.1 %collective-permute-start.1 = (bf16[128,1792]{1,0:T(8,128)(2,1)S(1)}, bf16[128,1792]{1,0:T(8,128)(2,1)S(1)}, u32[]{:S(2)}, u32[]{:S(2)}) collective-permute-start(bf16[128,1792]{1,0:T(8,128)(2,1)S(1)} %shard_map.75.mine_ref), channel_id=1, source_target_pairs={{0,1},{1,0},{2,3},{3,2},{4,5},{5,4},{6,7},{7,6},{8,9},{9,8},{10,11... | collective-permute-start | bytes 1376264 | tf_op jit(solution)/shard_map/ppermute | solution.py:197
  44.9 1.3 %copy-start = (bf16[128,1792]{1,0:T(8,128)(2,1)S(1)}, bf16[128,1792]{1,0:T(8,128)(2,1)}, u32[]{:S(2)}) copy-start(bf16[128,1792]{1,0:T(8,128)(2,1)} %refs_4_.1) | copy-start | bytes 1376260
  47.4 4.1 %collective-permute-start.2 = (f32[8,128]{1,0:T(8,128)S(1)}, f32[8,128]{1,0:T(8,128)S(1)}, u32[]{:S(2)}, u32[]{:S(2)}) collective-permute-start(f32[8,128]{1,0:T(8,128)S(1)} %shard_map.77.refs_0_), channel_id=1, source_target_pairs={{0,3},{1,2},{2,1},{3,0},{4,7},{5,6},{6,5},{7,4},{8,11},{9,10},{10,... | collective-permute-start | bytes 12296 | tf_op jit(solution)/shard_map/ppermute | solution.py:214
  48.2 3.3 %collective-permute-start.3 = (f32[8,128]{1,0:T(8,128)S(1)}, f32[8,128]{1,0:T(8,128)S(1)}, u32[]{:S(2)}, u32[]{:S(2)}) collective-permute-start(f32[8,128]{1,0:T(8,128)S(1)} %shard_map.77.refs_0_), channel_id=1, source_target_pairs={{0,2},{1,3},{2,0},{3,1},{4,6},{5,7},{6,4},{7,5},{8,10},{9,11},{10,... | collective-permute-start | bytes 12296 | tf_op jit(solution)/shard_map/ppermute | solution.py:214
  49.2 2.3 %collective-permute-start.4 = (f32[8,128]{1,0:T(8,128)S(1)}, f32[8,128]{1,0:T(8,128)S(1)}, u32[]{:S(2)}, u32[]{:S(2)}) collective-permute-start(f32[8,128]{1,0:T(8,128)S(1)} %shard_map.77.refs_0_), channel_id=1, source_target_pairs={{0,1},{1,0},{2,3},{3,2},{4,5},{5,4},{6,7},{7,6},{8,9},{9,8},{10,11... | collective-permute-start | bytes 12296 | tf_op jit(solution)/shard_map/ppermute | solution.py:214

commit v7 on v4

--- a/solution.py
+++ b/solution.py
@@ -16,19 +16,6 @@
 
 f32 = jnp.float32
 bf16 = jnp.bfloat16
-
-
-def chip_order():
-    order = []
-    for k in range(64):
-        a, b, c = k % 4, (k // 4) % 4, k // 16
-        order.append(a * 16 + (a + b) % 4 * 4 + (a + b + c) % 4)
-    return order
-
-
-def turn_of(chip):
-    z, y, x = chip >> 4, (chip >> 2) & 3, chip & 3
-    return z + ((y - z) & 3) * 4 + ((x - y) & 3) * 16
 
 
 def iota(shape, dim):
@@ -52,56 +39,71 @@
     )(*scalars, *inputs)
 
 
-def request_kernel(rows_held, hash_ref, out_ref):
-    row = hash_ref[...]
-    owner = row // rows_held
-    local = row - owner * rows_held
-    owner_rows = jnp.broadcast_to(owner.astype(f32), (LANES, LANES))
-    owner_cols = owner_rows.T
-    earlier = (owner_rows == owner_cols) & (iota((LANES, LANES), 0) < iota((LANES, LANES), 1))
-    slot = jnp.sum(earlier.astype(f32), axis=0, keepdims=True)
-    position = owner * 2 + slot.astype(jnp.int32)
-    place = iota((LANES, LANES), 0)
-    local_f = local.astype(f32)
-    zero = jnp.zeros((LANES, LANES), f32)
-    ask0 = jnp.sum(jnp.where(position == 2 * place, local_f, zero), axis=1, keepdims=True)
-    ask1 = jnp.sum(jnp.where(position == 2 * place + 1, local_f, zero), axis=1, keepdims=True)
-    asks = jnp.where(iota((LANES, LANES), 1) < LANES // 2, ask0, ask1)
-    where = jnp.broadcast_to(position.astype(f32), (LANES, LANES))
-    both = jnp.stack([where, asks], axis=1)
-    out_ref[...] = both.reshape(2 * LANES, LANES).astype(bf16)
-
-
-def gather_kernel(asked_ref, table_ref, out_ref):
-    asked = asked_ref[...].astype(f32)
-    rows = asked.shape[0]
-    even = (iota((rows, 1), 0) % 2) == 0
-    ahead = pltpu.roll(asked, rows - 1, 0)
-    index = jnp.where(even, ahead[:, 0:1], asked[:, LANES - 1 :])
-    held = table_ref.shape[0]
-    chosen = (index.astype(jnp.int32) == iota((rows, held), 1)).astype(f32).astype(bf16)
-    found = jnp.dot(chosen, table_ref[...], preferred_element_type=f32)
-    turns = [found[chip // 2 * 8 : chip // 2 * 8 + 8] for chip in chip_order()]
-    out_ref[...] = jnp.concatenate(turns, axis=0).astype(bf16)
-
-
-def place_kernel(heads, where_ref, asked_ref, arrived_ref, out_ref):
-    core = where_ref[0] & 1
-    start = pl.multiple_of((where_ref[0] >> 2) * 8, 8)
-    position = asked_ref[pl.ds(start, 8), :].astype(jnp.int32)
-    target = turn_of(position >> 2) * 8 + (position & 1)
-    target = jnp.where(((position >> 1) & 1) == core, target, -8).astype(f32)
+def request_kernel(rows_held, which, here_ref, hash_ref, *refs):
+    *before, out_ref, row_ref, sem = refs
+    half = here_ref[0] >> 6
+
+    @pl.when(half == which)
+    def _():
+        copy = pltpu.make_async_copy(hash_ref, row_ref, sem)
+        copy.start()
+        copy.wait()
+        row = row_ref[...]
+        owner = row // rows_held
+        local = (row - owner * rows_held).astype(f32)
+        owner_rows = jnp.broadcast_to(owner.astype(f32), (LANES, LANES))
+        owner_cols = owner_rows.T
+        earlier = (owner_rows == owner_cols) & (iota((LANES, LANES), 0) < iota((LANES, LANES), 1))
+        slot = jnp.sum(earlier.astype(f32), axis=0, keepdims=True).astype(jnp.int32)
+        z = owner >> 5
+        near = (z >> 1) == half
+        server = (jnp.where(near, z, 3 - z) & 1) * 32 + (owner & 31)
+        landing = server * 4 + jnp.where(near, slot, slot + 2)
+        rows = out_ref.shape[0]
+        asks = jnp.where(landing == iota((rows, LANES), 0), local, jnp.zeros((rows, LANES), f32))
+        asks = jnp.sum(asks, axis=1, keepdims=True)
+        where = landing.astype(f32)
+        turned = pltpu.roll(where, LANES // 2, 1)
+        first = (iota((rows, LANES), 0) & 3) == 0
+        message = jnp.where(iota((rows, LANES), 1) < LANES // 2, asks, jnp.where(first, turned, where))
+        out_ref[...] = message.astype(bf16)
+
+    for ref in before:
+
+        @pl.when(half != which)
+        def _():
+            out_ref[...] = ref[...]
+
+
+def gather_kernel(asked_ref, mine_ref, other_ref, out_ref):
+    index = asked_ref[...].astype(jnp.int32)[:, 0:1]
+    rows = index.shape[0]
+    held = mine_ref.shape[0]
+    index = jnp.where(((iota((rows, 1), 0) >> 1) & 1) == 0, index, index + held)
+    chosen = (index == iota((rows, 2 * held), 1)).astype(f32).astype(bf16)
+    table = jnp.concatenate([mine_ref[...], other_ref[...]], axis=0)
+    found = jnp.dot(chosen, table, preferred_element_type=f32).astype(bf16)
+    both = [found[start : start + 16] for start in range(0, rows, 16) for _ in range(2)]
+    out_ref[...] = jnp.concatenate(both, axis=0)
+
+
+def place_kernel(heads, here_ref, asked_ref, arrived_ref, out_ref):
+    core = here_ref[0] & 1
+    start = pl.multiple_of(((here_ref[0] >> 2) & 15) * 16, 16)
+    asked = asked_ref[pl.ds(start, 16), :].astype(f32)
     arrived = arrived_ref[...]
     slots = arrived.shape[0]
     width = arrived.shape[1]
-    chosen = []
-    for head in heads:
-        column = jnp.broadcast_to(target[2 * head : 2 * head + 1, :], (LANES, LANES)).T
-        column = column[:, 0:1].astype(jnp.int32) + 2 * head
-        chosen.append((column == iota((LANES, slots), 1)).astype(f32).astype(bf16))
-    found = jnp.dot(jnp.concatenate(chosen, axis=0), arrived, preferred_element_type=f32).astype(bf16)
-    for k in range(len(heads)):
-        out_ref[:, k * width : (k + 1) * width] = found[k * LANES : (k + 1) * LANES]
+    low = iota((1, LANES), 1) < LANES // 2
+    turned = pltpu.roll(asked, LANES // 2, 1)
+    for k, head in enumerate(heads):
+        landing = jnp.where(low, turned[4 * head : 4 * head + 1], asked[4 * head + 1 : 4 * head + 2])
+        landing = landing.astype(jnp.int32)
+        target = (landing >> 3) * 16 + head * 4 + (landing & 3)
+        target = jnp.where(((landing >> 2) & 1) == core, target, -1)
+        chosen = (target == iota((slots, LANES), 0)).astype(f32).astype(bf16)
+        found = lax.dot_general(chosen, arrived, (((0,), (0,)), ((), ())), preferred_element_type=f32)
+        out_ref[:, k * width : (k + 1) * width] = found.astype(bf16)
 
 
 def row_of_sums(terms):
@@ -111,7 +113,7 @@
     return jnp.sum(parts.T, axis=0, keepdims=True)
 
 
-def first_kernel(mine_ref, other_ref, weight_ref, out_ref):
+def first_kernel(mine_ref, other_ref, weight_ref, _, out_ref):
     memory = mine_ref[...] + other_ref[...]
     out_ref[...] = jnp.dot(memory, weight_ref[: memory.shape[1], :], preferred_element_type=f32)
 
@@ -162,20 +164,40 @@
 
     here = lax.axis_index(BOTH).astype(jnp.int32).reshape(1)
     hash_rows, here, hidden_gain, key_gain = lax.optimization_barrier((hash_rows, here, hidden_gain, key_gain))
-    message = call(
-        lambda *refs: request_kernel(rows_held, *refs),
-        shape((2 * devices, LANES), bf16),
-        [hash_rows.reshape(1, LANES)],
-        4 * MIB,
-        flops=COVER,
+    servers = devices // 2
+    rows = pltpu.with_memory_space_constraint(hash_rows.reshape(1, LANES), pltpu.HBM)
+
+    def request(which, *before):
+        return pl.pallas_call(
+            lambda *refs: request_kernel(rows_held, which, *refs),
+            out_shape=shape((4 * servers, LANES), bf16),
+            in_specs=[pl.BlockSpec(memory_space=pltpu.SMEM), pl.BlockSpec(memory_space=pltpu.HBM)] + vmem(len(before)),
+            out_specs=vmem(1)[0],
+            scratch_shapes=[pltpu.VMEM((1, LANES), jnp.int32), pltpu.SemaphoreType.DMA(())],
+            compiler_params=pltpu.CompilerParams(vmem_limit_bytes=2 * MIB),
+            cost_estimate=pl.CostEstimate(flops=COVER if before else 1, transcendentals=0, bytes_accessed=1),
+        )(here, rows, *before)
+
+    message = request(0)
+    message, memory_table = lax.optimization_barrier((message, memory_table))
+    swap = [(k, (3 - (k >> 5)) * 32 + (k & 31)) for k in range(devices)]
+    table_there = lax.ppermute(memory_table, BOTH, swap)
+    message = request(1, message)
+    halves_of_z = [[half * servers + k for k in range(servers)] for half in range(2)]
+    same_core = [[k for k in half if k % 2 == core] for half in halves_of_z for core in range(2)]
+    asked = lax.all_to_all(
+        message.reshape(servers, 4, LANES), BOTH, 0, 0, axis_index_groups=halves_of_z, tiled=True
+    ).reshape(4 * servers, LANES)
+    sent = call(
+        gather_kernel,
+        shape((8 * servers, row_width), bf16),
+        [asked, memory_table, table_there],
+        6 * MIB,
+        flops=14_000_000_000,
     )
-    asked = lax.all_to_all(message.reshape(devices, 2, LANES), BOTH, 0, 0, tiled=True)
-    asked = asked.reshape(2 * devices, LANES)
-    sent = call(gather_kernel, shape((4 * devices, row_width), bf16), [asked, memory_table], 6 * MIB, flops=COVER)
-    same_core = [[2 * chip + core for chip in chip_order()] for core in range(2)]
     arrived = lax.all_to_all(
-        sent.reshape(devices // 2, 8, row_width), BOTH, 0, 0, axis_index_groups=same_core, tiled=True
-    ).reshape(4 * devices, row_width)
+        sent.reshape(servers // 2, 16, row_width), BOTH, 0, 0, axis_index_groups=same_core, tiled=True
+    ).reshape(8 * servers, row_width)
     halves = []
     for heads in ((0, 1), (2, 3)):
         mine = call(
@@ -191,13 +213,7 @@
     key_weight = pltpu.with_memory_space_constraint(key_weight, pltpu.VMEM)
     value_weight = pltpu.with_memory_space_constraint(value_weight, pltpu.VMEM)
     partial = shape((LANES, columns), f32)
-    key = call(
-        lambda mine, other, weight, _, out: first_kernel(mine, other, weight, out),
-        partial,
-        [*halves[0], key_weight, value_weight],
-        6 * MIB,
-        flops=work,
-    )
+    key = call(first_kernel, partial, [*halves[0], key_weight, value_weight], 6 * MIB, flops=work)
     sums = call(
         key_kernel,
         shape((8, LANES), f32),

time: 53.5 us -> 51.2 us (0.957)
  blocking collectives: 39.9 us -> 34.4 us
  starting transfers between devices: 4.83 us -> 8.07 us
  local copies, waits for them, and re-layouts: 0.72 us -> 0.08 us
    all_to_all x2, blocking collectives: 39.9 us -> 34.4 us  [the longest x1 17.7 us: local(): lax.all_to_all(sent.reshape(servers // 2, 16, row_width), BOTH, 0, 0, axi...]
    ppermute x0 -> x1, starting transfers between devices: none -> 3.71 us  [local(): table_there = lax.ppermute(memory_table, BOTH, swap)]
    pallas_call x0 -> x2, Pallas kernels: none -> 0.97 us  [request(): pl.pallas_call(lambda *refs: request_kernel(rows_held, which, *refs), out...]
    unnamed x26 -> x24, local copies, waits for them, and re-layouts: 0.71 us -> 0.06 us
    pallas_call x7 -> x6, Pallas kernels: 6.06 us -> 5.59 us  [call(): pl.pallas_call(body, out_shape=out_shape, in_specs=[pl.BlockSpec(memory_s...]
  transfers between devices with their start and end apart: 5 -> 6, of which waited for: 1 -> 1; matrix products, arithmetic and copies ran while one was open for 0% -> 0% of each run, Pallas kernels for 7% -> 7%
where the time goes in v7:
time: 51.2 us; the launch traced here: 51.1 us
  blocking collectives  34.4 us (67%)
  starting transfers between devices  8.07 us (16%)
  Pallas kernels  7.55 us (15%)
  waiting for transfers between devices  0.75 us (1%)
    all_to_all x1, blocking collectives, local(): lax.all_to_all(sent.reshape(servers // 2, 16, row_width), BOTH, 0, 0, axi...  17.7 us
    all_to_all x1, blocking collectives, local(): lax.all_to_all(message.reshape(servers, 4, LANES), BOTH, 0, 0, axis_index...  16.7 us
    pallas_call x6, Pallas kernels, call(): pl.pallas_call(body, out_shape=out_shape, in_specs=[pl.BlockSpec(memory_s...  5.59 us
    ppermute x1, starting transfers between devices, local(): table_there = lax.ppermute(memory_table, BOTH, swap)  3.71 us
    ppermute x3, starting transfers between devices, local(): lax.ppermute(sums, 'tensor', [(k, k ^ d) for k in range(tensor)])  2.22 us
    ppermute x2, starting transfers between devices, local(): lax.ppermute(mine, 'tensor', [(k, k ^ 1) for k in range(tensor)])  2.14 us
  transfers between devices with their start and end apart: 6, of which 1 were waited for; matrix products, arithmetic and copies ran while one was open for 0% of the time, Pallas kernels for 7%

profile of v7, /device:TPU:1, one launch (start us, length us, event | category | flops | bytes accessed | tf_op | source)
XLA Modules:
  0.0 51.1 jit_solution(1770811319331396234)
XLA Ops:
  0.0 0.9 %shard_map.73.refs_2_ = bf16[256,128]{1,0:T(8,128)(2,1)S(1)} custom-call(s32[1]{0:T(128)} %bitcast.refs_0_, s32[1,128]{1,0:T(1,128)} %bitcast.17), custom_call_target="tpu_custom_call" | custom-call | flops 1 | bytes 1 | tf_op jit(solution)/shard_map/pallas_call | solution.py:171
  1.0 0.0 copy-start.1
  1.0 3.7 %collective-permute-start = (bf16[256,896]{1,0:T(8,128)(2,1)}, bf16[256,896]{1,0:T(8,128)(2,1)S(1)}, u32[]{:S(2)}, u32[]{:S(2)}) collective-permute-start(bf16[256,896]{1,0:T(8,128)(2,1)} %mine_ref), channel_id=1, source_target_pairs={{0,96},{1,97},{2,98},{3,99},{4,100},{5,101},{6,102},{7,103},{8,104... | collective-permute-start | bytes 1376264 | tf_op jit(solution)/shard_map/ppermute | solution.py:184
  4.7 0.0 slice-start
  4.7 0.0 slice-start.1
  4.7 0.0 slice-start.2
  4.7 0.0 slice-start.4
  4.7 0.0 slice-start.5
  4.7 0.0 slice-start.6
  4.8 16.7 %all_to_all.10 = bf16[64,4,128]{2,1,0:T(4,128)(2,1)S(1)} all-to-all(bf16[64,4,128]{2,1,0:T(4,128)(2,1)S(1)} %bitcast.16), channel_id=1, replica_groups={{0,1,2,3,4,5,6,7,8,9,10,11,12,13,14,15,16,17,18,19,20,21,22,23,24,25,26..., dimensions={0} | all-to-all | bytes 131072 | tf_op jit(solution)/shard_map/all_to_all | solution.py:188
  21.5 0.0 collective-permute-done.other_ref
  21.5 0.0 copy-done.1
  21.5 0.0 copy-start.2
  21.5 0.0 copy-start.3
  21.5 0.0 slice-start.3
  21.5 0.0 slice-start.7
  21.5 0.5 shard_map.75
  22.0 17.7 %all_to_all.11 = bf16[32,16,896]{2,1,0:T(8,128)(2,1)S(1)} all-to-all(bf16[32,16,896]{2,1,0:T(8,128)(2,1)S(1)} %bitcast.12), channel_id=1, replica_groups={{0,2,4,6,8,10,12,14,16,18,20,22,24,26,28,30,32,34,36,38,40,42,44,46,48,..., dimensions={0} | all-to-all | bytes 1835008 | tf_op jit(solution)/shard_map/all_to_all | solution.py:198
  39.7 0.5 %shard_map.77.mine_ref.mine0_ref = bf16[128,1792]{1,0:T(8,128)(2,1)S(1)} custom-call(s32[1]{0:T(128)} %bitcast.refs_0_, bf16[256,128]{1,0:T(8,128)(2,1)S(1)} %bitcast.14, bf16[512,896]{1,0:T(8,128)(2,1)S(1)} %bitcast.10), custom_call_target="tpu_custom_call" | custom-call | tf_op jit(solution)/shard_map/pallas_call | solution.py:31
  40.2 2.0 %collective-permute-start.2 = (bf16[128,1792]{1,0:T(8,128)(2,1)S(1)}, bf16[128,1792]{1,0:T(8,128)(2,1)S(1)}, u32[]{:S(2)}, u32[]{:S(2)}) collective-permute-start(bf16[128,1792]{1,0:T(8,128)(2,1)S(1)} %shard_map.77.mine_ref.mine0_ref), channel_id=1, source_target_pairs={{0,1},{1,0},{2,3},{3,2},{4,5},{5,4},{6,7},{7,6},{8,9},{9,8},{10,11... | collective-permute-start | bytes 1376264 | tf_op jit(solution)/shard_map/ppermute | solution.py:210
  42.3 0.5 %shard_map.76.mine_ref.mine1_ref = bf16[128,1792]{1,0:T(8,128)(2,1)S(1)} custom-call(s32[1]{0:T(128)} %bitcast.refs_0_, bf16[256,128]{1,0:T(8,128)(2,1)S(1)} %bitcast.15, bf16[512,896]{1,0:T(8,128)(2,1)S(1)} %bitcast.11), custom_call_target="tpu_custom_call" | custom-call | tf_op jit(solution)/shard_map/pallas_call | solution.py:31
  42.8 0.1 collective-permute-start.1
  42.9 0.0 copy-done.2
  42.9 0.0 copy-done.3
  43.0 0.0 copy-start
  43.0 0.7 %collective-permute-done.2.other_ref.other0_ref = bf16[128,1792]{1,0:T(8,128)(2,1)S(1)} collective-permute-done((bf16[128,1792]{1,0:T(8,128)(2,1)S(1)}, bf16[128,1792]{1,0:T(8,128)(2,1)S(1)}, u32[]{:S(2)}, u32[]{:S(2)}) %collective-permute-start.2) | collective-permute-done | bytes 458784 | tf_op jit(solution)/shard_map/ppermute | solution.py:210
  43.7 0.0 slice-done
  43.7 0.0 slice-done.1
  43.7 0.0 slice-done.2
  43.7 0.0 slice-done.4
  43.7 0.0 slice-done.5
  43.7 0.0 slice-done.6
  43.7 0.0 slice-done.3
  43.7 0.0 slice-done.7
  43.8 1.0 %shard_map.78.first_ref = f32[128,1792]{1,0:T(8,128)S(1)} custom-call(bf16[128,1792]{1,0:T(8,128)(2,1)S(1)} %shard_map.77.mine_ref.mine0_ref, bf16[128,1792]{1,0:T(8,128)(2,1)S(1)} %collective-permute-done.2.other_ref.other0_ref, bf16[3584,1792]{1,0:T(8,128)(2,1)S(1)} %bitcast.7, bf16[3584,1792]{1,0:T(8,128)(2,1)S(1)} %bitcast.9), custom_call_target="tpu_custom_call" | custom-call | flops 822083584 | tf_op jit(solution)/shard_map/pallas_call | solution.py:31
  44.8 0.0 collective-permute-done.1.other_ref.other1_ref
  44.8 0.0 copy-done
  44.8 1.1 %shard_map.79.refs_0_ = f32[8,128]{1,0:T(8,128)S(1)} custom-call(bf16[128,1792]{1,0:T(8,128)(2,1)S(1)} %shard_map.76.mine_ref.mine1_ref, bf16[128,1792]{1,0:T(8,128)(2,1)S(1)} %collective-permute-done.1.other_ref.other1_ref, bf16[3584,1792]{1,0:T(8,128)(2,1)S(1)} %bitcast.7, f32[128,1792]{1,0:T(8,128)S(1)} %shard_map.78.first_ref, ...), custom_call_target="tpu_custom_call" | custom-call | flops 822083584 | tf_op jit(solution)/shard_map/pallas_call | solution.py:31
  46.0 0.5 %collective-permute-start.3 = (f32[8,128]{1,0:T(8,128)S(1)}, f32[8,128]{1,0:T(8,128)S(1)}, u32[]{:S(2)}, u32[]{:S(2)}) collective-permute-start(f32[8,128]{1,0:T(8,128)S(1)} %shard_map.79.refs_0_), channel_id=1, source_target_pairs={{0,3},{1,2},{2,1},{3,0},{4,7},{5,6},{6,5},{7,4},{8,11},{9,10},{10,... | collective-permute-start | bytes 12296 | tf_op jit(solution)/shard_map/ppermute | solution.py:224
  46.5 1.3 %collective-permute-start.4 = (f32[8,128]{1,0:T(8,128)S(1)}, f32[8,128]{1,0:T(8,128)S(1)}, u32[]{:S(2)}, u32[]{:S(2)}) collective-permute-start(f32[8,128]{1,0:T(8,128)S(1)} %shard_map.79.refs_0_), channel_id=1, source_target_pairs={{0,2},{1,3},{2,0},{3,1},{4,6},{5,7},{6,4},{7,5},{8,10},{9,11},{10,... | collective-permute-start | bytes 12296 | tf_op jit(solution)/shard_map/ppermute | solution.py:224
  47.8 0.4 collective-permute-start.5
  48.2 1.9 %shard_map.80.refs_5_ = f32[128,1792]{1,0:T(8,128)S(1)} custom-call(bf16[128,1792]{1,0:T(8,128)(2,1)S(1)} %shard_map.77.mine_ref.mine0_ref, bf16[128,1792]{1,0:T(8,128)(2,1)S(1)} %collective-permute-done.2.other_ref.other0_ref, bf16[128,1792]{1,0:T(8,128)(2,1)S(1)} %shard_map.76.mine_ref.mine1_ref, ...), custom_call_target="tpu_custom_call" | custom-call | flops 1644167168 | tf_op jit(solution)/shard_map/pallas_call | solution.py:31
  50.1 0.0 collective-permute-done.3.refs_1_
  50.1 0.0 collective-permute-done.4.refs_2_
  50.1 0.0 collective-permute-done.5.refs_3_
  50.1 1.0 %shard_map.81 = bf16[128,1792]{1,0:T(8,128)(2,1)} custom-call(f32[8,128]{1,0:T(8,128)S(1)} %shard_map.79.refs_0_, f32[8,128]{1,0:T(8,128)S(1)} %collective-permute-done.3.refs_1_, f32[8,128]{1,0:T(8,128)S(1)} %collective-permute-done.4.refs_2_, f32[8,128]{1,0:T(8,128)S(1)} %collective-permute-done.5.refs_3_, bf16[128,1792]{1,0:T(8,128)(2,1)S(1)} %copy-done, ...), custom_call_target="tpu_custom_call" | custom-call | tf_op jit(solution)/shard_map/pallas_call | solution.py:227
  (5 shorter events, 0.0 us)
Async XLA Ops:
  1.0 20.5 %copy-start.1 = (bf16[256,896]{1,0:T(8,128)(2,1)S(1)}, bf16[256,896]{1,0:T(8,128)(2,1)}, u32[]{:S(2)}) copy-start(bf16[256,896]{1,0:T(8,128)(2,1)} %mine_ref) | copy-start | bytes 1376260
  1.0 20.5 %collective-permute-start = (bf16[256,896]{1,0:T(8,128)(2,1)}, bf16[256,896]{1,0:T(8,128)(2,1)S(1)}, u32[]{:S(2)}, u32[]{:S(2)}) collective-permute-start(bf16[256,896]{1,0:T(8,128)(2,1)} %mine_ref), channel_id=1, source_target_pairs={{0,96},{1,97},{2,98},{3,99},{4,100},{5,101},{6,102},{7,103},{8,104... | collective-permute-start | bytes 1376264 | tf_op jit(solution)/shard_map/ppermute | solution.py:184
  4.7 39.0 %slice-start = ((s8[12845056]{0:T(1024)(128)(4,1)}), s8[4194304]{0:T(1024)(128)(4,1)S(1)}, s32[]{:S(2)}) async-start(s8[12845056]{0:T(1024)(128)(4,1)} %bitcast.6), calls=%async_computation.2 | async-start | bytes 8388608
  4.7 39.0 %slice-start.1 = ((s8[12845056]{0:T(1024)(128)(4,1)}), s8[4194304]{0:T(1024)(128)(4,1)S(1)}, s32[]{:S(2)}) async-start(s8[12845056]{0:T(1024)(128)(4,1)} %bitcast.6), calls=%async_computation.3 | async-start | bytes 8388608
  4.7 39.0 %slice-start.2 = ((s8[12845056]{0:T(1024)(128)(4,1)}), s8[4194304]{0:T(1024)(128)(4,1)S(1)}, s32[]{:S(2)}) async-start(s8[12845056]{0:T(1024)(128)(4,1)} %bitcast.6), calls=%async_computation.4 | async-start | bytes 8388608
  4.7 39.0 %slice-start.4 = ((s8[12845056]{0:T(1024)(128)(4,1)}), s8[4194304]{0:T(1024)(128)(4,1)S(1)}, s32[]{:S(2)}) async-start(s8[12845056]{0:T(1024)(128)(4,1)} %bitcast.8), calls=%async_computation.6 | async-start | bytes 8388608
  4.7 39.0 %slice-start.5 = ((s8[12845056]{0:T(1024)(128)(4,1)}), s8[4194304]{0:T(1024)(128)(4,1)S(1)}, s32[]{:S(2)}) async-start(s8[12845056]{0:T(1024)(128)(4,1)} %bitcast.8), calls=%async_computation.7 | async-start | bytes 8388608
  4.7 39.0 %slice-start.6 = ((s8[12845056]{0:T(1024)(128)(4,1)}), s8[4194304]{0:T(1024)(128)(4,1)S(1)}, s32[]{:S(2)}) async-start(s8[12845056]{0:T(1024)(128)(4,1)} %bitcast.8), calls=%async_computation.8 | async-start | bytes 8388608
  21.5 21.4 %copy-start.2 = (f32[1792]{0:T(1024)S(1)}, f32[1792]{0:T(1024)}, u32[]{:S(2)}) copy-start(f32[1792]{0:T(1024)} %param.12) | copy-start | bytes 21508
  21.5 21.5 %copy-start.3 = (f32[1792]{0:T(1024)S(1)}, f32[1792]{0:T(1024)}, u32[]{:S(2)}) copy-start(f32[1792]{0:T(1024)} %param.13) | copy-start | bytes 21508
  21.5 22.3 %slice-start.3 = ((s8[12845056]{0:T(1024)(128)(4,1)}), s8[262144]{0:T(1024)(128)(4,1)S(1)}, s32[]{:S(2)}) async-start(s8[12845056]{0:T(1024)(128)(4,1)} %bitcast.6), calls=%async_computation.5 | async-start | bytes 524288
  21.5 22.2 %slice-start.7 = ((s8[12845056]{0:T(1024)(128)(4,1)}), s8[262144]{0:T(1024)(128)(4,1)S(1)}, s32[]{:S(2)}) async-start(s8[12845056]{0:T(1024)(128)(4,1)} %bitcast.8), calls=%async_computation.9 | async-start | bytes 524288
  40.2 3.5 %collective-permute-start.2 = (bf16[128,1792]{1,0:T(8,128)(2,1)S(1)}, bf16[128,1792]{1,0:T(8,128)(2,1)S(1)}, u32[]{:S(2)}, u32[]{:S(2)}) collective-permute-start(bf16[128,1792]{1,0:T(8,128)(2,1)S(1)} %shard_map.77.mine_ref.mine0_ref), channel_id=1, source_target_pairs={{0,1},{1,0},{2,3},{3,2},{4,5},{5,4},{6,7},{7,6},{8,9},{9,8},{10,11... | collective-permute-start | bytes 1376264 | tf_op jit(solution)/shard_map/ppermute | solution.py:210
  42.8 2.0 %collective-permute-start.1 = (bf16[128,1792]{1,0:T(8,128)(2,1)S(1)}, bf16[128,1792]{1,0:T(8,128)(2,1)S(1)}, u32[]{:S(2)}, u32[]{:S(2)}) collective-permute-start(bf16[128,1792]{1,0:T(8,128)(2,1)S(1)} %shard_map.76.mine_ref.mine1_ref), channel_id=1, source_target_pairs={{0,1},{1,0},{2,3},{3,2},{4,5},{5,4},{6,7},{7,6},{8,9},{9,8},{10,11... | collective-permute-start | bytes 1376264 | tf_op jit(solution)/shard_map/ppermute | solution.py:210
  43.0 1.9 %copy-start = (bf16[128,1792]{1,0:T(8,128)(2,1)S(1)}, bf16[128,1792]{1,0:T(8,128)(2,1)}, u32[]{:S(2)}) copy-start(bf16[128,1792]{1,0:T(8,128)(2,1)} %refs_4_.1) | copy-start | bytes 1376260
  46.0 4.1 %collective-permute-start.3 = (f32[8,128]{1,0:T(8,128)S(1)}, f32[8,128]{1,0:T(8,128)S(1)}, u32[]{:S(2)}, u32[]{:S(2)}) collective-permute-start(f32[8,128]{1,0:T(8,128)S(1)} %shard_map.79.refs_0_), channel_id=1, source_target_pairs={{0,3},{1,2},{2,1},{3,0},{4,7},{5,6},{6,5},{7,4},{8,11},{9,10},{10,... | collective-permute-start | bytes 12296 | tf_op jit(solution)/shard_map/ppermute | solution.py:224
  46.5 3.5 %collective-permute-start.4 = (f32[8,128]{1,0:T(8,128)S(1)}, f32[8,128]{1,0:T(8,128)S(1)}, u32[]{:S(2)}, u32[]{:S(2)}) collective-permute-start(f32[8,128]{1,0:T(8,128)S(1)} %shard_map.79.refs_0_), channel_id=1, source_target_pairs={{0,2},{1,3},{2,0},{3,1},{4,6},{5,7},{6,4},{7,5},{8,10},{9,11},{10,... | collective-permute-start | bytes 12296 | tf_op jit(solution)/shard_map/ppermute | solution.py:224
  47.8 2.3 %collective-permute-start.5 = (f32[8,128]{1,0:T(8,128)S(1)}, f32[8,128]{1,0:T(8,128)S(1)}, u32[]{:S(2)}, u32[]{:S(2)}) collective-permute-start(f32[8,128]{1,0:T(8,128)S(1)} %shard_map.79.refs_0_), channel_id=1, source_target_pairs={{0,1},{1,0},{2,3},{3,2},{4,5},{5,4},{6,7},{7,6},{8,9},{9,8},{10,11... | collective-permute-start | bytes 12296 | tf_op jit(solution)/shard_map/ppermute | solution.py:224

commit v8 on v7

--- a/solution.py
+++ b/solution.py
@@ -16,6 +16,19 @@
 
 f32 = jnp.float32
 bf16 = jnp.bfloat16
+
+
+def group_order():
+    order = []
+    for k in range(16):
+        e, p, q = k & 1, (k >> 1) & 1, k >> 2
+        order.append((p ^ e) * 8 + ((q + 2 * e) & 3) * 2 + e)
+    return order
+
+
+def turn_of(group):
+    z, y, e = group >> 3, (group >> 1) & 3, group & 1
+    return e + (z ^ e) * 2 + ((y - 2 * e) & 3) * 4
 
 
 def iota(shape, dim):
@@ -60,7 +73,8 @@
         server = (jnp.where(near, z, 3 - z) & 1) * 32 + (owner & 31)
         landing = server * 4 + jnp.where(near, slot, slot + 2)
         rows = out_ref.shape[0]
-        asks = jnp.where(landing == iota((rows, LANES), 0), local, jnp.zeros((rows, LANES), f32))
+        place = turn_of(server >> 2) * 16 + (landing & 15)
+        asks = jnp.where(place == iota((rows, LANES), 0), local, jnp.zeros((rows, LANES), f32))
         asks = jnp.sum(asks, axis=1, keepdims=True)
         where = landing.astype(f32)
         turned = pltpu.roll(where, LANES // 2, 1)
@@ -83,13 +97,14 @@
     chosen = (index == iota((rows, 2 * held), 1)).astype(f32).astype(bf16)
     table = jnp.concatenate([mine_ref[...], other_ref[...]], axis=0)
     found = jnp.dot(chosen, table, preferred_element_type=f32).astype(bf16)
-    both = [found[start : start + 16] for start in range(0, rows, 16) for _ in range(2)]
+    starts = [turn_of(chip // 2) * 16 for chip in range(rows // 8)]
+    both = [found[start : start + 16] for start in starts]
     out_ref[...] = jnp.concatenate(both, axis=0)
 
 
 def place_kernel(heads, here_ref, asked_ref, arrived_ref, out_ref):
     core = here_ref[0] & 1
-    start = pl.multiple_of(((here_ref[0] >> 2) & 15) * 16, 16)
+    start = pl.multiple_of(turn_of((here_ref[0] >> 2) & 15) * 16, 16)
     asked = asked_ref[pl.ds(start, 16), :].astype(f32)
     arrived = arrived_ref[...]
     slots = arrived.shape[0]
@@ -141,13 +156,15 @@
     key_power = sums[1:2] / D
     agreement = sums[2:3] * lax.rsqrt(hidden_power + EPSILON) * lax.rsqrt(key_power + EPSILON)
     gate = jax.nn.sigmoid(agreement / math.sqrt(D))
-    gate = jnp.broadcast_to(gate, (LANES, LANES)).T[:, 0:1]
+    gate = jnp.broadcast_to(gate, (LANES, LANES)).T
     rows = LANES // chunks
     copies = []
     for k in range(chunks):
         part = slice(k * rows, (k + 1) * rows)
-        joined = hidden_ref[part, :].astype(f32) + gate[part] * projected_ref[part, :]
-        joined_ref[part, :] = joined.astype(bf16)
+        for column in range(0, joined_ref.shape[1], LANES):
+            lanes = slice(column, column + LANES)
+            joined = hidden_ref[part, lanes].astype(f32) + gate[part] * projected_ref[part, lanes]
+            joined_ref[part, lanes] = joined.astype(bf16)
         copy = pltpu.make_async_copy(joined_ref.at[part, :], out_ref.at[part, :], sems.at[k])
         copy.start()
         copies.append(copy)
@@ -185,15 +202,16 @@
     message = request(1, message)
     halves_of_z = [[half * servers + k for k in range(servers)] for half in range(2)]
     same_core = [[k for k in half if k % 2 == core] for half in halves_of_z for core in range(2)]
+    by_group = [[half[4 * group + k] for group in group_order() for k in range(4)] for half in halves_of_z]
     asked = lax.all_to_all(
-        message.reshape(servers, 4, LANES), BOTH, 0, 0, axis_index_groups=halves_of_z, tiled=True
+        message.reshape(servers, 4, LANES), BOTH, 0, 0, axis_index_groups=by_group, tiled=True
     ).reshape(4 * servers, LANES)
     sent = call(
         gather_kernel,
         shape((8 * servers, row_width), bf16),
         [asked, memory_table, table_there],
         6 * MIB,
-        flops=14_000_000_000,
+        flops=COVER // 2,
     )
     arrived = lax.all_to_all(
         sent.reshape(servers // 2, 16, row_width), BOTH, 0, 0, axis_index_groups=same_core, tiled=True

time: 51.2 us -> 51.2 us (level)
    all_to_all x1, blocking collectives: 17.7 us -> 18.2 us  [local(): lax.all_to_all(sent.reshape(servers // 2, 16, row_width), BOTH, 0, 0, axi...]
    all_to_all x1, blocking collectives: 16.7 us -> 16.1 us  [local(): lax.all_to_all(message.reshape(servers, 4, LANES), BOTH, 0, 0, axis_index...]
where the time goes in v8:
time: 51.2 us; the launch traced here: 51 us
  blocking collectives  34.4 us (67%)
  starting transfers between devices  8.08 us (16%)
  Pallas kernels  7.47 us (15%)
  waiting for transfers between devices  0.75 us (1%)
    all_to_all x1, blocking collectives, local(): lax.all_to_all(sent.reshape(servers // 2, 16, row_width), BOTH, 0, 0, axi...  18.2 us
    all_to_all x1, blocking collectives, local(): lax.all_to_all(message.reshape(servers, 4, LANES), BOTH, 0, 0, axis_index...  16.1 us
    pallas_call x6, Pallas kernels, call(): pl.pallas_call(body, out_shape=out_shape, in_specs=[pl.BlockSpec(memory_s...  5.59 us
    ppermute x1, starting transfers between devices, local(): table_there = lax.ppermute(memory_table, BOTH, swap)  3.71 us
    ppermute x3, starting transfers between devices, local(): lax.ppermute(sums, 'tensor', [(k, k ^ d) for k in range(tensor)])  2.22 us
    ppermute x2, starting transfers between devices, local(): lax.ppermute(mine, 'tensor', [(k, k ^ 1) for k in range(tensor)])  2.14 us
  transfers between devices with their start and end apart: 6, of which 1 were waited for; matrix products, arithmetic and copies ran while one was open for 0% of the time, Pallas kernels for 7%

profile of v8, /device:TPU:1, one launch (start us, length us, event | category | flops | bytes accessed | tf_op | source)
XLA Modules:
  0.0 51.0 jit_solution(4338909658864067913)
XLA Ops:
  0.0 1.0 %shard_map.73.refs_2_ = bf16[256,128]{1,0:T(8,128)(2,1)S(1)} custom-call(s32[1]{0:T(128)} %bitcast.refs_0_, s32[1,128]{1,0:T(1,128)} %bitcast.17), custom_call_target="tpu_custom_call" | custom-call | flops 1 | bytes 1 | tf_op jit(solution)/shard_map/pallas_call | solution.py:188
  1.0 0.0 copy-start.1
  1.0 3.7 %collective-permute-start = (bf16[256,896]{1,0:T(8,128)(2,1)}, bf16[256,896]{1,0:T(8,128)(2,1)S(1)}, u32[]{:S(2)}, u32[]{:S(2)}) collective-permute-start(bf16[256,896]{1,0:T(8,128)(2,1)} %mine_ref), channel_id=1, source_target_pairs={{0,96},{1,97},{2,98},{3,99},{4,100},{5,101},{6,102},{7,103},{8,104... | collective-permute-start | bytes 1376264 | tf_op jit(solution)/shard_map/ppermute | solution.py:201
  4.7 16.1 %all_to_all.10 = bf16[64,4,128]{2,1,0:T(4,128)(2,1)S(1)} all-to-all(bf16[64,4,128]{2,1,0:T(4,128)(2,1)S(1)} %bitcast.16), channel_id=1, replica_groups={{0,1,2,3,52,53,54,55,32,33,34,35,20,21,22,23,8,9,10,11,60,61,62,63,40,4..., dimensions={0} | all-to-all | bytes 131072 | tf_op jit(solution)/shard_map/all_to_all | solution.py:206
  20.8 0.0 collective-permute-done.other_ref
  20.8 0.0 slice-start
  20.8 0.0 slice-start.4
  20.9 0.0 copy-done.1
  20.9 0.0 copy-start.2
  20.9 0.0 copy-start.3
  20.9 0.0 slice-start.1
  20.9 0.0 slice-start.2
  20.9 0.0 slice-start.3
  20.9 0.0 slice-start.5
  20.9 0.0 slice-start.6
  20.9 0.0 slice-start.7
  20.9 0.5 shard_map.75
  21.4 18.2 %all_to_all.11 = bf16[32,16,896]{2,1,0:T(8,128)(2,1)S(1)} all-to-all(bf16[32,16,896]{2,1,0:T(8,128)(2,1)S(1)} %bitcast.12), channel_id=1, replica_groups={{0,2,4,6,8,10,12,14,16,18,20,22,24,26,28,30,32,34,36,38,40,42,44,46,48,..., dimensions={0} | all-to-all | bytes 1835008 | tf_op jit(solution)/shard_map/all_to_all | solution.py:216
  39.7 0.5 %shard_map.77.mine_ref.mine0_ref = bf16[128,1792]{1,0:T(8,128)(2,1)S(1)} custom-call(s32[1]{0:T(128)} %bitcast.refs_0_, bf16[256,128]{1,0:T(8,128)(2,1)S(1)} %bitcast.14, bf16[512,896]{1,0:T(8,128)(2,1)S(1)} %bitcast.10), custom_call_target="tpu_custom_call" | custom-call | tf_op jit(solution)/shard_map/pallas_call | solution.py:44
  40.2 2.0 %collective-permute-start.2 = (bf16[128,1792]{1,0:T(8,128)(2,1)S(1)}, bf16[128,1792]{1,0:T(8,128)(2,1)S(1)}, u32[]{:S(2)}, u32[]{:S(2)}) collective-permute-start(bf16[128,1792]{1,0:T(8,128)(2,1)S(1)} %shard_map.77.mine_ref.mine0_ref), channel_id=1, source_target_pairs={{0,1},{1,0},{2,3},{3,2},{4,5},{5,4},{6,7},{7,6},{8,9},{9,8},{10,11... | collective-permute-start | bytes 1376264 | tf_op jit(solution)/shard_map/ppermute | solution.py:228
  42.3 0.5 %shard_map.76.mine_ref.mine1_ref = bf16[128,1792]{1,0:T(8,128)(2,1)S(1)} custom-call(s32[1]{0:T(128)} %bitcast.refs_0_, bf16[256,128]{1,0:T(8,128)(2,1)S(1)} %bitcast.15, bf16[512,896]{1,0:T(8,128)(2,1)S(1)} %bitcast.11), custom_call_target="tpu_custom_call" | custom-call | tf_op jit(solution)/shard_map/pallas_call | solution.py:44
  42.8 0.1 collective-permute-start.1
  42.9 0.0 copy-done.2
  43.0 0.0 copy-done.3
  43.0 0.0 copy-start
  43.0 0.7 %collective-permute-done.2.other_ref.other0_ref = bf16[128,1792]{1,0:T(8,128)(2,1)S(1)} collective-permute-done((bf16[128,1792]{1,0:T(8,128)(2,1)S(1)}, bf16[128,1792]{1,0:T(8,128)(2,1)S(1)}, u32[]{:S(2)}, u32[]{:S(2)}) %collective-permute-start.2) | collective-permute-done | bytes 458784 | tf_op jit(solution)/shard_map/ppermute | solution.py:228
  43.7 0.0 slice-done
  43.7 0.0 slice-done.4
  43.7 0.0 slice-done.1
  43.7 0.0 slice-done.2
  43.7 0.0 slice-done.3
  43.7 0.0 slice-done.5
  43.8 0.0 slice-done.6
  43.8 0.0 slice-done.7
  43.8 1.0 %shard_map.78.first_ref = f32[128,1792]{1,0:T(8,128)S(1)} custom-call(bf16[128,1792]{1,0:T(8,128)(2,1)S(1)} %shard_map.77.mine_ref.mine0_ref, bf16[128,1792]{1,0:T(8,128)(2,1)S(1)} %collective-permute-done.2.other_ref.other0_ref, bf16[3584,1792]{1,0:T(8,128)(2,1)S(1)} %bitcast.7, bf16[3584,1792]{1,0:T(8,128)(2,1)S(1)} %bitcast.9), custom_call_target="tpu_custom_call" | custom-call | flops 822083584 | tf_op jit(solution)/shard_map/pallas_call | solution.py:44
  44.8 0.0 collective-permute-done.1.other_ref.other1_ref
  44.8 0.0 copy-done
  44.8 1.1 %shard_map.79.refs_0_ = f32[8,128]{1,0:T(8,128)S(1)} custom-call(bf16[128,1792]{1,0:T(8,128)(2,1)S(1)} %shard_map.76.mine_ref.mine1_ref, bf16[128,1792]{1,0:T(8,128)(2,1)S(1)} %collective-permute-done.1.other_ref.other1_ref, bf16[3584,1792]{1,0:T(8,128)(2,1)S(1)} %bitcast.7, f32[128,1792]{1,0:T(8,128)S(1)} %shard_map.78.first_ref, ...), custom_call_target="tpu_custom_call" | custom-call | flops 822083584 | tf_op jit(solution)/shard_map/pallas_call | solution.py:44
  46.0 0.5 %collective-permute-start.3 = (f32[8,128]{1,0:T(8,128)S(1)}, f32[8,128]{1,0:T(8,128)S(1)}, u32[]{:S(2)}, u32[]{:S(2)}) collective-permute-start(f32[8,128]{1,0:T(8,128)S(1)} %shard_map.79.refs_0_), channel_id=1, source_target_pairs={{0,3},{1,2},{2,1},{3,0},{4,7},{5,6},{6,5},{7,4},{8,11},{9,10},{10,... | collective-permute-start | bytes 12296 | tf_op jit(solution)/shard_map/ppermute | solution.py:242
  46.5 1.3 %collective-permute-start.4 = (f32[8,128]{1,0:T(8,128)S(1)}, f32[8,128]{1,0:T(8,128)S(1)}, u32[]{:S(2)}, u32[]{:S(2)}) collective-permute-start(f32[8,128]{1,0:T(8,128)S(1)} %shard_map.79.refs_0_), channel_id=1, source_target_pairs={{0,2},{1,3},{2,0},{3,1},{4,6},{5,7},{6,4},{7,5},{8,10},{9,11},{10,... | collective-permute-start | bytes 12296 | tf_op jit(solution)/shard_map/ppermute | solution.py:242
  47.8 0.4 collective-permute-start.5
  48.2 1.8 %shard_map.80.refs_5_ = f32[128,1792]{1,0:T(8,128)S(1)} custom-call(bf16[128,1792]{1,0:T(8,128)(2,1)S(1)} %shard_map.77.mine_ref.mine0_ref, bf16[128,1792]{1,0:T(8,128)(2,1)S(1)} %collective-permute-done.2.other_ref.other0_ref, bf16[128,1792]{1,0:T(8,128)(2,1)S(1)} %shard_map.76.mine_ref.mine1_ref, ...), custom_call_target="tpu_custom_call" | custom-call | flops 1644167168 | tf_op jit(solution)/shard_map/pallas_call | solution.py:44
  50.1 0.0 collective-permute-done.3.refs_1_
  50.1 0.0 collective-permute-done.4.refs_2_
  50.1 0.0 collective-permute-done.5.refs_3_
  50.1 0.9 %shard_map.81 = bf16[128,1792]{1,0:T(8,128)(2,1)} custom-call(f32[8,128]{1,0:T(8,128)S(1)} %shard_map.79.refs_0_, f32[8,128]{1,0:T(8,128)S(1)} %collective-permute-done.3.refs_1_, f32[8,128]{1,0:T(8,128)S(1)} %collective-permute-done.4.refs_2_, f32[8,128]{1,0:T(8,128)S(1)} %collective-permute-done.5.refs_3_, bf16[128,1792]{1,0:T(8,128)(2,1)S(1)} %copy-done, ...), custom_call_target="tpu_custom_call" | custom-call | tf_op jit(solution)/shard_map/pallas_call | solution.py:245
  (5 shorter events, 0.0 us)
Async XLA Ops:
  1.0 19.9 %copy-start.1 = (bf16[256,896]{1,0:T(8,128)(2,1)S(1)}, bf16[256,896]{1,0:T(8,128)(2,1)}, u32[]{:S(2)}) copy-start(bf16[256,896]{1,0:T(8,128)(2,1)} %mine_ref) | copy-start | bytes 1376260
  1.0 19.9 %collective-permute-start = (bf16[256,896]{1,0:T(8,128)(2,1)}, bf16[256,896]{1,0:T(8,128)(2,1)S(1)}, u32[]{:S(2)}, u32[]{:S(2)}) collective-permute-start(bf16[256,896]{1,0:T(8,128)(2,1)} %mine_ref), channel_id=1, source_target_pairs={{0,96},{1,97},{2,98},{3,99},{4,100},{5,101},{6,102},{7,103},{8,104... | collective-permute-start | bytes 1376264 | tf_op jit(solution)/shard_map/ppermute | solution.py:201
  20.8 22.9 %slice-start = ((s8[12845056]{0:T(1024)(128)(4,1)}), s8[4194304]{0:T(1024)(128)(4,1)S(1)}, s32[]{:S(2)}) async-start(s8[12845056]{0:T(1024)(128)(4,1)} %bitcast.6), calls=%async_computation.2 | async-start | bytes 8388608
  20.8 22.9 %slice-start.4 = ((s8[12845056]{0:T(1024)(128)(4,1)}), s8[4194304]{0:T(1024)(128)(4,1)S(1)}, s32[]{:S(2)}) async-start(s8[12845056]{0:T(1024)(128)(4,1)} %bitcast.8), calls=%async_computation.6 | async-start | bytes 8388608
  20.9 22.1 %copy-start.2 = (f32[1792]{0:T(1024)S(1)}, f32[1792]{0:T(1024)}, u32[]{:S(2)}) copy-start(f32[1792]{0:T(1024)} %param.12) | copy-start | bytes 21508
  20.9 22.1 %copy-start.3 = (f32[1792]{0:T(1024)S(1)}, f32[1792]{0:T(1024)}, u32[]{:S(2)}) copy-start(f32[1792]{0:T(1024)} %param.13) | copy-start | bytes 21508
  20.9 22.8 %slice-start.1 = ((s8[12845056]{0:T(1024)(128)(4,1)}), s8[4194304]{0:T(1024)(128)(4,1)S(1)}, s32[]{:S(2)}) async-start(s8[12845056]{0:T(1024)(128)(4,1)} %bitcast.6), calls=%async_computation.3 | async-start | bytes 8388608
  20.9 22.8 %slice-start.2 = ((s8[12845056]{0:T(1024)(128)(4,1)}), s8[4194304]{0:T(1024)(128)(4,1)S(1)}, s32[]{:S(2)}) async-start(s8[12845056]{0:T(1024)(128)(4,1)} %bitcast.6), calls=%async_computation.4 | async-start | bytes 8388608
  20.9 22.8 %slice-start.3 = ((s8[12845056]{0:T(1024)(128)(4,1)}), s8[262144]{0:T(1024)(128)(4,1)S(1)}, s32[]{:S(2)}) async-start(s8[12845056]{0:T(1024)(128)(4,1)} %bitcast.6), calls=%async_computation.5 | async-start | bytes 524288
  20.9 22.8 %slice-start.5 = ((s8[12845056]{0:T(1024)(128)(4,1)}), s8[4194304]{0:T(1024)(128)(4,1)S(1)}, s32[]{:S(2)}) async-start(s8[12845056]{0:T(1024)(128)(4,1)} %bitcast.8), calls=%async_computation.7 | async-start | bytes 8388608
  20.9 22.8 %slice-start.6 = ((s8[12845056]{0:T(1024)(128)(4,1)}), s8[4194304]{0:T(1024)(128)(4,1)S(1)}, s32[]{:S(2)}) async-start(s8[12845056]{0:T(1024)(128)(4,1)} %bitcast.8), calls=%async_computation.8 | async-start | bytes 8388608
  20.9 22.8 %slice-start.7 = ((s8[12845056]{0:T(1024)(128)(4,1)}), s8[262144]{0:T(1024)(128)(4,1)S(1)}, s32[]{:S(2)}) async-start(s8[12845056]{0:T(1024)(128)(4,1)} %bitcast.8), calls=%async_computation.9 | async-start | bytes 524288
  40.2 3.5 %collective-permute-start.2 = (bf16[128,1792]{1,0:T(8,128)(2,1)S(1)}, bf16[128,1792]{1,0:T(8,128)(2,1)S(1)}, u32[]{:S(2)}, u32[]{:S(2)}) collective-permute-start(bf16[128,1792]{1,0:T(8,128)(2,1)S(1)} %shard_map.77.mine_ref.mine0_ref), channel_id=1, source_target_pairs={{0,1},{1,0},{2,3},{3,2},{4,5},{5,4},{6,7},{7,6},{8,9},{9,8},{10,11... | collective-permute-start | bytes 1376264 | tf_op jit(solution)/shard_map/ppermute | solution.py:228
  42.8 2.0 %collective-permute-start.1 = (bf16[128,1792]{1,0:T(8,128)(2,1)S(1)}, bf16[128,1792]{1,0:T(8,128)(2,1)S(1)}, u32[]{:S(2)}, u32[]{:S(2)}) collective-permute-start(bf16[128,1792]{1,0:T(8,128)(2,1)S(1)} %shard_map.76.mine_ref.mine1_ref), channel_id=1, source_target_pairs={{0,1},{1,0},{2,3},{3,2},{4,5},{5,4},{6,7},{7,6},{8,9},{9,8},{10,11... | collective-permute-start | bytes 1376264 | tf_op jit(solution)/shard_map/ppermute | solution.py:228
  43.0 1.9 %copy-start = (bf16[128,1792]{1,0:T(8,128)(2,1)S(1)}, bf16[128,1792]{1,0:T(8,128)(2,1)}, u32[]{:S(2)}) copy-start(bf16[128,1792]{1,0:T(8,128)(2,1)} %refs_4_.1) | copy-start | bytes 1376260
  46.0 4.1 %collective-permute-start.3 = (f32[8,128]{1,0:T(8,128)S(1)}, f32[8,128]{1,0:T(8,128)S(1)}, u32[]{:S(2)}, u32[]{:S(2)}) collective-permute-start(f32[8,128]{1,0:T(8,128)S(1)} %shard_map.79.refs_0_), channel_id=1, source_target_pairs={{0,3},{1,2},{2,1},{3,0},{4,7},{5,6},{6,5},{7,4},{8,11},{9,10},{10,... | collective-permute-start | bytes 12296 | tf_op jit(solution)/shard_map/ppermute | solution.py:242
  46.5 3.5 %collective-permute-start.4 = (f32[8,128]{1,0:T(8,128)S(1)}, f32[8,128]{1,0:T(8,128)S(1)}, u32[]{:S(2)}, u32[]{:S(2)}) collective-permute-start(f32[8,128]{1,0:T(8,128)S(1)} %shard_map.79.refs_0_), channel_id=1, source_target_pairs={{0,2},{1,3},{2,0},{3,1},{4,6},{5,7},{6,4},{7,5},{8,10},{9,11},{10,... | collective-permute-start | bytes 12296 | tf_op jit(solution)/shard_map/ppermute | solution.py:242
  47.8 2.3 %collective-permute-start.5 = (f32[8,128]{1,0:T(8,128)S(1)}, f32[8,128]{1,0:T(8,128)S(1)}, u32[]{:S(2)}, u32[]{:S(2)}) collective-permute-start(f32[8,128]{1,0:T(8,128)S(1)} %shard_map.79.refs_0_), channel_id=1, source_target_pairs={{0,1},{1,0},{2,3},{3,2},{4,5},{5,4},{6,7},{7,6},{8,9},{9,8},{10,11... | collective-permute-start | bytes 12296 | tf_op jit(solution)/shard_map/ppermute | solution.py:242

commit v9 on v8

--- a/solution.py
+++ b/solution.py
@@ -239,7 +239,7 @@
         6 * MIB,
         flops=work,
     )
-    others = [lax.ppermute(sums, "tensor", [(k, k ^ d) for k in range(tensor)]) for d in (3, 2, 1)]
+    others = [lax.ppermute(sums, "tensor", [(k, k ^ d) for k in range(tensor)]) for d in (2, 3, 1)]
     projected = call(value_kernel, partial, [*halves[0], *halves[1], value_weight], 6 * MIB, flops=2 * work)
     chunks = 4
     return pl.pallas_call(

time: 51.2 us -> 51 us (level)
  no operation moved by 1% of the time
where the time goes in v9:
time: 51 us; the launch traced here: 50.9 us
  blocking collectives  34.4 us (67%)
  starting transfers between devices  7.95 us (16%)
  Pallas kernels  7.47 us (15%)
  waiting for transfers between devices  0.75 us (1%)
    all_to_all x1, blocking collectives, local(): lax.all_to_all(sent.reshape(servers // 2, 16, row_width), BOTH, 0, 0, axi...  18.2 us
    all_to_all x1, blocking collectives, local(): lax.all_to_all(message.reshape(servers, 4, LANES), BOTH, 0, 0, axis_index...  16.1 us
    pallas_call x6, Pallas kernels, call(): pl.pallas_call(body, out_shape=out_shape, in_specs=[pl.BlockSpec(memory_s...  5.59 us
    ppermute x1, starting transfers between devices, local(): table_there = lax.ppermute(memory_table, BOTH, swap)  3.71 us
    ppermute x2, starting transfers between devices, local(): lax.ppermute(mine, 'tensor', [(k, k ^ 1) for k in range(tensor)])  2.14 us
    ppermute x3, starting transfers between devices, local(): lax.ppermute(sums, 'tensor', [(k, k ^ d) for k in range(tensor)])  2.09 us
  transfers between devices with their start and end apart: 6, of which 1 were waited for; matrix products, arithmetic and copies ran while one was open for 0% of the time, Pallas kernels for 7%

profile of v9, /device:TPU:1, one launch (start us, length us, event | category | flops | bytes accessed | tf_op | source)
XLA Modules:
  0.0 50.9 jit_solution(3603004366422455399)
XLA Ops:
  0.0 1.0 %shard_map.73.refs_2_ = bf16[256,128]{1,0:T(8,128)(2,1)S(1)} custom-call(s32[1]{0:T(128)} %bitcast.refs_0_, s32[1,128]{1,0:T(1,128)} %bitcast.17), custom_call_target="tpu_custom_call" | custom-call | flops 1 | bytes 1 | tf_op jit(solution)/shard_map/pallas_call | solution.py:188
  1.0 0.0 copy-start.1
  1.0 3.7 %collective-permute-start = (bf16[256,896]{1,0:T(8,128)(2,1)}, bf16[256,896]{1,0:T(8,128)(2,1)S(1)}, u32[]{:S(2)}, u32[]{:S(2)}) collective-permute-start(bf16[256,896]{1,0:T(8,128)(2,1)} %mine_ref), channel_id=1, source_target_pairs={{0,96},{1,97},{2,98},{3,99},{4,100},{5,101},{6,102},{7,103},{8,104... | collective-permute-start | bytes 1376264 | tf_op jit(solution)/shard_map/ppermute | solution.py:201
  4.7 16.1 %all_to_all.10 = bf16[64,4,128]{2,1,0:T(4,128)(2,1)S(1)} all-to-all(bf16[64,4,128]{2,1,0:T(4,128)(2,1)S(1)} %bitcast.16), channel_id=1, replica_groups={{0,1,2,3,52,53,54,55,32,33,34,35,20,21,22,23,8,9,10,11,60,61,62,63,40,4..., dimensions={0} | all-to-all | bytes 131072 | tf_op jit(solution)/shard_map/all_to_all | solution.py:206
  20.8 0.0 collective-permute-done.other_ref
  20.8 0.0 slice-start
  20.8 0.0 slice-start.4
  20.9 0.0 copy-done.1
  20.9 0.0 copy-start.2
  20.9 0.0 copy-start.3
  20.9 0.0 slice-start.1
  20.9 0.0 slice-start.2
  20.9 0.0 slice-start.3
  20.9 0.0 slice-start.5
  20.9 0.0 slice-start.6
  20.9 0.0 slice-start.7
  20.9 0.5 shard_map.75
  21.4 18.2 %all_to_all.11 = bf16[32,16,896]{2,1,0:T(8,128)(2,1)S(1)} all-to-all(bf16[32,16,896]{2,1,0:T(8,128)(2,1)S(1)} %bitcast.12), channel_id=1, replica_groups={{0,2,4,6,8,10,12,14,16,18,20,22,24,26,28,30,32,34,36,38,40,42,44,46,48,..., dimensions={0} | all-to-all | bytes 1835008 | tf_op jit(solution)/shard_map/all_to_all | solution.py:216
  39.7 0.5 %shard_map.77.mine_ref.mine0_ref = bf16[128,1792]{1,0:T(8,128)(2,1)S(1)} custom-call(s32[1]{0:T(128)} %bitcast.refs_0_, bf16[256,128]{1,0:T(8,128)(2,1)S(1)} %bitcast.14, bf16[512,896]{1,0:T(8,128)(2,1)S(1)} %bitcast.10), custom_call_target="tpu_custom_call" | custom-call | tf_op jit(solution)/shard_map/pallas_call | solution.py:44
  40.2 2.0 %collective-permute-start.2 = (bf16[128,1792]{1,0:T(8,128)(2,1)S(1)}, bf16[128,1792]{1,0:T(8,128)(2,1)S(1)}, u32[]{:S(2)}, u32[]{:S(2)}) collective-permute-start(bf16[128,1792]{1,0:T(8,128)(2,1)S(1)} %shard_map.77.mine_ref.mine0_ref), channel_id=1, source_target_pairs={{0,1},{1,0},{2,3},{3,2},{4,5},{5,4},{6,7},{7,6},{8,9},{9,8},{10,11... | collective-permute-start | bytes 1376264 | tf_op jit(solution)/shard_map/ppermute | solution.py:228
  42.3 0.5 %shard_map.76.mine_ref.mine1_ref = bf16[128,1792]{1,0:T(8,128)(2,1)S(1)} custom-call(s32[1]{0:T(128)} %bitcast.refs_0_, bf16[256,128]{1,0:T(8,128)(2,1)S(1)} %bitcast.15, bf16[512,896]{1,0:T(8,128)(2,1)S(1)} %bitcast.11), custom_call_target="tpu_custom_call" | custom-call | tf_op jit(solution)/shard_map/pallas_call | solution.py:44
  42.8 0.1 collective-permute-start.1
  42.9 0.0 copy-done.2
  43.0 0.0 copy-done.3
  43.0 0.0 copy-start
  43.0 0.7 %collective-permute-done.2.other_ref.other0_ref = bf16[128,1792]{1,0:T(8,128)(2,1)S(1)} collective-permute-done((bf16[128,1792]{1,0:T(8,128)(2,1)S(1)}, bf16[128,1792]{1,0:T(8,128)(2,1)S(1)}, u32[]{:S(2)}, u32[]{:S(2)}) %collective-permute-start.2) | collective-permute-done | bytes 458784 | tf_op jit(solution)/shard_map/ppermute | solution.py:228
  43.7 0.0 slice-done
  43.7 0.0 slice-done.4
  43.7 0.0 slice-done.1
  43.7 0.0 slice-done.2
  43.7 0.0 slice-done.3
  43.7 0.0 slice-done.5
  43.8 0.0 slice-done.6
  43.8 0.0 slice-done.7
  43.8 1.0 %shard_map.78.first_ref = f32[128,1792]{1,0:T(8,128)S(1)} custom-call(bf16[128,1792]{1,0:T(8,128)(2,1)S(1)} %shard_map.77.mine_ref.mine0_ref, bf16[128,1792]{1,0:T(8,128)(2,1)S(1)} %collective-permute-done.2.other_ref.other0_ref, bf16[3584,1792]{1,0:T(8,128)(2,1)S(1)} %bitcast.7, bf16[3584,1792]{1,0:T(8,128)(2,1)S(1)} %bitcast.9), custom_call_target="tpu_custom_call" | custom-call | flops 822083584 | tf_op jit(solution)/shard_map/pallas_call | solution.py:44
  44.8 0.0 collective-permute-done.1.other_ref.other1_ref
  44.8 0.0 copy-done
  44.8 1.1 %shard_map.79.refs_0_ = f32[8,128]{1,0:T(8,128)S(1)} custom-call(bf16[128,1792]{1,0:T(8,128)(2,1)S(1)} %shard_map.76.mine_ref.mine1_ref, bf16[128,1792]{1,0:T(8,128)(2,1)S(1)} %collective-permute-done.1.other_ref.other1_ref, bf16[3584,1792]{1,0:T(8,128)(2,1)S(1)} %bitcast.7, f32[128,1792]{1,0:T(8,128)S(1)} %shard_map.78.first_ref, ...), custom_call_target="tpu_custom_call" | custom-call | flops 822083584 | tf_op jit(solution)/shard_map/pallas_call | solution.py:44
  46.0 0.3 collective-permute-start.3
  46.3 1.8 %collective-permute-start.4 = (f32[8,128]{1,0:T(8,128)S(1)}, f32[8,128]{1,0:T(8,128)S(1)}, u32[]{:S(2)}, u32[]{:S(2)}) collective-permute-start(f32[8,128]{1,0:T(8,128)S(1)} %shard_map.79.refs_0_), channel_id=1, source_target_pairs={{0,3},{1,2},{2,1},{3,0},{4,7},{5,6},{6,5},{7,4},{8,11},{9,10},{10,... | collective-permute-start | bytes 12296 | tf_op jit(solution)/shard_map/ppermute | solution.py:242
  48.1 0.0 collective-permute-start.5
  48.1 1.8 %shard_map.80.refs_5_ = f32[128,1792]{1,0:T(8,128)S(1)} custom-call(bf16[128,1792]{1,0:T(8,128)(2,1)S(1)} %shard_map.77.mine_ref.mine0_ref, bf16[128,1792]{1,0:T(8,128)(2,1)S(1)} %collective-permute-done.2.other_ref.other0_ref, bf16[128,1792]{1,0:T(8,128)(2,1)S(1)} %shard_map.76.mine_ref.mine1_ref, ...), custom_call_target="tpu_custom_call" | custom-call | flops 1644167168 | tf_op jit(solution)/shard_map/pallas_call | solution.py:44
  49.9 0.0 collective-permute-done.3.refs_1_
  50.0 0.0 collective-permute-done.4.refs_2_
  50.0 0.0 collective-permute-done.5.refs_3_
  50.0 0.9 %shard_map.81 = bf16[128,1792]{1,0:T(8,128)(2,1)} custom-call(f32[8,128]{1,0:T(8,128)S(1)} %shard_map.79.refs_0_, f32[8,128]{1,0:T(8,128)S(1)} %collective-permute-done.3.refs_1_, f32[8,128]{1,0:T(8,128)S(1)} %collective-permute-done.4.refs_2_, f32[8,128]{1,0:T(8,128)S(1)} %collective-permute-done.5.refs_3_, bf16[128,1792]{1,0:T(8,128)(2,1)S(1)} %copy-done, ...), custom_call_target="tpu_custom_call" | custom-call | tf_op jit(solution)/shard_map/pallas_call | solution.py:245
  (5 shorter events, 0.0 us)
Async XLA Ops:
  1.0 19.9 %copy-start.1 = (bf16[256,896]{1,0:T(8,128)(2,1)S(1)}, bf16[256,896]{1,0:T(8,128)(2,1)}, u32[]{:S(2)}) copy-start(bf16[256,896]{1,0:T(8,128)(2,1)} %mine_ref) | copy-start | bytes 1376260
  1.0 19.9 %collective-permute-start = (bf16[256,896]{1,0:T(8,128)(2,1)}, bf16[256,896]{1,0:T(8,128)(2,1)S(1)}, u32[]{:S(2)}, u32[]{:S(2)}) collective-permute-start(bf16[256,896]{1,0:T(8,128)(2,1)} %mine_ref), channel_id=1, source_target_pairs={{0,96},{1,97},{2,98},{3,99},{4,100},{5,101},{6,102},{7,103},{8,104... | collective-permute-start | bytes 1376264 | tf_op jit(solution)/shard_map/ppermute | solution.py:201
  20.8 22.9 %slice-start = ((s8[12845056]{0:T(1024)(128)(4,1)}), s8[4194304]{0:T(1024)(128)(4,1)S(1)}, s32[]{:S(2)}) async-start(s8[12845056]{0:T(1024)(128)(4,1)} %bitcast.6), calls=%async_computation.2 | async-start | bytes 8388608
  20.8 22.9 %slice-start.4 = ((s8[12845056]{0:T(1024)(128)(4,1)}), s8[4194304]{0:T(1024)(128)(4,1)S(1)}, s32[]{:S(2)}) async-start(s8[12845056]{0:T(1024)(128)(4,1)} %bitcast.8), calls=%async_computation.6 | async-start | bytes 8388608
  20.9 22.1 %copy-start.2 = (f32[1792]{0:T(1024)S(1)}, f32[1792]{0:T(1024)}, u32[]{:S(2)}) copy-start(f32[1792]{0:T(1024)} %param.12) | copy-start | bytes 21508
  20.9 22.1 %copy-start.3 = (f32[1792]{0:T(1024)S(1)}, f32[1792]{0:T(1024)}, u32[]{:S(2)}) copy-start(f32[1792]{0:T(1024)} %param.13) | copy-start | bytes 21508
  20.9 22.8 %slice-start.1 = ((s8[12845056]{0:T(1024)(128)(4,1)}), s8[4194304]{0:T(1024)(128)(4,1)S(1)}, s32[]{:S(2)}) async-start(s8[12845056]{0:T(1024)(128)(4,1)} %bitcast.6), calls=%async_computation.3 | async-start | bytes 8388608
  20.9 22.8 %slice-start.2 = ((s8[12845056]{0:T(1024)(128)(4,1)}), s8[4194304]{0:T(1024)(128)(4,1)S(1)}, s32[]{:S(2)}) async-start(s8[12845056]{0:T(1024)(128)(4,1)} %bitcast.6), calls=%async_computation.4 | async-start | bytes 8388608
  20.9 22.8 %slice-start.3 = ((s8[12845056]{0:T(1024)(128)(4,1)}), s8[262144]{0:T(1024)(128)(4,1)S(1)}, s32[]{:S(2)}) async-start(s8[12845056]{0:T(1024)(128)(4,1)} %bitcast.6), calls=%async_computation.5 | async-start | bytes 524288
  20.9 22.8 %slice-start.5 = ((s8[12845056]{0:T(1024)(128)(4,1)}), s8[4194304]{0:T(1024)(128)(4,1)S(1)}, s32[]{:S(2)}) async-start(s8[12845056]{0:T(1024)(128)(4,1)} %bitcast.8), calls=%async_computation.7 | async-start | bytes 8388608
  20.9 22.8 %slice-start.6 = ((s8[12845056]{0:T(1024)(128)(4,1)}), s8[4194304]{0:T(1024)(128)(4,1)S(1)}, s32[]{:S(2)}) async-start(s8[12845056]{0:T(1024)(128)(4,1)} %bitcast.8), calls=%async_computation.8 | async-start | bytes 8388608
  20.9 22.8 %slice-start.7 = ((s8[12845056]{0:T(1024)(128)(4,1)}), s8[262144]{0:T(1024)(128)(4,1)S(1)}, s32[]{:S(2)}) async-start(s8[12845056]{0:T(1024)(128)(4,1)} %bitcast.8), calls=%async_computation.9 | async-start | bytes 524288
  40.2 3.5 %collective-permute-start.2 = (bf16[128,1792]{1,0:T(8,128)(2,1)S(1)}, bf16[128,1792]{1,0:T(8,128)(2,1)S(1)}, u32[]{:S(2)}, u32[]{:S(2)}) collective-permute-start(bf16[128,1792]{1,0:T(8,128)(2,1)S(1)} %shard_map.77.mine_ref.mine0_ref), channel_id=1, source_target_pairs={{0,1},{1,0},{2,3},{3,2},{4,5},{5,4},{6,7},{7,6},{8,9},{9,8},{10,11... | collective-permute-start | bytes 1376264 | tf_op jit(solution)/shard_map/ppermute | solution.py:228
  42.8 2.0 %collective-permute-start.1 = (bf16[128,1792]{1,0:T(8,128)(2,1)S(1)}, bf16[128,1792]{1,0:T(8,128)(2,1)S(1)}, u32[]{:S(2)}, u32[]{:S(2)}) collective-permute-start(bf16[128,1792]{1,0:T(8,128)(2,1)S(1)} %shard_map.76.mine_ref.mine1_ref), channel_id=1, source_target_pairs={{0,1},{1,0},{2,3},{3,2},{4,5},{5,4},{6,7},{7,6},{8,9},{9,8},{10,11... | collective-permute-start | bytes 1376264 | tf_op jit(solution)/shard_map/ppermute | solution.py:228
  43.0 1.9 %copy-start = (bf16[128,1792]{1,0:T(8,128)(2,1)S(1)}, bf16[128,1792]{1,0:T(8,128)(2,1)}, u32[]{:S(2)}) copy-start(bf16[128,1792]{1,0:T(8,128)(2,1)} %refs_4_.1) | copy-start | bytes 1376260
  46.0 4.0 %collective-permute-start.3 = (f32[8,128]{1,0:T(8,128)S(1)}, f32[8,128]{1,0:T(8,128)S(1)}, u32[]{:S(2)}, u32[]{:S(2)}) collective-permute-start(f32[8,128]{1,0:T(8,128)S(1)} %shard_map.79.refs_0_), channel_id=1, source_target_pairs={{0,2},{1,3},{2,0},{3,1},{4,6},{5,7},{6,4},{7,5},{8,10},{9,11},{10,... | collective-permute-start | bytes 12296 | tf_op jit(solution)/shard_map/ppermute | solution.py:242
  46.3 3.7 %collective-permute-start.4 = (f32[8,128]{1,0:T(8,128)S(1)}, f32[8,128]{1,0:T(8,128)S(1)}, u32[]{:S(2)}, u32[]{:S(2)}) collective-permute-start(f32[8,128]{1,0:T(8,128)S(1)} %shard_map.79.refs_0_), channel_id=1, source_target_pairs={{0,3},{1,2},{2,1},{3,0},{4,7},{5,6},{6,5},{7,4},{8,11},{9,10},{10,... | collective-permute-start | bytes 12296 | tf_op jit(solution)/shard_map/ppermute | solution.py:242
  48.1 1.9 %collective-permute-start.5 = (f32[8,128]{1,0:T(8,128)S(1)}, f32[8,128]{1,0:T(8,128)S(1)}, u32[]{:S(2)}, u32[]{:S(2)}) collective-permute-start(f32[8,128]{1,0:T(8,128)S(1)} %shard_map.79.refs_0_), channel_id=1, source_target_pairs={{0,1},{1,0},{2,3},{3,2},{4,5},{5,4},{6,7},{7,6},{8,9},{9,8},{10,11... | collective-permute-start | bytes 12296 | tf_op jit(solution)/shard_map/ppermute | solution.py:242

commit v10 on v9

--- a/solution.py
+++ b/solution.py
@@ -241,7 +241,7 @@
     )
     others = [lax.ppermute(sums, "tensor", [(k, k ^ d) for k in range(tensor)]) for d in (2, 3, 1)]
     projected = call(value_kernel, partial, [*halves[0], *halves[1], value_weight], 6 * MIB, flops=2 * work)
-    chunks = 4
+    chunks = 2
     return pl.pallas_call(
         lambda *refs: join_kernel(chunks, *refs),
         out_shape=shape(hidden.shape, bf16),

time: 51 us -> 51.1 us (level)
  no operation moved by 1% of the time
where the time goes in v10:
time: 51.1 us; the launch traced here: 50.9 us
  blocking collectives  34.4 us (67%)
  starting transfers between devices  7.95 us (16%)
  Pallas kernels  7.49 us (15%)
  waiting for transfers between devices  0.75 us (1%)
    all_to_all x1, blocking collectives, local(): lax.all_to_all(sent.reshape(servers // 2, 16, row_width), BOTH, 0, 0, axi...  18.2 us
    all_to_all x1, blocking collectives, local(): lax.all_to_all(message.reshape(servers, 4, LANES), BOTH, 0, 0, axis_index...  16.1 us
    pallas_call x6, Pallas kernels, call(): pl.pallas_call(body, out_shape=out_shape, in_specs=[pl.BlockSpec(memory_s...  5.59 us
    ppermute x1, starting transfers between devices, local(): table_there = lax.ppermute(memory_table, BOTH, swap)  3.71 us
    ppermute x2, starting transfers between devices, local(): lax.ppermute(mine, 'tensor', [(k, k ^ 1) for k in range(tensor)])  2.14 us
    ppermute x3, starting transfers between devices, local(): lax.ppermute(sums, 'tensor', [(k, k ^ d) for k in range(tensor)])  2.09 us
  transfers between devices with their start and end apart: 6, of which 1 were waited for; matrix products, arithmetic and copies ran while one was open for 0% of the time, Pallas kernels for 7%

profile of v10, /device:TPU:1, one launch (start us, length us, event | category | flops | bytes accessed | tf_op | source)
XLA Modules:
  0.0 50.9 jit_solution(15738441153056773578)
XLA Ops:
  0.0 1.0 %shard_map.73.refs_2_ = bf16[256,128]{1,0:T(8,128)(2,1)S(1)} custom-call(s32[1]{0:T(128)} %bitcast.refs_0_, s32[1,128]{1,0:T(1,128)} %bitcast.17), custom_call_target="tpu_custom_call" | custom-call | flops 1 | bytes 1 | tf_op jit(solution)/shard_map/pallas_call | solution.py:188
  1.0 0.0 copy-start.1
  1.0 3.7 %collective-permute-start = (bf16[256,896]{1,0:T(8,128)(2,1)}, bf16[256,896]{1,0:T(8,128)(2,1)S(1)}, u32[]{:S(2)}, u32[]{:S(2)}) collective-permute-start(bf16[256,896]{1,0:T(8,128)(2,1)} %mine_ref), channel_id=1, source_target_pairs={{0,96},{1,97},{2,98},{3,99},{4,100},{5,101},{6,102},{7,103},{8,104... | collective-permute-start | bytes 1376264 | tf_op jit(solution)/shard_map/ppermute | solution.py:201
  4.7 16.1 %all_to_all.10 = bf16[64,4,128]{2,1,0:T(4,128)(2,1)S(1)} all-to-all(bf16[64,4,128]{2,1,0:T(4,128)(2,1)S(1)} %bitcast.16), channel_id=1, replica_groups={{0,1,2,3,52,53,54,55,32,33,34,35,20,21,22,23,8,9,10,11,60,61,62,63,40,4..., dimensions={0} | all-to-all | bytes 131072 | tf_op jit(solution)/shard_map/all_to_all | solution.py:206
  20.8 0.0 collective-permute-done.other_ref
  20.8 0.0 slice-start
  20.8 0.0 slice-start.4
  20.9 0.0 copy-done.1
  20.9 0.0 copy-start.2
  20.9 0.0 copy-start.3
  20.9 0.0 slice-start.1
  20.9 0.0 slice-start.2
  20.9 0.0 slice-start.3
  20.9 0.0 slice-start.5
  20.9 0.0 slice-start.6
  20.9 0.0 slice-start.7
  20.9 0.5 shard_map.75
  21.4 18.2 %all_to_all.11 = bf16[32,16,896]{2,1,0:T(8,128)(2,1)S(1)} all-to-all(bf16[32,16,896]{2,1,0:T(8,128)(2,1)S(1)} %bitcast.12), channel_id=1, replica_groups={{0,2,4,6,8,10,12,14,16,18,20,22,24,26,28,30,32,34,36,38,40,42,44,46,48,..., dimensions={0} | all-to-all | bytes 1835008 | tf_op jit(solution)/shard_map/all_to_all | solution.py:216
  39.7 0.5 %shard_map.77.mine_ref.mine0_ref = bf16[128,1792]{1,0:T(8,128)(2,1)S(1)} custom-call(s32[1]{0:T(128)} %bitcast.refs_0_, bf16[256,128]{1,0:T(8,128)(2,1)S(1)} %bitcast.14, bf16[512,896]{1,0:T(8,128)(2,1)S(1)} %bitcast.10), custom_call_target="tpu_custom_call" | custom-call | tf_op jit(solution)/shard_map/pallas_call | solution.py:44
  40.2 2.0 %collective-permute-start.2 = (bf16[128,1792]{1,0:T(8,128)(2,1)S(1)}, bf16[128,1792]{1,0:T(8,128)(2,1)S(1)}, u32[]{:S(2)}, u32[]{:S(2)}) collective-permute-start(bf16[128,1792]{1,0:T(8,128)(2,1)S(1)} %shard_map.77.mine_ref.mine0_ref), channel_id=1, source_target_pairs={{0,1},{1,0},{2,3},{3,2},{4,5},{5,4},{6,7},{7,6},{8,9},{9,8},{10,11... | collective-permute-start | bytes 1376264 | tf_op jit(solution)/shard_map/ppermute | solution.py:228
  42.3 0.5 %shard_map.76.mine_ref.mine1_ref = bf16[128,1792]{1,0:T(8,128)(2,1)S(1)} custom-call(s32[1]{0:T(128)} %bitcast.refs_0_, bf16[256,128]{1,0:T(8,128)(2,1)S(1)} %bitcast.15, bf16[512,896]{1,0:T(8,128)(2,1)S(1)} %bitcast.11), custom_call_target="tpu_custom_call" | custom-call | tf_op jit(solution)/shard_map/pallas_call | solution.py:44
  42.8 0.1 collective-permute-start.1
  42.9 0.0 copy-done.2
  43.0 0.0 copy-done.3
  43.0 0.0 copy-start
  43.0 0.7 %collective-permute-done.2.other_ref.other0_ref = bf16[128,1792]{1,0:T(8,128)(2,1)S(1)} collective-permute-done((bf16[128,1792]{1,0:T(8,128)(2,1)S(1)}, bf16[128,1792]{1,0:T(8,128)(2,1)S(1)}, u32[]{:S(2)}, u32[]{:S(2)}) %collective-permute-start.2) | collective-permute-done | bytes 458784 | tf_op jit(solution)/shard_map/ppermute | solution.py:228
  43.7 0.0 slice-done
  43.7 0.0 slice-done.4
  43.7 0.0 slice-done.1
  43.7 0.0 slice-done.2
  43.7 0.0 slice-done.3
  43.7 0.0 slice-done.5
  43.8 0.0 slice-done.6
  43.8 0.0 slice-done.7
  43.8 1.0 %shard_map.78.first_ref = f32[128,1792]{1,0:T(8,128)S(1)} custom-call(bf16[128,1792]{1,0:T(8,128)(2,1)S(1)} %shard_map.77.mine_ref.mine0_ref, bf16[128,1792]{1,0:T(8,128)(2,1)S(1)} %collective-permute-done.2.other_ref.other0_ref, bf16[3584,1792]{1,0:T(8,128)(2,1)S(1)} %bitcast.7, bf16[3584,1792]{1,0:T(8,128)(2,1)S(1)} %bitcast.9), custom_call_target="tpu_custom_call" | custom-call | flops 822083584 | tf_op jit(solution)/shard_map/pallas_call | solution.py:44
  44.8 0.0 collective-permute-done.1.other_ref.other1_ref
  44.8 0.0 copy-done
  44.8 1.1 %shard_map.79.refs_0_ = f32[8,128]{1,0:T(8,128)S(1)} custom-call(bf16[128,1792]{1,0:T(8,128)(2,1)S(1)} %shard_map.76.mine_ref.mine1_ref, bf16[128,1792]{1,0:T(8,128)(2,1)S(1)} %collective-permute-done.1.other_ref.other1_ref, bf16[3584,1792]{1,0:T(8,128)(2,1)S(1)} %bitcast.7, f32[128,1792]{1,0:T(8,128)S(1)} %shard_map.78.first_ref, ...), custom_call_target="tpu_custom_call" | custom-call | flops 822083584 | tf_op jit(solution)/shard_map/pallas_call | solution.py:44
  46.0 0.3 collective-permute-start.3
  46.3 1.8 %collective-permute-start.4 = (f32[8,128]{1,0:T(8,128)S(1)}, f32[8,128]{1,0:T(8,128)S(1)}, u32[]{:S(2)}, u32[]{:S(2)}) collective-permute-start(f32[8,128]{1,0:T(8,128)S(1)} %shard_map.79.refs_0_), channel_id=1, source_target_pairs={{0,3},{1,2},{2,1},{3,0},{4,7},{5,6},{6,5},{7,4},{8,11},{9,10},{10,... | collective-permute-start | bytes 12296 | tf_op jit(solution)/shard_map/ppermute | solution.py:242
  48.1 0.0 collective-permute-start.5
  48.1 1.8 %shard_map.80.refs_5_ = f32[128,1792]{1,0:T(8,128)S(1)} custom-call(bf16[128,1792]{1,0:T(8,128)(2,1)S(1)} %shard_map.77.mine_ref.mine0_ref, bf16[128,1792]{1,0:T(8,128)(2,1)S(1)} %collective-permute-done.2.other_ref.other0_ref, bf16[128,1792]{1,0:T(8,128)(2,1)S(1)} %shard_map.76.mine_ref.mine1_ref, ...), custom_call_target="tpu_custom_call" | custom-call | flops 1644167168 | tf_op jit(solution)/shard_map/pallas_call | solution.py:44
  49.9 0.0 collective-permute-done.3.refs_1_
  50.0 0.0 collective-permute-done.4.refs_2_
  50.0 0.0 collective-permute-done.5.refs_3_
  50.0 0.9 %shard_map.81 = bf16[128,1792]{1,0:T(8,128)(2,1)} custom-call(f32[8,128]{1,0:T(8,128)S(1)} %shard_map.79.refs_0_, f32[8,128]{1,0:T(8,128)S(1)} %collective-permute-done.3.refs_1_, f32[8,128]{1,0:T(8,128)S(1)} %collective-permute-done.4.refs_2_, f32[8,128]{1,0:T(8,128)S(1)} %collective-permute-done.5.refs_3_, bf16[128,1792]{1,0:T(8,128)(2,1)S(1)} %copy-done, ...), custom_call_target="tpu_custom_call" | custom-call | tf_op jit(solution)/shard_map/pallas_call | solution.py:245
  (5 shorter events, 0.0 us)
Async XLA Ops:
  1.0 19.9 %copy-start.1 = (bf16[256,896]{1,0:T(8,128)(2,1)S(1)}, bf16[256,896]{1,0:T(8,128)(2,1)}, u32[]{:S(2)}) copy-start(bf16[256,896]{1,0:T(8,128)(2,1)} %mine_ref) | copy-start | bytes 1376260
  1.0 19.9 %collective-permute-start = (bf16[256,896]{1,0:T(8,128)(2,1)}, bf16[256,896]{1,0:T(8,128)(2,1)S(1)}, u32[]{:S(2)}, u32[]{:S(2)}) collective-permute-start(bf16[256,896]{1,0:T(8,128)(2,1)} %mine_ref), channel_id=1, source_target_pairs={{0,96},{1,97},{2,98},{3,99},{4,100},{5,101},{6,102},{7,103},{8,104... | collective-permute-start | bytes 1376264 | tf_op jit(solution)/shard_map/ppermute | solution.py:201
  20.8 22.9 %slice-start = ((s8[12845056]{0:T(1024)(128)(4,1)}), s8[4194304]{0:T(1024)(128)(4,1)S(1)}, s32[]{:S(2)}) async-start(s8[12845056]{0:T(1024)(128)(4,1)} %bitcast.6), calls=%async_computation.2 | async-start | bytes 8388608
  20.8 22.9 %slice-start.4 = ((s8[12845056]{0:T(1024)(128)(4,1)}), s8[4194304]{0:T(1024)(128)(4,1)S(1)}, s32[]{:S(2)}) async-start(s8[12845056]{0:T(1024)(128)(4,1)} %bitcast.8), calls=%async_computation.6 | async-start | bytes 8388608
  20.9 22.1 %copy-start.2 = (f32[1792]{0:T(1024)S(1)}, f32[1792]{0:T(1024)}, u32[]{:S(2)}) copy-start(f32[1792]{0:T(1024)} %param.12) | copy-start | bytes 21508
  20.9 22.1 %copy-start.3 = (f32[1792]{0:T(1024)S(1)}, f32[1792]{0:T(1024)}, u32[]{:S(2)}) copy-start(f32[1792]{0:T(1024)} %param.13) | copy-start | bytes 21508
  20.9 22.8 %slice-start.1 = ((s8[12845056]{0:T(1024)(128)(4,1)}), s8[4194304]{0:T(1024)(128)(4,1)S(1)}, s32[]{:S(2)}) async-start(s8[12845056]{0:T(1024)(128)(4,1)} %bitcast.6), calls=%async_computation.3 | async-start | bytes 8388608
  20.9 22.8 %slice-start.2 = ((s8[12845056]{0:T(1024)(128)(4,1)}), s8[4194304]{0:T(1024)(128)(4,1)S(1)}, s32[]{:S(2)}) async-start(s8[12845056]{0:T(1024)(128)(4,1)} %bitcast.6), calls=%async_computation.4 | async-start | bytes 8388608
  20.9 22.8 %slice-start.3 = ((s8[12845056]{0:T(1024)(128)(4,1)}), s8[262144]{0:T(1024)(128)(4,1)S(1)}, s32[]{:S(2)}) async-start(s8[12845056]{0:T(1024)(128)(4,1)} %bitcast.6), calls=%async_computation.5 | async-start | bytes 524288
  20.9 22.8 %slice-start.5 = ((s8[12845056]{0:T(1024)(128)(4,1)}), s8[4194304]{0:T(1024)(128)(4,1)S(1)}, s32[]{:S(2)}) async-start(s8[12845056]{0:T(1024)(128)(4,1)} %bitcast.8), calls=%async_computation.7 | async-start | bytes 8388608
  20.9 22.8 %slice-start.6 = ((s8[12845056]{0:T(1024)(128)(4,1)}), s8[4194304]{0:T(1024)(128)(4,1)S(1)}, s32[]{:S(2)}) async-start(s8[12845056]{0:T(1024)(128)(4,1)} %bitcast.8), calls=%async_computation.8 | async-start | bytes 8388608
  20.9 22.8 %slice-start.7 = ((s8[12845056]{0:T(1024)(128)(4,1)}), s8[262144]{0:T(1024)(128)(4,1)S(1)}, s32[]{:S(2)}) async-start(s8[12845056]{0:T(1024)(128)(4,1)} %bitcast.8), calls=%async_computation.9 | async-start | bytes 524288
  40.2 3.5 %collective-permute-start.2 = (bf16[128,1792]{1,0:T(8,128)(2,1)S(1)}, bf16[128,1792]{1,0:T(8,128)(2,1)S(1)}, u32[]{:S(2)}, u32[]{:S(2)}) collective-permute-start(bf16[128,1792]{1,0:T(8,128)(2,1)S(1)} %shard_map.77.mine_ref.mine0_ref), channel_id=1, source_target_pairs={{0,1},{1,0},{2,3},{3,2},{4,5},{5,4},{6,7},{7,6},{8,9},{9,8},{10,11... | collective-permute-start | bytes 1376264 | tf_op jit(solution)/shard_map/ppermute | solution.py:228
  42.8 2.0 %collective-permute-start.1 = (bf16[128,1792]{1,0:T(8,128)(2,1)S(1)}, bf16[128,1792]{1,0:T(8,128)(2,1)S(1)}, u32[]{:S(2)}, u32[]{:S(2)}) collective-permute-start(bf16[128,1792]{1,0:T(8,128)(2,1)S(1)} %shard_map.76.mine_ref.mine1_ref), channel_id=1, source_target_pairs={{0,1},{1,0},{2,3},{3,2},{4,5},{5,4},{6,7},{7,6},{8,9},{9,8},{10,11... | collective-permute-start | bytes 1376264 | tf_op jit(solution)/shard_map/ppermute | solution.py:228
  43.0 1.9 %copy-start = (bf16[128,1792]{1,0:T(8,128)(2,1)S(1)}, bf16[128,1792]{1,0:T(8,128)(2,1)}, u32[]{:S(2)}) copy-start(bf16[128,1792]{1,0:T(8,128)(2,1)} %refs_4_.1) | copy-start | bytes 1376260
  46.0 4.0 %collective-permute-start.3 = (f32[8,128]{1,0:T(8,128)S(1)}, f32[8,128]{1,0:T(8,128)S(1)}, u32[]{:S(2)}, u32[]{:S(2)}) collective-permute-start(f32[8,128]{1,0:T(8,128)S(1)} %shard_map.79.refs_0_), channel_id=1, source_target_pairs={{0,2},{1,3},{2,0},{3,1},{4,6},{5,7},{6,4},{7,5},{8,10},{9,11},{10,... | collective-permute-start | bytes 12296 | tf_op jit(solution)/shard_map/ppermute | solution.py:242
  46.3 3.7 %collective-permute-start.4 = (f32[8,128]{1,0:T(8,128)S(1)}, f32[8,128]{1,0:T(8,128)S(1)}, u32[]{:S(2)}, u32[]{:S(2)}) collective-permute-start(f32[8,128]{1,0:T(8,128)S(1)} %shard_map.79.refs_0_), channel_id=1, source_target_pairs={{0,3},{1,2},{2,1},{3,0},{4,7},{5,6},{6,5},{7,4},{8,11},{9,10},{10,... | collective-permute-start | bytes 12296 | tf_op jit(solution)/shard_map/ppermute | solution.py:242
  48.1 1.9 %collective-permute-start.5 = (f32[8,128]{1,0:T(8,128)S(1)}, f32[8,128]{1,0:T(8,128)S(1)}, u32[]{:S(2)}, u32[]{:S(2)}) collective-permute-start(f32[8,128]{1,0:T(8,128)S(1)} %shard_map.79.refs_0_), channel_id=1, source_target_pairs={{0,1},{1,0},{2,3},{3,2},{4,5},{5,4},{6,7},{7,6},{8,9},{9,8},{10,11... | collective-permute-start | bytes 12296 | tf_op jit(solution)/shard_map/ppermute | solution.py:242
